TPU v7x, 32 devices: a whole 2x2x4 slice. The times are simulated.
32 devices in a mesh: slab: 4 (over z), col: 8 (over y, x, core).
Axes of the slice: x: 2, y: 2, z: 4, core: 2. Of those that a mesh axis runs over, the one named last changes fastest.
Arguments:
- field: bfloat16 [2, 64, 256, 1024], P(None, 'slab', 'col'), may hold values from -6 to 6
- fine_plane: int32 [32, 256, 1024], P('slab', 'col'), may hold values from 0 to 15, as said below
- fine_frac: int32 [32, 256, 1024], P('slab', 'col'), may hold values from 0 to 7
- counts: int32 [4, 256, 1024], P('slab', 'col'), may hold values from 1 to 8
Outputs:
- fine_color: float32 [256, 1024], P('col', 'slab')
- fine_depth: float32 [256, 1024], P('col', 'slab')
- coarse_color: float32 [256, 1024], P('col', 'slab')
Inputs may be any that keep to these rules, and one draw needn't show every extreme that they name: For each ray and slab the positions 8 * fine_plane + fine_frac are nondecreasing over the 8 slots.
All inputs are finite; a program needn't handle non-finite values.
Results may differ from a plain program's by a relative error of at most 0.0003.
Values may be sent and summed in bfloat16 or wider, within the bound.
No kernel may reach another device: no remote copies, remote signals or barrier semaphores. Data moves between devices by JAX's collectives and lax.ppermute only.
A program may use at most 64 MiB of HBM per device.

v0:
```python
import jax
import jax.numpy as jnp
from jax import lax
from jax.sharding import PartitionSpec as P


def shifted(block, axis, distance):
    devices = range(lax.axis_size(axis))
    route = [(i - distance, i) for i in devices if i - distance in devices]
    return lax.ppermute(block, axis, route)


def extended(block, sides, width):
    for axis, dim in sides:
        count = lax.axis_size(axis)
        forward = [(i, i + 1) for i in range(count - 1)]
        backward = [(target, source) for source, target in forward]
        low = lax.ppermute(
            lax.slice_in_dim(block, block.shape[dim] - width, None, axis=dim), axis, forward
        )
        high = lax.ppermute(lax.slice_in_dim(block, 0, width, axis=dim), axis, backward)
        block = jnp.concatenate([low, block, high], axis=dim)
    return block


def shade(values, total_depth):
    density = 2.0 / total_depth * jax.nn.softplus(values[0])
    emission = jax.nn.sigmoid(values[1])
    return (density, emission)


def exclusive_product(factor):
    totals = jnp.cumprod(factor, axis=0)
    return (jnp.concatenate([jnp.ones_like(factor[:1]), totals[:-1]], axis=0), totals[-1])


def select_planes(volume, fine_plane, depth_dev):
    low = jnp.zeros((2,) + fine_plane.shape, jnp.float32)
    high = jnp.zeros((2,) + fine_plane.shape, jnp.float32)
    for plane in range(depth_dev):
        hit = (fine_plane == plane)[None]
        low = low + jnp.where(
            hit, volume[:, plane : plane + 1].astype(jnp.float32), jnp.float32(0.0)
        )
        high = high + jnp.where(
            hit, volume[:, plane + 1 : plane + 2].astype(jnp.float32), jnp.float32(0.0)
        )
    return (low, high)


def body(field, fine_plane, fine_frac, counts):
    depth_dev = field.shape[1]
    total_depth = depth_dev * lax.axis_size("slab")
    slots = fine_plane.shape[0]
    following = shifted(field[:, :1], "slab", -1)
    volume = jnp.concatenate([field, following], axis=1)
    lower = volume[:, 7:depth_dev:8].astype(jnp.float32)
    upper = volume[:, 8 : depth_dev + 1 : 8].astype(jnp.float32)
    density, emission = shade(0.5 * (lower + upper), total_depth)
    factor = jnp.exp(-8.0 * density)
    opacity = 1.0 - factor
    before, coarse_pass = exclusive_product(factor)
    coarse_part = jnp.sum(before * opacity * emission, axis=0)
    low, high = select_planes(volume, fine_plane, depth_dev)
    weight = fine_frac.astype(jnp.float32) / 8.0
    density, emission = shade((1.0 - weight) * low + weight * high, total_depth)
    position = jnp.arange(slots, dtype=jnp.int32)[:, None, None]
    live = position < counts
    factor = jnp.where(live, jnp.exp(-(depth_dev / slots) * density), jnp.float32(1.0))
    opacity = 1.0 - factor
    before, fine_pass = exclusive_product(factor)
    weighted = before * opacity
    start = fine_plane + lax.axis_index("slab") * depth_dev
    color_part = jnp.sum(weighted * emission, axis=0)
    depth_part = jnp.sum(weighted * ((start.astype(jnp.float32) + weight) / total_depth), axis=0)
    parts = jnp.stack([color_part, depth_part, coarse_part])[None]
    passes = jnp.stack([fine_pass, coarse_pass])[None]
    got_parts, got_passes = (
        lax.all_to_all(parts, "slab", split_axis=3, concat_axis=0, tiled=True),
        lax.all_to_all(passes, "slab", split_axis=3, concat_axis=0, tiled=True),
    )
    front, unused_total = exclusive_product(got_passes)
    color = jnp.sum(front[:, 0] * got_parts[:, 0], axis=0)
    depth = jnp.sum(front[:, 0] * got_parts[:, 1], axis=0)
    coarse = jnp.sum(front[:, 1] * got_parts[:, 2], axis=0)
    stacked = jnp.stack([color, depth, coarse])
    padded = extended(stacked, (("col", 1),), 1)
    smooth = 0.25 * padded[:, :-2] + 0.5 * padded[:, 1:-1] + 0.25 * padded[:, 2:]
    return (smooth[0], smooth[1], smooth[2])


def solution(mesh):
    in_specs = (
        P(None, "slab", "col", None),
        P("slab", "col", None),
        P("slab", "col", None),
        P("slab", "col", None),
    )
    out_specs = (P("col", "slab"), P("col", "slab"), P("col", "slab"))
    return jax.shard_map(body, mesh=mesh, in_specs=in_specs, out_specs=out_specs, check_vma=False)
```

profile of v0, /device:TPU:3, one launch (start us, length us, event | category | flops | bytes accessed | tf_op | source)
XLA Modules:
  0.0 81.9 jit_solution(8695800712832682692)
XLA Ops:
  0.6 3.6 %bitcast_convert_fusion.16 = (f32[2,32,1024]{2,1,0:T(8,128)S(1)}, f32[2,32,1024]{2,1,0:T(8,128)}, f32[2,32,1024]{2,1,0:T(8,128)}, f32[2,32,1024]{2,1,0:T(8,128)}...) fusion(bf16[2,16,32,1024]{3,2,1,0:T(8,128)(2,1)} %param.4), kind=kLoop, calls=%fused_computation.73 | loop fusion | flops 1048576 | bytes 6422528 | tf_op jit(solution)/shard_map/jit(_where)/broadcast_in_dim | solution.py:42
  4.3 1.4 %collective-permute-start = (bf16[2,1,32,1024]{3,2,1,0:T(8,128)(2,1)S(1)}, bf16[2,1,32,1024]{3,2,1,0:T(8,128)(2,1)S(1)}, u32[]{:S(2)}, u32[]{:S(2)}) collective-permute-start(bf16[2,1,32,1024]{3,2,1,0:T(8,128)(2,1)S(1)} %get-tuple-element.30), channel_id=1, source_target_pairs={{8,0},{16,8},{24,16},{9,1},{17,9},{25,17},{10,2},{18,10},{26,18},{... | collective-permute-start | bytes 393224 | tf_op jit(solution)/shard_map/ppermute | solution.py:10
  5.7 3.6 %broadcast_compare_fusion.15 = (pred[8,32,1024]{2,1,0:T(8,128)(4,1)}, pred[8,32,1024]{2,1,0:T(8,128)(4,1)}, pred[8,32,1024]{2,1,0:T(8,128)(4,1)}, pred[8,32,1024...) fusion(s32[8,32,1024]{2,1,0:T(8,128)S(1)} %copy-done.3), kind=kLoop, calls=%fused_computation.35 | loop fusion | flops 4194304 | bytes 5242880 | tf_op jit(solution)/shard_map/eq | solution.py:41
  9.3 1.2 %broadcast_subtract_fusion = (f32[8,32,1024]{2,1,0:T(8,128)S(1)}, f32[8,32,1024]{2,1,0:T(8,128)}) fusion(s32[8,32,1024]{2,1,0:T(8,128)S(1)} %copy-done.2), kind=kLoop, calls=%fused_computation.36 | loop fusion | flops 786432 | bytes 3145728 | tf_op jit(solution)/shard_map/sub | solution.py:66
  11.3 7.6 %multiply_add_fusion = f32[2,8,32,1024]{3,2,1,0:T(8,128)S(1)} fusion(f32[2,32,1024]{2,1,0:T(8,128)S(1)} %bitcast_convert_fusion, f32[8,32,1024]{2,1,0:T(8,128)} %get-tuple-element.48, f32[2,32,1024]{2,1,0:T(8,128)} %get-tuple-element.15, f32[2,32,1024]{2,1,0:T(8,128)} %get-tuple-element.16, f32[2,32,1024]{2,1,0:T(8,128)} %get-tuple-element.17, ...), kind=kLoop, calls=%fused_computation.2 | loop fusion | flops 34078720 | bytes 12845056 | tf_op jit(solution)/shard_map/add | solution.py:66
  18.9 1.0 %fusion.29 = f32[8,32,1024]{2,1,0:T(8,128)S(1)} fusion(f32[2,8,32,1024]{3,2,1,0:T(8,128)S(1)} %multiply_add_fusion, s32[32,1024]{1,0:T(8,128)S(1)} %bitcast.117), kind=kOutput, calls=%fused_computation.91 | output fusion | flops 4194304 | bytes 2228224 | tf_op jit(solution)/shard_map/jit(cumprod)/reduce_window | solution.py:33
  21.6 1.3 %copy.59 = f32[2,32,1024]{1,0,2:T(2,128)} copy(f32[2,32,1024]{2,1,0:T(8,128)S(1)} %get-tuple-element.56) | data formatting | bytes 524288 | tf_op jit(solution)/shard_map/stack | solution.py:77
  22.9 2.4 %bitcast_bitcast_fusion = f32[1024,1,2,32]{3,2,1,0:T(2,128)} fusion(f32[2,32,1024]{1,0,2:T(2,128)} %copy.59), kind=kLoop, calls=%fused_computation.94 | loop fusion | bytes 524288
  25.3 3.0 %reshape.58 = f32[4,1,16384]{2,1,0:T(1,128)} reshape(f32[1024,1,2,32]{3,2,1,0:T(2,128)} %bitcast_bitcast_fusion) | data formatting | bytes 524288
  28.4 5.3 %all-to-all-start = ((f32[4,1,16384]{2,1,0:T(1,128)}), f32[4,1,16384]{2,1,0:T(1,128)S(1)}, u32[]{:S(2)}, u32[]{:S(2)}) async-start(f32[4,1,16384]{2,1,0:T(1,128)} %reshape.58), calls=%async_computation | async-start | bytes 524288 | tf_op jit(solution)/shard_map/all_to_all | solution.py:80
  33.6 2.8 %fusion.8 = (f32[32,1024]{1,0:T(8,128)S(1)}, f32[32,1024]{1,0:T(8,128)S(1)}) fusion(f32[2,8,32,1024]{3,2,1,0:T(8,128)S(1)} %multiply_add_fusion, f32[7,32,1024]{2,1,0:T(8,128)S(1)} %slice-done, s32[32,1024]{1,0:T(8,128)S(1)} %bitcast.118, s32[8,32,1024]{2,1,0:T(8,128)} %param.6, s32[8,32,1024]{2,1,0:T(8,128)} %param.5, s32[]{:T(128)S(6)} %mul.98), kind=kLoop, calls=%fused_computation.17 | loop fusion | flops 6225920 | bytes 5505028 | tf_op jit(solution)/shard_map/reduce_sum | solution.py:74
  36.5 2.7 %copy.61 = f32[1,3,32,1024]{2,0,1,3:T(1,128)} copy(f32[1,3,32,1024]{3,2,1,0:T(8,128)S(1)} %maximum_bitcast_fusion) | data formatting | bytes 786432 | tf_op jit(solution)/shard_map/broadcast_in_dim | solution.py:76
  39.8 6.5 %reduce.3 = f32[1024,3,32]{2,1,0:T(4,128)S(1)} reduce(f32[1024,3,1,32]{3,2,1,0:T(1,128)} %bitcast.111, f32[]{:T(128)} %broadcast.71), dimensions={2}, to_apply=%bitcast.104.reduce_sub_computation | reduce | bytes 786436
  46.2 2.0 %reshape.56 = f32[4,1,24576]{2,1,0:T(1,128)} reshape(f32[1024,3,32]{2,1,0:T(4,128)S(1)} %reduce.3) | data formatting | bytes 786432
  48.2 4.5 %all-to-all-start.1 = ((f32[4,1,24576]{2,1,0:T(1,128)}), f32[4,1,24576]{2,1,0:T(1,128)S(1)}, u32[]{:S(2)}, u32[]{:S(2)}) async-start(f32[4,1,24576]{2,1,0:T(1,128)} %reshape.56), calls=%async_computation.1 | async-start | bytes 786432 | tf_op jit(solution)/shard_map/all_to_all | solution.py:79
  52.8 1.4 %reduce.5 = f32[4,16384]{1,0:T(4,128)S(1)} reduce(f32[4,1,16384]{2,1,0:T(1,128)S(1)} %all-to-all-done, f32[]{:T(128)} %broadcast.71), dimensions={1}, to_apply=%all_to_all.26.reduce_sub_computation | reduce | bytes 524292 | tf_op jit(solution)/shard_map/all_to_all | solution.py:80
  54.1 0.9 %reshape.59 = f32[1024,1,2,32]{3,2,1,0:T(2,128)S(1)} reshape(f32[4,16384]{1,0:T(4,128)S(1)} %reduce.5) | data formatting | bytes 524288
  56.0 6.5 %all-to-all-done.1 = f32[4,1,24576]{2,1,0:T(1,128)S(1)} async-done(((f32[4,1,24576]{2,1,0:T(1,128)}), f32[4,1,24576]{2,1,0:T(1,128)S(1)}, u32[]{:S(2)}, u32[]{:S(2)}) %all-to-all-start.1) | async-done | bytes 393248 | tf_op jit(solution)/shard_map/all_to_all | solution.py:79
  62.4 1.8 %reduce.4 = f32[4,24576]{1,0:T(4,128)S(1)} reduce(f32[4,1,24576]{2,1,0:T(1,128)S(1)} %all-to-all-done.1, f32[]{:T(128)} %broadcast.71), dimensions={1}, to_apply=%all_to_all.30.reduce_sub_computation | reduce | bytes 786436 | tf_op jit(solution)/shard_map/all_to_all | solution.py:79
  64.2 2.4 %reshape.57 = f32[1024,3,1,32]{3,2,1,0:T(1,128)S(1)} reshape(f32[4,24576]{1,0:T(4,128)S(1)} %reduce.4) | data formatting | bytes 786432
  66.6 1.8 %copy.62 = f32[1,3,32,1024]{3,2,1,0:T(8,128)S(1)} copy(f32[1,3,32,1024]{2,0,1,3:T(1,128)S(1)} %bitcast.112) | data formatting | bytes 786432 | tf_op jit(solution)/shard_map/all_to_all | solution.py:79
  69.4 6.0 %collective-permute-start.1 = (f32[3,1,256]{2,1,0:T(1,128)S(1)}, f32[3,1,256]{2,1,0:T(1,128)S(1)}, u32[]{:S(2)}, u32[]{:S(2)}) collective-permute-start(f32[3,1,256]{2,1,0:T(1,128)S(1)} %get-tuple-element.54), channel_id=1, source_target_pairs={{0,1},{1,2},{2,3},{3,4},{4,5},{5,6},{6,7},{8,9},{9,10},{10,11},{11... | collective-permute-start | bytes 9224 | tf_op jit(solution)/shard_map/ppermute | solution.py:18
  75.4 1.9 %collective-permute-start.2 = (f32[3,1,256]{2,1,0:T(1,128)S(1)}, f32[3,1,256]{2,1,0:T(1,128)S(1)}, u32[]{:S(2)}, u32[]{:S(2)}) collective-permute-start(f32[3,1,256]{2,1,0:T(1,128)S(1)} %get-tuple-element.55), channel_id=1, source_target_pairs={{1,0},{2,1},{3,2},{4,3},{5,4},{6,5},{7,6},{9,8},{10,9},{11,10},{12... | collective-permute-start | bytes 9224 | tf_op jit(solution)/shard_map/ppermute | solution.py:21
  77.3 3.9 %collective-permute-done.2 = f32[3,1,256]{2,1,0:T(1,128)S(1)} collective-permute-done((f32[3,1,256]{2,1,0:T(1,128)S(1)}, f32[3,1,256]{2,1,0:T(1,128)S(1)}, u32[]{:S(2)}, u32[]{:S(2)}) %collective-permute-start.2) | collective-permute-done | bytes 3104 | tf_op jit(solution)/shard_map/ppermute | solution.py:21
  (42 shorter events, 5.6 us)
Async XLA Ops:
  0.6 5.1 %copy-start.3 = (s32[8,32,1024]{2,1,0:T(8,128)S(1)}, s32[8,32,1024]{2,1,0:T(8,128)}, u32[]{:S(2)}) copy-start(s32[8,32,1024]{2,1,0:T(8,128)} %param.5) | copy-start | bytes 3145732
  4.3 5.1 %copy-start.2 = (s32[8,32,1024]{2,1,0:T(8,128)S(1)}, s32[8,32,1024]{2,1,0:T(8,128)}, u32[]{:S(2)}) copy-start(s32[8,32,1024]{2,1,0:T(8,128)} %param.6) | copy-start | bytes 3145732
  4.3 6.4 %collective-permute-start = (bf16[2,1,32,1024]{3,2,1,0:T(8,128)(2,1)S(1)}, bf16[2,1,32,1024]{3,2,1,0:T(8,128)(2,1)S(1)}, u32[]{:S(2)}, u32[]{:S(2)}) collective-permute-start(bf16[2,1,32,1024]{3,2,1,0:T(8,128)(2,1)S(1)} %get-tuple-element.30), channel_id=1, source_target_pairs={{8,0},{16,8},{24,16},{9,1},{17,9},{25,17},{10,2},{18,10},{26,18},{... | collective-permute-start | bytes 393224 | tf_op jit(solution)/shard_map/ppermute | solution.py:10
  10.7 0.7 copy-start.5
  11.3 7.6 %copy-start.4 = (s32[1,32,1024]{2,1,0:T(8,128)S(1)}, s32[1,32,1024]{2,1,0:T(8,128)}, u32[]{:S(2)}) copy-start(s32[1,32,1024]{2,1,0:T(8,128)} %param.7) | copy-start | bytes 393220
  18.9 1.6 %copy-start = (bf16[2,16,32,1024]{3,2,1,0:T(8,128)(2,1)S(1)}, bf16[2,16,32,1024]{3,2,1,0:T(8,128)(2,1)}, u32[]{:S(2)}) copy-start(bf16[2,16,32,1024]{3,2,1,0:T(8,128)(2,1)} %param.4) | copy-start | bytes 6291460
  18.9 1.6 %copy-start.6 = (bf16[2,1,32,1024]{3,2,1,0:T(8,128)(2,1)S(1)}, bf16[2,1,32,1024]{3,2,1,0:T(8,128)(2,1)}, u32[]{:S(2)}) copy-start(bf16[2,1,32,1024]{3,2,1,0:T(8,128)(2,1)} %copy-done.5) | copy-start | bytes 393220
  19.9 1.0 %copy-start.1 = (f32[8,32,1024]{2,1,0:T(8,128)}, f32[8,32,1024]{2,1,0:T(8,128)S(1)}, u32[]{:S(2)}) copy-start(f32[8,32,1024]{2,1,0:T(8,128)S(1)} %fusion.29) | copy-start | bytes 3145732
  22.9 10.7 %slice-start = ((f32[8,32,1024]{2,1,0:T(8,128)}), f32[7,32,1024]{2,1,0:T(8,128)S(1)}, s32[]{:S(2)}) async-start(f32[8,32,1024]{2,1,0:T(8,128)} %copy-done.1), calls=%async_computation.2 | async-start | bytes 1835008 | tf_op jit(solution)/shard_map/slice | solution.py:34
  28.4 19.9 %all-to-all-start = ((f32[4,1,16384]{2,1,0:T(1,128)}), f32[4,1,16384]{2,1,0:T(1,128)S(1)}, u32[]{:S(2)}, u32[]{:S(2)}) async-start(f32[4,1,16384]{2,1,0:T(1,128)} %reshape.58), calls=%async_computation | async-start | bytes 524288 | tf_op jit(solution)/shard_map/all_to_all | solution.py:80
  48.2 14.2 %all-to-all-start.1 = ((f32[4,1,24576]{2,1,0:T(1,128)}), f32[4,1,24576]{2,1,0:T(1,128)S(1)}, u32[]{:S(2)}, u32[]{:S(2)}) async-start(f32[4,1,24576]{2,1,0:T(1,128)} %reshape.56), calls=%async_computation.1 | async-start | bytes 786432 | tf_op jit(solution)/shard_map/all_to_all | solution.py:79
  69.4 7.9 %collective-permute-start.1 = (f32[3,1,256]{2,1,0:T(1,128)S(1)}, f32[3,1,256]{2,1,0:T(1,128)S(1)}, u32[]{:S(2)}, u32[]{:S(2)}) collective-permute-start(f32[3,1,256]{2,1,0:T(1,128)S(1)} %get-tuple-element.54), channel_id=1, source_target_pairs={{0,1},{1,2},{2,3},{3,4},{4,5},{5,6},{6,7},{8,9},{9,10},{10,11},{11... | collective-permute-start | bytes 9224 | tf_op jit(solution)/shard_map/ppermute | solution.py:18
  75.4 5.8 %collective-permute-start.2 = (f32[3,1,256]{2,1,0:T(1,128)S(1)}, f32[3,1,256]{2,1,0:T(1,128)S(1)}, u32[]{:S(2)}, u32[]{:S(2)}) collective-permute-start(f32[3,1,256]{2,1,0:T(1,128)S(1)} %get-tuple-element.55), channel_id=1, source_target_pairs={{1,0},{2,1},{3,2},{4,3},{5,4},{6,5},{7,6},{9,8},{10,9},{11,10},{12... | collective-permute-start | bytes 9224 | tf_op jit(solution)/shard_map/ppermute | solution.py:21
where the time goes:
time: 82.5 us; the launch traced here: 81.9 us
  other arithmetic  31.1 us (38%)
  local copies, waits for them, and re-layouts  20.3 us (25%)
  starting transfers between devices  19.1 us (23%)
  waiting for transfers between devices  10.5 us (13%)
  between operations  0.89 us (1%)
    unnamed x23, local copies, waits for them, and re-layouts  12.9 us
    add x1, other arithmetic, body(): density, emission = shade((1.0 - weight) * low + weight * high, total_depth)  7.56 us
    all_to_all x1, waiting for transfers between devices, body(): lax.all_to_all(parts, 'slab', split_axis=3, concat_axis=0, tiled=True)  6.49 us
    unnamed x1, other arithmetic  6.48 us
    ppermute x1, starting transfers between devices, extended(): lax.ppermute(lax.slice_in_dim(block, block.shape[dim] - width, None, axis...  5.95 us
    all_to_all x1, starting transfers between devices, body(): lax.all_to_all(passes, 'slab', split_axis=3, concat_axis=0, tiled=True)  5.29 us
    all_to_all x1, starting transfers between devices, body(): lax.all_to_all(parts, 'slab', split_axis=3, concat_axis=0, tiled=True)  4.53 us
    ppermute x1, waiting for transfers between devices, extended(): lax.ppermute(lax.slice_in_dim(block, 0, width, axis=dim), axis, backward)  3.88 us
  transfers between devices with their start and end apart: 5, of which 3 were waited for; matrix products, arithmetic and copies ran while one was open for 28% of the time, Pallas kernels for 0%

commit v1 on v0

v1 whole, which is shorter than its diff:
```python
import functools

import jax
import jax.numpy as jnp
from jax import lax
from jax.experimental import pallas as pl
from jax.experimental.pallas import tpu as pltpu
from jax.sharding import PartitionSpec as P

LOG2E = 1.4426950408889634
ROWS = 16
LANES = 128
COLOR, DEEP, FINE, COARSE, COARSE_PASS = range(5)
OCTAVES = 24.0
STEPS = 65534.0 / OCTAVES
WIRE = jnp.int16


def vmem():
    return pl.BlockSpec(memory_space=pltpu.VMEM)


def smem():
    return pl.BlockSpec(memory_space=pltpu.SMEM)


def encode(x):
    if WIRE == jnp.float32:
        return x
    y = jnp.maximum(jnp.log2(x) * STEPS + 65535.5, 0.0)
    return (y.astype(jnp.int32) - 32768).astype(jnp.int16)


def decode(code):
    if WIRE == jnp.float32:
        return code
    y = code.astype(jnp.int32).astype(jnp.float32)
    x = jnp.exp2((y - 32767.0) * (1.0 / STEPS))
    return jnp.where(y > -32767.5, x, 0.0)


def shade(raw0, raw1, power):
    soft = jnp.log2(1.0 + jnp.exp2(raw0 * LOG2E))
    return jnp.exp2(soft * power), 1.0 + jnp.tanh(0.5 * raw1)


def march_rows(field, follow, plane, frac, counts, store, here, cols, base, total_depth):
    depth, slots = field.shape[1], plane.shape[0]
    unit = 8 if 8 * depth <= 256 else 1
    size = (ROWS, LANES)

    def load(ch, z):
        return field[ch, z, here, cols] if z < depth else follow[ch, 0, here, cols]

    live = counts[0, here, cols]
    color = jnp.zeros(size, jnp.float32)
    deep = jnp.zeros(size, jnp.float32)
    passed = jnp.ones(size, jnp.float32)
    for i in range(slots):
        place = plane[i, here, cols] * 8 + frac[i, here, cols]
        k = (place & 15).astype(jnp.float32)
        to_odd = jnp.minimum(k, 16.0 - k) * 0.125
        place = place.astype(jnp.float32)
        spot = (place if unit == 8 else plane[i, here, cols].astype(jnp.float32)).astype(jnp.bfloat16)
        even = [load(ch, 0) for ch in (0, 1)]
        odd = [load(ch, 1) for ch in (0, 1)]
        for z in range(1, depth):
            hit = spot >= jnp.bfloat16(unit * z)
            group = even if z % 2 else odd
            for ch in (0, 1):
                group[ch] = jnp.where(hit, load(ch, z + 1), group[ch])
        values = []
        for ch in (0, 1):
            e, o = even[ch].astype(jnp.float32), odd[ch].astype(jnp.float32)
            values.append(e + to_odd * (o - e))
        factor, emission = shade(*values, -(depth / slots) * (2.0 / total_depth))
        factor = jnp.where(live > i, factor, 1.0)
        weight = passed * (1.0 - factor)
        color = color + weight * emission
        deep = deep + weight * (place + base)
        passed = passed * factor
    store(COLOR, 0.5 * color)
    store(DEEP, deep * (1.0 / (8.0 * total_depth)))
    store(FINE, passed)
    color = jnp.zeros(size, jnp.float32)
    passed = jnp.ones(size, jnp.float32)
    for z in range(7, depth, 8):
        values = [
            0.5 * (load(ch, z).astype(jnp.float32) + load(ch, z + 1).astype(jnp.float32))
            for ch in (0, 1)
        ]
        factor, emission = shade(*values, -8.0 * (2.0 / total_depth))
        color = color + passed * (1.0 - factor) * emission
        passed = passed * factor
    store(COARSE, 0.5 * color)
    store(COARSE_PASS, passed)


def march(field, follow, plane, frac, counts, slab, steps, block_of, width, coded):
    _, depth, rows, _ = field.shape
    slots = plane.shape[0]
    total_depth = depth * lax.axis_size("slab")

    def kernel(slab_ref, field, follow, plane, frac, counts, out):
        base = (slab_ref[0] * (8 * depth)).astype(jnp.float32)

        def step(at, carry):
            r = at // (width // LANES)
            c = at % (width // LANES)
            here = pl.ds(pl.multiple_of(r * ROWS, ROWS), ROWS)
            cols = pl.ds(pl.multiple_of(c * LANES, LANES), LANES)

            def store(what, value):
                out[0, what, here, cols] = encode(value) if coded else value

            march_rows(
                field, follow, plane, frac, counts, store, here, cols, base, total_depth
            )
            return carry

        lax.fori_loop(0, (rows // ROWS) * (width // LANES), step, 0)

    def spec(*lead):
        zeros = (0,) * len(lead)
        return pl.BlockSpec(lead + (rows, width), lambda b, s: zeros + (0, block_of(b, s[0])))

    return pl.pallas_call(
        kernel,
        grid_spec=pltpu.PrefetchScalarGridSpec(
            num_scalar_prefetch=1,
            grid=(steps,),
            in_specs=[spec(2, depth), spec(2, 1), spec(slots), spec(slots), spec(1)],
            out_specs=pl.BlockSpec((1, 5, rows, width), lambda b, s: (b, 0, 0, 0)),
        ),
        out_shape=jax.ShapeDtypeStruct(
            (steps, 5, rows, width), WIRE if coded else jnp.float32
        ),
        compiler_params=pltpu.CompilerParams(vmem_limit_bytes=24 << 20),
        cost_estimate=pl.CostEstimate(
            flops=steps * rows * width * 3000, bytes_accessed=steps * rows * width * 128,
            transcendentals=0,
        ),
        name="march",
    )(slab, field, follow, plane, frac, counts)


def join(mine, got, got_first):
    first = [jnp.where(got_first, g, m) for m, g in zip(mine, got)]
    last = [jnp.where(got_first, m, g) for m, g in zip(mine, got)]
    return [
        first[COLOR] + first[FINE] * last[COLOR],
        first[DEEP] + first[FINE] * last[DEEP],
        first[FINE] * last[FINE],
        first[COARSE] + first[COARSE_PASS] * last[COARSE],
        first[COARSE_PASS] * last[COARSE_PASS],
    ]


def halve(mine, got, slab, bit):
    blocks, kinds, rows, width = mine.shape

    def kernel(slab_ref, mine, got, send, keep):
        got_first = (slab_ref[0] >> bit) & 1 == 1
        want = (slab_ref[0] >> (bit + 1)) & 1
        for i in range(blocks // 2):
            for out, at in ((send, 2 * i + 1 - want), (keep, 2 * i + want)):
                for r in range(0, rows, ROWS):
                    here = pl.ds(r, ROWS)
                    done = join(
                        [mine[at, what, here, :] for what in range(kinds)],
                        [decode(got[at, what, here, :]) for what in range(kinds)],
                        got_first,
                    )
                    for what in range(kinds):
                        out[i, what, here, :] = (
                            encode(done[what]) if out is send else done[what]
                        )

    shape = (blocks // 2, kinds, rows, width)
    return pl.pallas_call(
        kernel,
        in_specs=[smem(), vmem(), vmem()],
        out_specs=[vmem(), vmem()],
        out_shape=[jax.ShapeDtypeStruct(shape, WIRE), jax.ShapeDtypeStruct(shape, jnp.float32)],
        compiler_params=pltpu.CompilerParams(vmem_limit_bytes=16 << 20),
        name="halve",
    )(slab, mine, got)


def finish(mine, got, slab, bit, col):
    _, kinds, rows, width = mine.shape
    runs = [mine] if got is None else [mine, got]

    def kernel(slab_ref, col_ref, mine, *refs):
        *partner, image, near, far = refs
        odd = col_ref[0] % 2 == 1
        done = [mine[0, what] for what in range(kinds)]
        for got in partner:
            got_first = (slab_ref[0] >> bit) & 1 == 1
            done = join(done, [decode(got[0, what]) for what in range(kinds)], got_first)
        row = lax.broadcasted_iota(jnp.int32, (rows, width), 0)
        for at, what in enumerate((COLOR, DEEP, COARSE)):
            x = done[what]
            up = jnp.where(row == 0, 0.0, pltpu.roll(x, 1, 0))
            down = jnp.where(row == rows - 1, 0.0, pltpu.roll(x, rows - 1, 0))
            image[at] = 0.25 * up + 0.5 * x + 0.25 * down
            top, bottom = x[0:1], x[rows - 1 : rows]
            near[pl.ds(at, 1), :] = 0.25 * jnp.where(odd, top, bottom)
            far[pl.ds(at, 1), :] = 0.25 * jnp.where(odd, bottom, top)

    edge = jax.ShapeDtypeStruct((3, width), jnp.float32)
    return pl.pallas_call(
        kernel,
        in_specs=[smem(), smem()] + [vmem()] * len(runs),
        out_specs=[vmem()] * 3,
        out_shape=[jax.ShapeDtypeStruct((3, rows, width), jnp.float32), edge, edge],
        compiler_params=pltpu.CompilerParams(vmem_limit_bytes=16 << 20),
        name="finish",
    )(slab, col, *runs)


def border(image, near, far, col):
    _, rows, width = image.shape

    def kernel(col_ref, image, near, far, *outs):
        odd = col_ref[0] % 2 == 1
        row = lax.broadcasted_iota(jnp.int32, (rows, width), 0)
        for at, out in enumerate(outs):
            a, b = near[pl.ds(at, 1), :], far[pl.ds(at, 1), :]
            above, below = jnp.where(odd, a, b), jnp.where(odd, b, a)
            extra = jnp.where(row == 0, above, 0.0) + jnp.where(row == rows - 1, below, 0.0)
            out[...] = image[at] + extra

    return pl.pallas_call(
        kernel,
        in_specs=[smem()] + [vmem()] * 3,
        out_specs=[vmem()] * 3,
        out_shape=[jax.ShapeDtypeStruct((rows, width), jnp.float32)] * 3,
        compiler_params=pltpu.CompilerParams(vmem_limit_bytes=16 << 20),
        name="border",
    )(col, image, near, far)


def pairs(low, high):
    route = list(zip(low, high))
    return route + [(b, a) for a, b in route]


def neighbours(near, far):
    count = lax.axis_size("col")
    near = lax.ppermute(near, "col", pairs(range(0, count - 1, 2), range(1, count, 2)))
    far = lax.ppermute(far, "col", pairs(range(1, count - 1, 2), range(2, count, 2)))
    return near, far


def wide_exchange(parts, slabs, width):
    blocks, kinds, rows, lanes = parts.shape
    tiles = parts.transpose(1, 2, 0, 3).reshape(kinds, rows, slabs, width).transpose(2, 0, 1, 3)
    got = lax.all_to_all(tiles, "slab", 0, 0)
    done = [got[0, what] for what in range(kinds)]
    for s in range(1, slabs):
        done = join(done, [got[s, what] for what in range(kinds)], False)
    return jnp.stack(done)[None]


def body(field, fine_plane, fine_frac, counts):
    slabs = lax.axis_size("slab")
    columns = field.shape[3]
    width = columns // slabs
    slab = lax.axis_index("slab").reshape(1).astype(jnp.int32)
    col = lax.axis_index("col").reshape(1).astype(jnp.int32)
    follow = lax.ppermute(field[:, :1], "slab", [(i + 1, i) for i in range(slabs - 1)])
    args = (field, follow, fine_plane, fine_frac, counts, slab)
    if width % LANES:
        parts = march(*args, columns // LANES, lambda b, s: b, LANES, False)
        image, near, far = finish(wide_exchange(parts, slabs, width), None, slab, 0, col)
        return border(image, *neighbours(near, far), col)
    send = march(*args, slabs // 2, lambda b, s: 2 * b + 1 - (s & 1), width, True)
    keep = march(*args, slabs // 2, lambda b, s: 2 * b + (s & 1), width, False)
    bit = 0
    while True:
        low = [i for i in range(slabs) if not (i >> bit) & 1]
        got = lax.ppermute(send, "slab", pairs(low, [i + (1 << bit) for i in low]))
        if 2 << bit == slabs:
            break
        send, keep = halve(keep, got, slab, bit)
        bit += 1
    image, near, far = finish(keep, got, slab, bit, col)
    near, far = neighbours(near, far)
    return border(image, near, far, col)


def solution(mesh):
    in_specs = (
        P(None, "slab", "col", None),
        P("slab", "col", None),
        P("slab", "col", None),
        P("slab", "col", None),
    )
    out_specs = (P("col", "slab"), P("col", "slab"), P("col", "slab"))
    return jax.shard_map(body, mesh=mesh, in_specs=in_specs, out_specs=out_specs, check_vma=False)
```

time: 82.5 us -> 34.1 us (0.41)
  other arithmetic: 31.1 us -> 0 us
  local copies, waits for them, and re-layouts: 20.3 us -> 5.86 us
  starting transfers between devices: 19.1 us -> 11.9 us
  Pallas kernels: 0 us -> 4.61 us
    all_to_all x2 -> x0, starting transfers between devices: 9.82 us -> none  [the longest x1 5.29 us: body(): lax.all_to_all(passes, 'slab', split_axis=3, concat_axis=0, tiled=True)]
    unnamed x23 -> x8, local copies, waits for them, and re-layouts: 12.9 us -> 4.94 us
    add x2 -> x0, other arithmetic: 7.6 us -> none  [the longest x1 7.56 us: body(): density, emission = shade((1.0 - weight) * low + weight * high, total_depth)]
    ppermute x3 -> x5, waiting for transfers between devices: 3.98 us -> 10.7 us  [the longest x1 4.97 us: body(): lax.ppermute(field[:, :1], 'slab', [(i + 1, i) for i in range(slabs - 1)])]
    all_to_all x2 -> x0, waiting for transfers between devices: 6.49 us -> none  [the longest x1 6.49 us: body(): lax.all_to_all(parts, 'slab', split_axis=3, concat_axis=0, tiled=True)]
    unnamed x1 -> x0, other arithmetic: 6.48 us -> none
    pallas_call x0 -> x5, Pallas kernels: none -> 4.61 us  [the longest x2 3.71 us: march(): pl.pallas_call(kernel, grid_spec=pltpu.PrefetchScalarGridSpec(num_scalar_...]
    broadcast_in_dim x3 -> x0, other arithmetic: 3.67 us -> none  [the longest x1 3.62 us: select_planes(): jnp.where(hit, volume[:, plane:plane + 1].astype(jnp.float32), jnp.float3...]
  transfers between devices with their start and end apart: 5 -> 5, of which waited for: 3 -> 4; matrix products, arithmetic and copies ran while one was open for 28% -> 0% of each run, Pallas kernels for 0% -> 5%
where the time goes in v1:
time: 34.1 us; the launch traced here: 33.8 us
  starting transfers between devices  11.9 us (35%)
  waiting for transfers between devices  10.7 us (31%)
  local copies, waits for them, and re-layouts  5.86 us (17%)
  Pallas kernels  4.61 us (14%)
  between operations  0.69 us (2%)
    ppermute x1, waiting for transfers between devices, body(): lax.ppermute(field[:, :1], 'slab', [(i + 1, i) for i in range(slabs - 1)])  4.97 us
    unnamed x8, local copies, waits for them, and re-layouts  4.94 us
    ppermute x1, starting transfers between devices, neighbours(): lax.ppermute(near, 'col', pairs(range(0, count - 1, 2), range(1, count, 2)))  3.89 us
    ppermute x2, starting transfers between devices, body(): got = lax.ppermute(send, 'slab', pairs(low, [i + (1 << bit) for i in low]))  3.74 us
    pallas_call x2, Pallas kernels, march(): pl.pallas_call(kernel, grid_spec=pltpu.PrefetchScalarGridSpec(num_scalar_...  3.71 us
    ppermute x1, starting transfers between devices, neighbours(): lax.ppermute(far, 'col', pairs(range(1, count - 1, 2), range(2, count, 2)))  3.02 us
    ppermute x2, waiting for transfers between devices, body(): got = lax.ppermute(send, 'slab', pairs(low, [i + (1 << bit) for i in low]))  2.97 us
    ppermute x1, waiting for transfers between devices, neighbours(): lax.ppermute(far, 'col', pairs(range(1, count - 1, 2), range(2, count, 2)))  2.78 us
  transfers between devices with their start and end apart: 5, of which 4 were waited for; matrix products, arithmetic and copies ran while one was open for 0% of the time, Pallas kernels for 5%

profile of v1, /device:TPU:3, one launch (start us, length us, event | category | flops | bytes accessed | tf_op | source)
XLA Modules:
  0.0 33.8 jit_solution(10774970600109524896)
XLA Ops:
  0.6 0.9 %slice.3 = bf16[2,1,32,1024]{3,2,1,0:T(8,128)(2,1)S(1)} slice(bf16[2,16,32,1024]{3,2,1,0:T(8,128)(2,1)} %field.3), slice={[0:2], [0:1], [0:32], [0:1024]} | slice | bytes 262144 | tf_op jit(solution)/shard_map/slice | solution.py:272
  1.6 1.3 %collective-permute-start = (bf16[2,1,32,1024]{3,2,1,0:T(8,128)(2,1)S(1)}, bf16[2,1,32,1024]{3,2,1,0:T(8,128)(2,1)S(1)}, u32[]{:S(2)}, u32[]{:S(2)}) collective-permute-start(bf16[2,1,32,1024]{3,2,1,0:T(8,128)(2,1)S(1)} %slice.3), channel_id=1, source_target_pairs={{8,0},{16,8},{24,16},{9,1},{17,9},{25,17},{10,2},{18,10},{26,18},{... | collective-permute-start | bytes 393224 | tf_op jit(solution)/shard_map/ppermute | solution.py:272
  2.9 5.0 %collective-permute-done.follow = bf16[2,1,32,1024]{3,2,1,0:T(8,128)(2,1)S(1)} collective-permute-done((bf16[2,1,32,1024]{3,2,1,0:T(8,128)(2,1)S(1)}, bf16[2,1,32,1024]{3,2,1,0:T(8,128)(2,1)S(1)}, u32[]{:S(2)}, u32[]{:S(2)}) %collective-permute-start) | collective-permute-done | bytes 131104 | tf_op jit(solution)/shard_map/ppermute | solution.py:272
  7.8 0.0 copy-start
  7.8 1.6 %copy-done = bf16[2,16,32,1024]{3,2,1,0:T(8,128)(2,1)S(1)} copy-done((bf16[2,16,32,1024]{3,2,1,0:T(8,128)(2,1)S(1)}, bf16[2,16,32,1024]{3,2,1,0:T(8,128)(2,1)}, u32[]{:S(2)}) %copy-start) | copy-done | bytes 2097176
  9.4 0.0 copy-start.1
  9.4 1.2 %copy-done.1 = s32[8,32,1024]{2,1,0:T(8,128)S(1)} copy-done((s32[8,32,1024]{2,1,0:T(8,128)S(1)}, s32[8,32,1024]{2,1,0:T(8,128)}, u32[]{:S(2)}) %copy-start.1) | copy-done | bytes 1048600
  10.6 0.0 copy-start.2
  10.6 1.2 %copy-done.2 = s32[8,32,1024]{2,1,0:T(8,128)S(1)} copy-done((s32[8,32,1024]{2,1,0:T(8,128)S(1)}, s32[8,32,1024]{2,1,0:T(8,128)}, u32[]{:S(2)}) %copy-start.2) | copy-done | bytes 1048600
  11.9 0.0 copy-start.3
  11.9 0.9 %copy-done.3 = s32[1,32,1024]{2,1,0:T(8,128)S(1)} copy-done((s32[1,32,1024]{2,1,0:T(8,128)S(1)}, s32[1,32,1024]{2,1,0:T(8,128)}, u32[]{:S(2)}) %copy-start.3) | copy-done | bytes 131096
  12.8 1.9 %march.3 = s16[2,5,32,256]{3,2,1,0:T(8,128)(2,1)S(1)} custom-call(s32[1]{0:T(128)} %bitcast.1.slab_ref, bf16[2,16,32,1024]{3,2,1,0:T(8,128)(2,1)S(1)} %copy-done, bf16[2,1,32,1024]{3,2,1,0:T(8,128)(2,1)S(1)} %collective-permute-done.follow, s32[8,32,1024]{2,1,0:T(8,128)S(1)} %copy-done.1, s32[8,32,1024]{2,1,0:T(8,128)S(1)} %copy-done.2, ...), custom_call_target="tpu_custom_call" | custom-call | flops 49152000 | bytes 2097152 | tf_op jit(solution)/shard_map/march/pallas_call | solution.py:127
  14.7 1.4 %collective-permute-start.1 = (s16[2,5,32,256]{3,2,1,0:T(8,128)(2,1)S(1)}, s16[2,5,32,256]{3,2,1,0:T(8,128)(2,1)S(1)}, u32[]{:S(2)}, u32[]{:S(2)}) collective-permute-start(s16[2,5,32,256]{3,2,1,0:T(8,128)(2,1)S(1)} %march.3), channel_id=1, source_target_pairs={{0,8},{16,24},{8,0},{24,16},{1,9},{17,25},{9,1},{25,17},{2,10},{18... | collective-permute-start | bytes 491528 | tf_op jit(solution)/shard_map/ppermute | solution.py:283
  16.1 1.8 %march.2.mine = f32[2,5,32,256]{3,2,1,0:T(8,128)S(1)} custom-call(s32[1]{0:T(128)} %bitcast.1.slab_ref, bf16[2,16,32,1024]{3,2,1,0:T(8,128)(2,1)S(1)} %copy-done, bf16[2,1,32,1024]{3,2,1,0:T(8,128)(2,1)S(1)} %collective-permute-done.follow, s32[8,32,1024]{2,1,0:T(8,128)S(1)} %copy-done.1, s32[8,32,1024]{2,1,0:T(8,128)S(1)} %copy-done.2, ...), custom_call_target="tpu_custom_call" | custom-call | flops 49152000 | bytes 2097152 | tf_op jit(solution)/shard_map/march/pallas_call | solution.py:127
  17.9 1.1 %collective-permute-done.1.got = s16[2,5,32,256]{3,2,1,0:T(8,128)(2,1)S(1)} collective-permute-done((s16[2,5,32,256]{3,2,1,0:T(8,128)(2,1)S(1)}, s16[2,5,32,256]{3,2,1,0:T(8,128)(2,1)S(1)}, u32[]{:S(2)}, u32[]{:S(2)}) %collective-permute-start.1) | collective-permute-done | bytes 163872 | tf_op jit(solution)/shard_map/ppermute | solution.py:283
  19.0 0.2 halve.1
  19.1 2.4 %collective-permute-start.2 = (s16[1,5,32,256]{3,2,1,0:T(8,128)(2,1)S(1)}, s16[1,5,32,256]{3,2,1,0:T(8,128)(2,1)S(1)}, u32[]{:S(2)}, u32[]{:S(2)}) collective-permute-start(s16[1,5,32,256]{3,2,1,0:T(8,128)(2,1)S(1)} %get-tuple-element.9), channel_id=1, source_target_pairs={{0,16},{8,24},{16,0},{24,8},{1,17},{9,25},{17,1},{25,9},{2,18},{10... | collective-permute-start | bytes 245768 | tf_op jit(solution)/shard_map/ppermute | solution.py:283
  21.5 1.9 %collective-permute-done.2.refs_0_ = s16[1,5,32,256]{3,2,1,0:T(8,128)(2,1)S(1)} collective-permute-done((s16[1,5,32,256]{3,2,1,0:T(8,128)(2,1)S(1)}, s16[1,5,32,256]{3,2,1,0:T(8,128)(2,1)S(1)}, u32[]{:S(2)}, u32[]{:S(2)}) %collective-permute-start.2) | collective-permute-done | bytes 81952 | tf_op jit(solution)/shard_map/ppermute | solution.py:283
  23.4 0.1 finish.1
  23.5 3.9 %collective-permute-start.3 = (f32[3,256]{1,0:T(4,128)S(1)}, f32[3,256]{1,0:T(4,128)S(1)}, u32[]{:S(2)}, u32[]{:S(2)}) collective-permute-start(f32[3,256]{1,0:T(4,128)S(1)} %get-tuple-element.11), channel_id=1, source_target_pairs={{0,1},{2,3},{4,5},{6,7},{1,0},{3,2},{5,4},{7,6},{8,9},{10,11},{12,... | collective-permute-start | bytes 9224 | tf_op jit(solution)/shard_map/ppermute | solution.py:251
  27.4 3.0 %collective-permute-start.4 = (f32[3,256]{1,0:T(4,128)S(1)}, f32[3,256]{1,0:T(4,128)S(1)}, u32[]{:S(2)}, u32[]{:S(2)}) collective-permute-start(f32[3,256]{1,0:T(4,128)S(1)} %get-tuple-element.12), channel_id=1, source_target_pairs={{1,2},{3,4},{5,6},{2,1},{4,3},{6,5},{9,10},{11,12},{13,14},{10,9},... | collective-permute-start | bytes 9224 | tf_op jit(solution)/shard_map/ppermute | solution.py:252
  30.4 0.0 collective-permute-done.3.near
  30.4 2.8 %collective-permute-done.4.far = f32[3,256]{1,0:T(4,128)S(1)} collective-permute-done((f32[3,256]{1,0:T(4,128)S(1)}, f32[3,256]{1,0:T(4,128)S(1)}, u32[]{:S(2)}, u32[]{:S(2)}) %collective-permute-start.4) | collective-permute-done | bytes 3104 | tf_op jit(solution)/shard_map/ppermute | solution.py:252
  33.2 0.6 %border.1 = (f32[32,256]{1,0:T(8,128)}, f32[32,256]{1,0:T(8,128)}, f32[32,256]{1,0:T(8,128)}) custom-call(s32[1]{0:T(128)} %bitcast.col_ref, f32[3,32,256]{2,1,0:T(8,128)S(1)} %get-tuple-element.10.image, f32[3,256]{1,0:T(4,128)S(1)} %collective-permute-done.3.near, f32[3,256]{1,0:T(4,128)S(1)} %collective-permute-done.4.far), custom_call_target="tpu_custom_call" | custom-call | tf_op jit(solution)/shard_map/border/pallas_call | solution.py:234
Async XLA Ops:
  1.6 6.3 %collective-permute-start = (bf16[2,1,32,1024]{3,2,1,0:T(8,128)(2,1)S(1)}, bf16[2,1,32,1024]{3,2,1,0:T(8,128)(2,1)S(1)}, u32[]{:S(2)}, u32[]{:S(2)}) collective-permute-start(bf16[2,1,32,1024]{3,2,1,0:T(8,128)(2,1)S(1)} %slice.3), channel_id=1, source_target_pairs={{8,0},{16,8},{24,16},{9,1},{17,9},{25,17},{10,2},{18,10},{26,18},{... | collective-permute-start | bytes 393224 | tf_op jit(solution)/shard_map/ppermute | solution.py:272
  7.8 1.6 %copy-start = (bf16[2,16,32,1024]{3,2,1,0:T(8,128)(2,1)S(1)}, bf16[2,16,32,1024]{3,2,1,0:T(8,128)(2,1)}, u32[]{:S(2)}) copy-start(bf16[2,16,32,1024]{3,2,1,0:T(8,128)(2,1)} %field.3) | copy-start | bytes 6291460
  9.4 1.2 %copy-start.1 = (s32[8,32,1024]{2,1,0:T(8,128)S(1)}, s32[8,32,1024]{2,1,0:T(8,128)}, u32[]{:S(2)}) copy-start(s32[8,32,1024]{2,1,0:T(8,128)} %plane.3) | copy-start | bytes 3145732
  10.6 1.2 %copy-start.2 = (s32[8,32,1024]{2,1,0:T(8,128)S(1)}, s32[8,32,1024]{2,1,0:T(8,128)}, u32[]{:S(2)}) copy-start(s32[8,32,1024]{2,1,0:T(8,128)} %frac.3) | copy-start | bytes 3145732
  11.9 0.9 %copy-start.3 = (s32[1,32,1024]{2,1,0:T(8,128)S(1)}, s32[1,32,1024]{2,1,0:T(8,128)}, u32[]{:S(2)}) copy-start(s32[1,32,1024]{2,1,0:T(8,128)} %counts.3) | copy-start | bytes 393220
  14.7 4.2 %collective-permute-start.1 = (s16[2,5,32,256]{3,2,1,0:T(8,128)(2,1)S(1)}, s16[2,5,32,256]{3,2,1,0:T(8,128)(2,1)S(1)}, u32[]{:S(2)}, u32[]{:S(2)}) collective-permute-start(s16[2,5,32,256]{3,2,1,0:T(8,128)(2,1)S(1)} %march.3), channel_id=1, source_target_pairs={{0,8},{16,24},{8,0},{24,16},{1,9},{17,25},{9,1},{25,17},{2,10},{18... | collective-permute-start | bytes 491528 | tf_op jit(solution)/shard_map/ppermute | solution.py:283
  19.1 4.3 %collective-permute-start.2 = (s16[1,5,32,256]{3,2,1,0:T(8,128)(2,1)S(1)}, s16[1,5,32,256]{3,2,1,0:T(8,128)(2,1)S(1)}, u32[]{:S(2)}, u32[]{:S(2)}) collective-permute-start(s16[1,5,32,256]{3,2,1,0:T(8,128)(2,1)S(1)} %get-tuple-element.9), channel_id=1, source_target_pairs={{0,16},{8,24},{16,0},{24,8},{1,17},{9,25},{17,1},{25,9},{2,18},{10... | collective-permute-start | bytes 245768 | tf_op jit(solution)/shard_map/ppermute | solution.py:283
  23.5 6.9 %collective-permute-start.3 = (f32[3,256]{1,0:T(4,128)S(1)}, f32[3,256]{1,0:T(4,128)S(1)}, u32[]{:S(2)}, u32[]{:S(2)}) collective-permute-start(f32[3,256]{1,0:T(4,128)S(1)} %get-tuple-element.11), channel_id=1, source_target_pairs={{0,1},{2,3},{4,5},{6,7},{1,0},{3,2},{5,4},{7,6},{8,9},{10,11},{12,... | collective-permute-start | bytes 9224 | tf_op jit(solution)/shard_map/ppermute | solution.py:251
  27.4 5.8 %collective-permute-start.4 = (f32[3,256]{1,0:T(4,128)S(1)}, f32[3,256]{1,0:T(4,128)S(1)}, u32[]{:S(2)}, u32[]{:S(2)}) collective-permute-start(f32[3,256]{1,0:T(4,128)S(1)} %get-tuple-element.12), channel_id=1, source_target_pairs={{1,2},{3,4},{5,6},{2,1},{4,3},{6,5},{9,10},{11,12},{13,14},{10,9},... | collective-permute-start | bytes 9224 | tf_op jit(solution)/shard_map/ppermute | solution.py:252

commit v2 on v1

--- a/solution.py
+++ b/solution.py
@@ -14,6 +14,7 @@
 OCTAVES = 24.0
 STEPS = 65534.0 / OCTAVES
 WIRE = jnp.int16
+MARCH_LIMIT = 24 << 20
 
 
 def vmem():
@@ -44,14 +45,10 @@
     return jnp.exp2(soft * power), 1.0 + jnp.tanh(0.5 * raw1)
 
 
-def march_rows(field, follow, plane, frac, counts, store, here, cols, base, total_depth):
+def march_rows(field, plane, frac, counts, run, late, here, cols, base, total_depth):
     depth, slots = field.shape[1], plane.shape[0]
     unit = 8 if 8 * depth <= 256 else 1
     size = (ROWS, LANES)
-
-    def load(ch, z):
-        return field[ch, z, here, cols] if z < depth else follow[ch, 0, here, cols]
-
     live = counts[0, here, cols]
     color = jnp.zeros(size, jnp.float32)
     deep = jnp.zeros(size, jnp.float32)
@@ -61,87 +58,147 @@
         k = (place & 15).astype(jnp.float32)
         to_odd = jnp.minimum(k, 16.0 - k) * 0.125
         place = place.astype(jnp.float32)
-        spot = (place if unit == 8 else plane[i, here, cols].astype(jnp.float32)).astype(jnp.bfloat16)
-        even = [load(ch, 0) for ch in (0, 1)]
-        odd = [load(ch, 1) for ch in (0, 1)]
-        for z in range(1, depth):
+        spot = place if unit == 8 else plane[i, here, cols].astype(jnp.float32)
+        spot = spot.astype(jnp.bfloat16)
+        even = [field[ch, 0, here, cols] for ch in (0, 1)]
+        odd = [field[ch, 1, here, cols] for ch in (0, 1)]
+        for z in range(1, depth - 1):
             hit = spot >= jnp.bfloat16(unit * z)
             group = even if z % 2 else odd
             for ch in (0, 1):
-                group[ch] = jnp.where(hit, load(ch, z + 1), group[ch])
+                group[ch] = jnp.where(hit, field[ch, z + 1, here, cols], group[ch])
         values = []
         for ch in (0, 1):
             e, o = even[ch].astype(jnp.float32), odd[ch].astype(jnp.float32)
             values.append(e + to_odd * (o - e))
         factor, emission = shade(*values, -(depth / slots) * (2.0 / total_depth))
-        factor = jnp.where(live > i, factor, 1.0)
+        rest = jnp.where(live > i, place - 8.0 * (depth - 1), -1.0)
+        early = (live > i) & (place < 8.0 * (depth - 1))
+        late[i, here, cols] = jnp.maximum(rest, -1.0).astype(jnp.bfloat16)
+        factor = jnp.where(early, factor, 1.0)
         weight = passed * (1.0 - factor)
         color = color + weight * emission
         deep = deep + weight * (place + base)
         passed = passed * factor
-    store(COLOR, 0.5 * color)
-    store(DEEP, deep * (1.0 / (8.0 * total_depth)))
-    store(FINE, passed)
+    run[COLOR, here, cols] = color
+    run[DEEP, here, cols] = deep
+    run[FINE, here, cols] = passed
     color = jnp.zeros(size, jnp.float32)
     passed = jnp.ones(size, jnp.float32)
-    for z in range(7, depth, 8):
+    for z in range(7, depth - 1, 8):
         values = [
-            0.5 * (load(ch, z).astype(jnp.float32) + load(ch, z + 1).astype(jnp.float32))
+            0.5 * (field[ch, z, here, cols].astype(jnp.float32)
+                   + field[ch, z + 1, here, cols].astype(jnp.float32))
             for ch in (0, 1)
         ]
         factor, emission = shade(*values, -8.0 * (2.0 / total_depth))
         color = color + passed * (1.0 - factor) * emission
         passed = passed * factor
-    store(COARSE, 0.5 * color)
-    store(COARSE_PASS, passed)
-
-
-def march(field, follow, plane, frac, counts, slab, steps, block_of, width, coded):
-    _, depth, rows, _ = field.shape
-    slots = plane.shape[0]
+    run[COARSE, here, cols] = color
+    run[COARSE_PASS, here, cols] = passed
+
+
+def tiles(rows, width, step):
+    across = width // LANES
+
+    def one(at, carry):
+        here = pl.ds(pl.multiple_of((at // across) * ROWS, ROWS), ROWS)
+        step(here, pl.ds(pl.multiple_of((at % across) * LANES, LANES), LANES))
+        return carry
+
+    lax.fori_loop(0, (rows // ROWS) * across, one, 0)
+
+
+def march(field, plane, frac, counts, slab, width):
+    _, depth, rows, columns = field.shape
+    slots, blocks = plane.shape[0], columns // width
     total_depth = depth * lax.axis_size("slab")
 
-    def kernel(slab_ref, field, follow, plane, frac, counts, out):
+    def kernel(slab_ref, field, plane, frac, counts, run, late, last):
         base = (slab_ref[0] * (8 * depth)).astype(jnp.float32)
-
-        def step(at, carry):
-            r = at // (width // LANES)
-            c = at % (width // LANES)
-            here = pl.ds(pl.multiple_of(r * ROWS, ROWS), ROWS)
-            cols = pl.ds(pl.multiple_of(c * LANES, LANES), LANES)
-
-            def store(what, value):
-                out[0, what, here, cols] = encode(value) if coded else value
-
-            march_rows(
-                field, follow, plane, frac, counts, store, here, cols, base, total_depth
-            )
-            return carry
-
-        lax.fori_loop(0, (rows // ROWS) * (width // LANES), step, 0)
+        last[0] = field[:, depth - 1]
+        tiles(rows, width, lambda here, cols: march_rows(
+            field, plane, frac, counts, run.at[0], late.at[0], here, cols, base, total_depth
+        ))
 
     def spec(*lead):
         zeros = (0,) * len(lead)
-        return pl.BlockSpec(lead + (rows, width), lambda b, s: zeros + (0, block_of(b, s[0])))
-
-    return pl.pallas_call(
-        kernel,
-        grid_spec=pltpu.PrefetchScalarGridSpec(
-            num_scalar_prefetch=1,
-            grid=(steps,),
-            in_specs=[spec(2, depth), spec(2, 1), spec(slots), spec(slots), spec(1)],
-            out_specs=pl.BlockSpec((1, 5, rows, width), lambda b, s: (b, 0, 0, 0)),
+        return pl.BlockSpec(lead + (rows, width), lambda b: zeros + (0, b))
+
+    def out(*lead):
+        zeros = (0,) * len(lead)
+        return pl.BlockSpec((1,) + lead + (rows, width), lambda b: (b,) + zeros + (0, 0))
+
+    def shape(*lead, kind):
+        return jax.ShapeDtypeStruct((blocks,) + lead + (rows, width), kind)
+
+    return pl.pallas_call(
+        kernel,
+        grid=(blocks,),
+        in_specs=[smem(), spec(2, depth), spec(slots), spec(slots), spec(1)],
+        out_specs=[out(5), out(slots), out(2)],
+        out_shape=[
+            shape(5, kind=jnp.float32), shape(slots, kind=jnp.bfloat16),
+            shape(2, kind=jnp.bfloat16),
+        ],
+        compiler_params=pltpu.CompilerParams(vmem_limit_bytes=MARCH_LIMIT),
+        cost_estimate=pl.CostEstimate(
+            flops=rows * columns * 3000, bytes_accessed=rows * columns * 128, transcendentals=0
         ),
-        out_shape=jax.ShapeDtypeStruct(
-            (steps, 5, rows, width), WIRE if coded else jnp.float32
-        ),
+        name="march",
+    )(slab, *(pltpu.with_memory_space_constraint(x, pltpu.HBM) for x in (field, plane, frac, counts)))
+
+
+def close(run, late, last, follow, slab, depth, steps, block_of, coded):
+    _, slots, rows, width = late.shape
+    total_depth = depth * lax.axis_size("slab")
+
+    def kernel(slab_ref, run, late, last, follow, out):
+        s = slab_ref[0]
+        base = (s * (8 * depth) + 8 * (depth - 1)).astype(jnp.float32)
+
+        def step(i, here, cols):
+            b = block_of(i, s)
+            there = pl.ds(pl.multiple_of(b * width + cols.start, LANES), LANES)
+            low = [last[b, ch, here, cols].astype(jnp.float32) for ch in (0, 1)]
+            high = [follow[ch, 0, here, there].astype(jnp.float32) for ch in (0, 1)]
+            slope = [(h - l) * 0.125 for h, l in zip(high, low)]
+            color, deep, passed = (run[b, what, here, cols] for what in (COLOR, DEEP, FINE))
+            for k in range(slots):
+                eighths = late[b, k, here, cols].astype(jnp.float32)
+                values = [l + eighths * d for l, d in zip(low, slope)]
+                factor, emission = shade(*values, -(depth / slots) * (2.0 / total_depth))
+                factor = jnp.where(eighths >= 0.0, factor, 1.0)
+                weight = passed * (1.0 - factor)
+                color = color + weight * emission
+                deep = deep + weight * (eighths + base)
+                passed = passed * factor
+            values = [0.5 * (h + l) for h, l in zip(high, low)]
+            factor, emission = shade(*values, -8.0 * (2.0 / total_depth))
+            coarse, through = (run[b, what, here, cols] for what in (COARSE, COARSE_PASS))
+            coarse = coarse + through * (1.0 - factor) * emission
+            done = {
+                COLOR: 0.5 * color, DEEP: deep * (1.0 / (8.0 * total_depth)), FINE: passed,
+                COARSE: 0.5 * coarse, COARSE_PASS: through * factor,
+            }
+            for what, value in done.items():
+                out[i, what, here, cols] = encode(value) if coded else value
+
+        for i in range(steps):
+            tiles(rows, width, functools.partial(step, i))
+
+    return pl.pallas_call(
+        kernel,
+        in_specs=[smem()] + [vmem()] * 4,
+        out_specs=vmem(),
+        out_shape=jax.ShapeDtypeStruct((steps, 5, rows, width), WIRE if coded else jnp.float32),
         compiler_params=pltpu.CompilerParams(vmem_limit_bytes=24 << 20),
         cost_estimate=pl.CostEstimate(
-            flops=steps * rows * width * 3000, bytes_accessed=steps * rows * width * 128,
+            flops=steps * rows * width * 1500, bytes_accessed=steps * rows * width * 64,
             transcendentals=0,
         ),
-        name="march",
-    )(slab, field, follow, plane, frac, counts)
+        name="close",
+    )(slab, run, late, last, follow)
 
 
 def join(mine, got, got_first):
@@ -248,8 +305,8 @@
 
 def neighbours(near, far):
     count = lax.axis_size("col")
+    far = lax.ppermute(far, "col", pairs(range(1, count - 1, 2), range(2, count, 2)))
     near = lax.ppermute(near, "col", pairs(range(0, count - 1, 2), range(1, count, 2)))
-    far = lax.ppermute(far, "col", pairs(range(1, count - 1, 2), range(2, count, 2)))
     return near, far
 
 
@@ -270,13 +327,15 @@
     slab = lax.axis_index("slab").reshape(1).astype(jnp.int32)
     col = lax.axis_index("col").reshape(1).astype(jnp.int32)
     follow = lax.ppermute(field[:, :1], "slab", [(i + 1, i) for i in range(slabs - 1)])
-    args = (field, follow, fine_plane, fine_frac, counts, slab)
-    if width % LANES:
-        parts = march(*args, columns // LANES, lambda b, s: b, LANES, False)
+    block = width if width % LANES == 0 else LANES
+    ahead = march(field, fine_plane, fine_frac, counts, slab, block)
+    close_ = functools.partial(close, *ahead, follow, slab, field.shape[1])
+    if width != block:
+        parts = close_(columns // block, lambda b, s: b, False)
         image, near, far = finish(wide_exchange(parts, slabs, width), None, slab, 0, col)
         return border(image, *neighbours(near, far), col)
-    send = march(*args, slabs // 2, lambda b, s: 2 * b + 1 - (s & 1), width, True)
-    keep = march(*args, slabs // 2, lambda b, s: 2 * b + (s & 1), width, False)
+    send = close_(slabs // 2, lambda b, s: 2 * b + 1 - (s & 1), True)
+    keep = close_(slabs // 2, lambda b, s: 2 * b + (s & 1), False)
     bit = 0
     while True:
         low = [i for i in range(slabs) if not (i >> bit) & 1]

time: 34.1 us -> 29 us (0.85)
  the two profiles are of different devices: /device:TPU:3 before, /device:TPU:27 now
where the time goes in v2:
time: 29 us; the launch traced here: 28.8 us
  waiting for transfers between devices  11.7 us (40%)
  starting transfers between devices  8.47 us (29%)
  Pallas kernels  7.06 us (24%)
  local copies, waits for them, and re-layouts  0.92 us (3%)
  between operations  0.7 us (2%)
    ppermute x2, waiting for transfers between devices, body(): got = lax.ppermute(send, 'slab', pairs(low, [i + (1 << bit) for i in low]))  8.87 us
    pallas_call x1, Pallas kernels, march(): pl.pallas_call(kernel, grid=(blocks,), in_specs=[smem(), spec(2, depth),...  4.7 us
    ppermute x1, starting transfers between devices, neighbours(): lax.ppermute(near, 'col', pairs(range(0, count - 1, 2), range(1, count, 2)))  3.05 us
    ppermute x1, starting transfers between devices, neighbours(): lax.ppermute(far, 'col', pairs(range(1, count - 1, 2), range(2, count, 2)))  3.02 us
    ppermute x1, waiting for transfers between devices, neighbours(): lax.ppermute(far, 'col', pairs(range(1, count - 1, 2), range(2, count, 2)))  2.78 us
    ppermute x1, starting transfers between devices, body(): lax.ppermute(field[:, :1], 'slab', [(i + 1, i) for i in range(slabs - 1)])  2.08 us
    pallas_call x2, Pallas kernels, close(): pl.pallas_call(kernel, in_specs=[smem()] + [vmem()] * 4, out_specs=vmem()...  1.46 us
    slice x1, local copies, waits for them, and re-layouts, body(): field[:, :1]  0.92 us
  transfers between devices with their start and end apart: 5, of which 3 were waited for; matrix products, arithmetic and copies ran while one was open for 0% of the time, Pallas kernels for 19%

profile of v2, /device:TPU:27, one launch (start us, length us, event | category | flops | bytes accessed | tf_op | source)
XLA Modules:
  0.0 28.8 jit_solution(7839207553555219199)
XLA Ops:
  0.6 0.9 %slice.3 = bf16[2,1,32,1024]{3,2,1,0:T(8,128)(2,1)S(1)} slice(bf16[2,16,32,1024]{3,2,1,0:T(8,128)(2,1)} %field.1), slice={[0:2], [0:1], [0:32], [0:1024]} | slice | bytes 262144 | tf_op jit(solution)/shard_map/slice | solution.py:329
  1.6 2.1 %collective-permute-start = (bf16[2,1,32,1024]{3,2,1,0:T(8,128)(2,1)S(1)}, bf16[2,1,32,1024]{3,2,1,0:T(8,128)(2,1)S(1)}, u32[]{:S(2)}, u32[]{:S(2)}) collective-permute-start(bf16[2,1,32,1024]{3,2,1,0:T(8,128)(2,1)S(1)} %slice.3), channel_id=1, source_target_pairs={{8,0},{16,8},{24,16},{9,1},{17,9},{25,17},{10,2},{18,10},{26,18},{... | collective-permute-start | bytes 393224 | tf_op jit(solution)/shard_map/ppermute | solution.py:329
  3.6 4.7 %march.1 = (f32[4,5,32,256]{3,2,1,0:T(8,128)S(1)}, bf16[4,8,32,256]{3,2,1,0:T(8,128)(2,1)S(1)}, bf16[4,2,32,256]{3,2,1,0:T(8,128)(2,1)S(1)}) custom-call(s32[1]{0:T(128)} %bitcast.1.slab_ref, bf16[2,16,32,1024]{3,2,1,0:T(8,128)(2,1)} %field.1, s32[8,32,1024]{2,1,0:T(8,128)} %plane.1, s32[8,32,1024]{2,1,0:T(8,128)} %frac.1, s32[1,32,1024]{2,1,0:T(8,128)} %counts.1), custom_call_target="tpu_custom_call" | custom-call | flops 98304000 | bytes 4194304 | tf_op jit(solution)/shard_map/march/pallas_call | solution.py:135
  8.3 0.0 collective-permute-done.follow
  8.4 0.8 %close.3 = s16[2,5,32,256]{3,2,1,0:T(8,128)(2,1)S(1)} custom-call(s32[1]{0:T(128)} %bitcast.1.slab_ref, f32[4,5,32,256]{3,2,1,0:T(8,128)S(1)} %get-tuple-element.11.run, bf16[4,8,32,256]{3,2,1,0:T(8,128)(2,1)S(1)} %get-tuple-element.12.late, bf16[4,2,32,256]{3,2,1,0:T(8,128)(2,1)S(1)} %get-tuple-element.13.last, ...), custom_call_target="tpu_custom_call" | custom-call | flops 24576000 | bytes 1048576 | tf_op jit(solution)/shard_map/close/pallas_call | solution.py:190
  9.2 0.2 collective-permute-start.1
  9.4 0.7 %close.2.mine = f32[2,5,32,256]{3,2,1,0:T(8,128)S(1)} custom-call(s32[1]{0:T(128)} %bitcast.1.slab_ref, f32[4,5,32,256]{3,2,1,0:T(8,128)S(1)} %get-tuple-element.11.run, bf16[4,8,32,256]{3,2,1,0:T(8,128)(2,1)S(1)} %get-tuple-element.12.late, bf16[4,2,32,256]{3,2,1,0:T(8,128)(2,1)S(1)} %get-tuple-element.13.last, ...), custom_call_target="tpu_custom_call" | custom-call | flops 24576000 | bytes 1048576 | tf_op jit(solution)/shard_map/close/pallas_call | solution.py:190
  10.1 4.0 %collective-permute-done.1.got = s16[2,5,32,256]{3,2,1,0:T(8,128)(2,1)S(1)} collective-permute-done((s16[2,5,32,256]{3,2,1,0:T(8,128)(2,1)S(1)}, s16[2,5,32,256]{3,2,1,0:T(8,128)(2,1)S(1)}, u32[]{:S(2)}, u32[]{:S(2)}) %collective-permute-start.1) | collective-permute-done | bytes 163872 | tf_op jit(solution)/shard_map/ppermute | solution.py:342
  14.0 0.2 halve.1
  14.2 0.1 collective-permute-start.2
  14.3 4.9 %collective-permute-done.2.refs_0_ = s16[1,5,32,256]{3,2,1,0:T(8,128)(2,1)S(1)} collective-permute-done((s16[1,5,32,256]{3,2,1,0:T(8,128)(2,1)S(1)}, s16[1,5,32,256]{3,2,1,0:T(8,128)(2,1)S(1)}, u32[]{:S(2)}, u32[]{:S(2)}) %collective-permute-start.2) | collective-permute-done | bytes 81952 | tf_op jit(solution)/shard_map/ppermute | solution.py:342
  19.2 0.1 finish.1
  19.3 3.1 %collective-permute-start.3 = (f32[3,256]{1,0:T(4,128)S(1)}, f32[3,256]{1,0:T(4,128)S(1)}, u32[]{:S(2)}, u32[]{:S(2)}) collective-permute-start(f32[3,256]{1,0:T(4,128)S(1)} %get-tuple-element.17), channel_id=1, source_target_pairs={{0,1},{2,3},{4,5},{6,7},{1,0},{3,2},{5,4},{7,6},{8,9},{10,11},{12,... | collective-permute-start | bytes 9224 | tf_op jit(solution)/shard_map/ppermute | solution.py:309
  22.3 3.0 %collective-permute-start.4 = (f32[3,256]{1,0:T(4,128)S(1)}, f32[3,256]{1,0:T(4,128)S(1)}, u32[]{:S(2)}, u32[]{:S(2)}) collective-permute-start(f32[3,256]{1,0:T(4,128)S(1)} %get-tuple-element.18), channel_id=1, source_target_pairs={{1,2},{3,4},{5,6},{2,1},{4,3},{6,5},{9,10},{11,12},{13,14},{10,9},... | collective-permute-start | bytes 9224 | tf_op jit(solution)/shard_map/ppermute | solution.py:308
  25.4 0.0 collective-permute-done.3.near
  25.4 2.8 %collective-permute-done.4.far = f32[3,256]{1,0:T(4,128)S(1)} collective-permute-done((f32[3,256]{1,0:T(4,128)S(1)}, f32[3,256]{1,0:T(4,128)S(1)}, u32[]{:S(2)}, u32[]{:S(2)}) %collective-permute-start.4) | collective-permute-done | bytes 3104 | tf_op jit(solution)/shard_map/ppermute | solution.py:308
  28.2 0.6 %border.1 = (f32[32,256]{1,0:T(8,128)}, f32[32,256]{1,0:T(8,128)}, f32[32,256]{1,0:T(8,128)}) custom-call(s32[1]{0:T(128)} %bitcast.col_ref, f32[3,32,256]{2,1,0:T(8,128)S(1)} %get-tuple-element.16.image, f32[3,256]{1,0:T(4,128)S(1)} %collective-permute-done.3.near, f32[3,256]{1,0:T(4,128)S(1)} %collective-permute-done.4.far), custom_call_target="tpu_custom_call" | custom-call | tf_op jit(solution)/shard_map/border/pallas_call | solution.py:291
Async XLA Ops:
  1.6 6.8 %collective-permute-start = (bf16[2,1,32,1024]{3,2,1,0:T(8,128)(2,1)S(1)}, bf16[2,1,32,1024]{3,2,1,0:T(8,128)(2,1)S(1)}, u32[]{:S(2)}, u32[]{:S(2)}) collective-permute-start(bf16[2,1,32,1024]{3,2,1,0:T(8,128)(2,1)S(1)} %slice.3), channel_id=1, source_target_pairs={{8,0},{16,8},{24,16},{9,1},{17,9},{25,17},{10,2},{18,10},{26,18},{... | collective-permute-start | bytes 393224 | tf_op jit(solution)/shard_map/ppermute | solution.py:329
  9.2 4.9 %collective-permute-start.1 = (s16[2,5,32,256]{3,2,1,0:T(8,128)(2,1)S(1)}, s16[2,5,32,256]{3,2,1,0:T(8,128)(2,1)S(1)}, u32[]{:S(2)}, u32[]{:S(2)}) collective-permute-start(s16[2,5,32,256]{3,2,1,0:T(8,128)(2,1)S(1)} %close.3), channel_id=1, source_target_pairs={{0,8},{16,24},{8,0},{24,16},{1,9},{17,25},{9,1},{25,17},{2,10},{18... | collective-permute-start | bytes 491528 | tf_op jit(solution)/shard_map/ppermute | solution.py:342
  14.2 5.0 %collective-permute-start.2 = (s16[1,5,32,256]{3,2,1,0:T(8,128)(2,1)S(1)}, s16[1,5,32,256]{3,2,1,0:T(8,128)(2,1)S(1)}, u32[]{:S(2)}, u32[]{:S(2)}) collective-permute-start(s16[1,5,32,256]{3,2,1,0:T(8,128)(2,1)S(1)} %get-tuple-element.15), channel_id=1, source_target_pairs={{0,16},{8,24},{16,0},{24,8},{1,17},{9,25},{17,1},{25,9},{2,18},{10... | collective-permute-start | bytes 245768 | tf_op jit(solution)/shard_map/ppermute | solution.py:342
  19.3 6.1 %collective-permute-start.3 = (f32[3,256]{1,0:T(4,128)S(1)}, f32[3,256]{1,0:T(4,128)S(1)}, u32[]{:S(2)}, u32[]{:S(2)}) collective-permute-start(f32[3,256]{1,0:T(4,128)S(1)} %get-tuple-element.17), channel_id=1, source_target_pairs={{0,1},{2,3},{4,5},{6,7},{1,0},{3,2},{5,4},{7,6},{8,9},{10,11},{12,... | collective-permute-start | bytes 9224 | tf_op jit(solution)/shard_map/ppermute | solution.py:309
  22.3 5.8 %collective-permute-start.4 = (f32[3,256]{1,0:T(4,128)S(1)}, f32[3,256]{1,0:T(4,128)S(1)}, u32[]{:S(2)}, u32[]{:S(2)}) collective-permute-start(f32[3,256]{1,0:T(4,128)S(1)} %get-tuple-element.18), channel_id=1, source_target_pairs={{1,2},{3,4},{5,6},{2,1},{4,3},{6,5},{9,10},{11,12},{13,14},{10,9},... | collective-permute-start | bytes 9224 | tf_op jit(solution)/shard_map/ppermute | solution.py:308

commit v3 on v2

--- a/solution.py
+++ b/solution.py
@@ -14,7 +14,6 @@
 OCTAVES = 24.0
 STEPS = 65534.0 / OCTAVES
 WIRE = jnp.int16
-MARCH_LIMIT = 24 << 20
 
 
 def vmem():
@@ -109,9 +108,9 @@
     lax.fori_loop(0, (rows // ROWS) * across, one, 0)
 
 
-def march(field, plane, frac, counts, slab, width):
-    _, depth, rows, columns = field.shape
-    slots, blocks = plane.shape[0], columns // width
+def march(field, plane, frac, counts, slab, steps, block_of, width):
+    _, depth, rows, _ = field.shape
+    slots = plane.shape[0]
     total_depth = depth * lax.axis_size("slab")
 
     def kernel(slab_ref, field, plane, frac, counts, run, late, last):
@@ -123,33 +122,39 @@
 
     def spec(*lead):
         zeros = (0,) * len(lead)
-        return pl.BlockSpec(lead + (rows, width), lambda b: zeros + (0, b))
+        return pl.BlockSpec(lead + (rows, width), lambda b, s: zeros + (0, block_of(b, s[0])))
 
     def out(*lead):
         zeros = (0,) * len(lead)
-        return pl.BlockSpec((1,) + lead + (rows, width), lambda b: (b,) + zeros + (0, 0))
+        return pl.BlockSpec((1,) + lead + (rows, width), lambda b, s: (b,) + zeros + (0, 0))
 
     def shape(*lead, kind):
-        return jax.ShapeDtypeStruct((blocks,) + lead + (rows, width), kind)
-
-    return pl.pallas_call(
-        kernel,
-        grid=(blocks,),
-        in_specs=[smem(), spec(2, depth), spec(slots), spec(slots), spec(1)],
-        out_specs=[out(5), out(slots), out(2)],
+        return jax.ShapeDtypeStruct((steps,) + lead + (rows, width), kind)
+
+    return pl.pallas_call(
+        kernel,
+        grid_spec=pltpu.PrefetchScalarGridSpec(
+            num_scalar_prefetch=1,
+            grid=(steps,),
+            in_specs=[spec(2, depth), spec(slots), spec(slots), spec(1)],
+            out_specs=[out(5), out(slots), out(2)],
+        ),
         out_shape=[
             shape(5, kind=jnp.float32), shape(slots, kind=jnp.bfloat16),
             shape(2, kind=jnp.bfloat16),
         ],
-        compiler_params=pltpu.CompilerParams(vmem_limit_bytes=MARCH_LIMIT),
+        compiler_params=pltpu.CompilerParams(vmem_limit_bytes=24 << 20),
         cost_estimate=pl.CostEstimate(
-            flops=rows * columns * 3000, bytes_accessed=rows * columns * 128, transcendentals=0
+            flops=steps * rows * width * 3000, bytes_accessed=steps * rows * width * 128,
+            transcendentals=0,
         ),
         name="march",
-    )(slab, *(pltpu.with_memory_space_constraint(x, pltpu.HBM) for x in (field, plane, frac, counts)))
-
-
-def close(run, late, last, follow, slab, depth, steps, block_of, coded):
+    )(slab, *(pltpu.with_memory_space_constraint(x, pltpu.HBM)
+              for x in (field, plane, frac, counts)))
+
+
+def close(ahead, follow, slab, depth, first, steps, block_of, coded):
+    run, late, last = ahead
     _, slots, rows, width = late.shape
     total_depth = depth * lax.axis_size("slab")
 
@@ -158,8 +163,9 @@
         base = (s * (8 * depth) + 8 * (depth - 1)).astype(jnp.float32)
 
         def step(i, here, cols):
-            b = block_of(i, s)
-            there = pl.ds(pl.multiple_of(b * width + cols.start, LANES), LANES)
+            b = first + i
+            start = block_of(b, s) * width + cols.start
+            there = pl.ds(pl.multiple_of(start, LANES), LANES)
             low = [last[b, ch, here, cols].astype(jnp.float32) for ch in (0, 1)]
             high = [follow[ch, 0, here, there].astype(jnp.float32) for ch in (0, 1)]
             slope = [(h - l) * 0.125 for h, l in zip(high, low)]
@@ -213,46 +219,40 @@
     ]
 
 
-def halve(mine, got, slab, bit):
-    blocks, kinds, rows, width = mine.shape
-
-    def kernel(slab_ref, mine, got, send, keep):
-        got_first = (slab_ref[0] >> bit) & 1 == 1
-        want = (slab_ref[0] >> (bit + 1)) & 1
-        for i in range(blocks // 2):
-            for out, at in ((send, 2 * i + 1 - want), (keep, 2 * i + want)):
-                for r in range(0, rows, ROWS):
-                    here = pl.ds(r, ROWS)
-                    done = join(
-                        [mine[at, what, here, :] for what in range(kinds)],
-                        [decode(got[at, what, here, :]) for what in range(kinds)],
-                        got_first,
-                    )
-                    for what in range(kinds):
-                        out[i, what, here, :] = (
-                            encode(done[what]) if out is send else done[what]
-                        )
-
-    shape = (blocks // 2, kinds, rows, width)
+def relay(mine, got, slab):
+    _, kinds, rows, _ = mine.shape
+
+    def kernel(slab_ref, mine, got, send):
+        got_first = slab_ref[0] & 1 == 1
+        for r in range(0, rows, ROWS):
+            here = pl.ds(r, ROWS)
+            done = join(
+                [mine[0, what, here, :] for what in range(kinds)],
+                [decode(got[0, what, here, :]) for what in range(kinds)],
+                got_first,
+            )
+            for what in range(kinds):
+                send[0, what, here, :] = encode(done[what])
+
     return pl.pallas_call(
         kernel,
         in_specs=[smem(), vmem(), vmem()],
-        out_specs=[vmem(), vmem()],
-        out_shape=[jax.ShapeDtypeStruct(shape, WIRE), jax.ShapeDtypeStruct(shape, jnp.float32)],
+        out_specs=vmem(),
+        out_shape=jax.ShapeDtypeStruct(got.shape, WIRE),
         compiler_params=pltpu.CompilerParams(vmem_limit_bytes=16 << 20),
-        name="halve",
+        name="relay",
     )(slab, mine, got)
 
 
-def finish(mine, got, slab, bit, col):
+def finish(mine, got, slab, col):
     _, kinds, rows, width = mine.shape
-    runs = [mine] if got is None else [mine, got]
+    runs = [mine, *got]
 
     def kernel(slab_ref, col_ref, mine, *refs):
         *partner, image, near, far = refs
         odd = col_ref[0] % 2 == 1
         done = [mine[0, what] for what in range(kinds)]
-        for got in partner:
+        for bit, got in enumerate(partner):
             got_first = (slab_ref[0] >> bit) & 1 == 1
             done = join(done, [decode(got[0, what]) for what in range(kinds)], got_first)
         row = lax.broadcasted_iota(jnp.int32, (rows, width), 0)
@@ -311,7 +311,7 @@
 
 
 def wide_exchange(parts, slabs, width):
-    blocks, kinds, rows, lanes = parts.shape
+    _, kinds, rows, _ = parts.shape
     tiles = parts.transpose(1, 2, 0, 3).reshape(kinds, rows, slabs, width).transpose(2, 0, 1, 3)
     got = lax.all_to_all(tiles, "slab", 0, 0)
     done = [got[0, what] for what in range(kinds)]
@@ -320,33 +320,45 @@
     return jnp.stack(done)[None]
 
 
+def swap(x, count, distance):
+    low = [i for i in range(count) if not i & distance]
+    return lax.ppermute(x, "slab", pairs(low, [i + distance for i in low]))
+
+
 def body(field, fine_plane, fine_frac, counts):
     slabs = lax.axis_size("slab")
-    columns = field.shape[3]
+    depth, columns = field.shape[1], field.shape[3]
     width = columns // slabs
     slab = lax.axis_index("slab").reshape(1).astype(jnp.int32)
     col = lax.axis_index("col").reshape(1).astype(jnp.int32)
+    fast = slabs == 4 and width % LANES == 0
+    block = width if fast else LANES
+    blocks = columns // block
+
+    def block_of(b, s):
+        if not fast:
+            return b
+        parity = jnp.where(b < 2, 1 - (s & 1), s & 1)
+        return 2 * (((s >> 1) & 1) ^ 1 ^ (b & 1)) + parity
+
     follow = lax.ppermute(field[:, :1], "slab", [(i + 1, i) for i in range(slabs - 1)])
-    block = width if width % LANES == 0 else LANES
-    ahead = march(field, fine_plane, fine_frac, counts, slab, block)
-    close_ = functools.partial(close, *ahead, follow, slab, field.shape[1])
-    if width != block:
-        parts = close_(columns // block, lambda b, s: b, False)
-        image, near, far = finish(wide_exchange(parts, slabs, width), None, slab, 0, col)
+    ahead = march(field, fine_plane, fine_frac, counts, slab, blocks, block_of, block)
+
+    def part(first, steps, coded):
+        return close(ahead, follow, slab, depth, first, steps, block_of, coded)
+
+    if not fast:
+        parts = part(0, blocks, False)
+        image, near, far = finish(wide_exchange(parts, slabs, width), (), slab, col)
         return border(image, *neighbours(near, far), col)
-    send = close_(slabs // 2, lambda b, s: 2 * b + 1 - (s & 1), True)
-    keep = close_(slabs // 2, lambda b, s: 2 * b + (s & 1), False)
-    bit = 0
-    while True:
-        low = [i for i in range(slabs) if not (i >> bit) & 1]
-        got = lax.ppermute(send, "slab", pairs(low, [i + (1 << bit) for i in low]))
-        if 2 << bit == slabs:
-            break
-        send, keep = halve(keep, got, slab, bit)
-        bit += 1
-    image, near, far = finish(keep, got, slab, bit, col)
-    near, far = neighbours(near, far)
-    return border(image, near, far, col)
+
+    got_a = swap(part(0, 1, True), slabs, 1)
+    keep_a = part(2, 1, False)
+    got = swap(relay(keep_a, got_a, slab), slabs, 2)
+    got_b = swap(part(1, 1, True), slabs, 1)
+    keep_b = part(3, 1, False)
+    image, near, far = finish(keep_b, (got_b, got), slab, col)
+    return border(image, *neighbours(near, far), col)
 
 
 def solution(mesh):
@@ -357,4 +369,5 @@
         P("slab", "col", None),
     )
     out_specs = (P("col", "slab"), P("col", "slab"), P("col", "slab"))
+
     return jax.shard_map(body, mesh=mesh, in_specs=in_specs, out_specs=out_specs, check_vma=False)

time: 29 us -> 27.9 us (0.962)
  waiting for transfers between devices: 11.7 us -> 8.37 us
  starting transfers between devices: 8.47 us -> 10.6 us
    ppermute x2 -> x3, waiting for transfers between devices: 8.87 us -> 5.58 us  [swap(): return lax.ppermute(x, 'slab', pairs(low, [i + distance for i in low]))]
    ppermute x2 -> x3, starting transfers between devices: 0.32 us -> 1.71 us  [swap(): return lax.ppermute(x, 'slab', pairs(low, [i + distance for i in low]))]
    ppermute x1, starting transfers between devices: 3.05 us -> 3.78 us  [neighbours(): lax.ppermute(near, 'col', pairs(range(0, count - 1, 2), range(1, count, 2)))]
    pallas_call x2 -> x4, Pallas kernels: 1.46 us -> 1.47 us  [close(): pl.pallas_call(kernel, in_specs=[smem()] + [vmem()] * 4, out_specs=vmem()...]
  transfers between devices with their start and end apart: 5 -> 6, of which waited for: 3 -> 4; matrix products, arithmetic and copies ran while one was open for 0% -> 0% of each run, Pallas kernels for 19% -> 21%
where the time goes in v3:
time: 27.9 us; the launch traced here: 27.7 us
  starting transfers between devices  10.6 us (38%)
  waiting for transfers between devices  8.37 us (30%)
  Pallas kernels  7.11 us (25%)
  local copies, waits for them, and re-layouts  0.92 us (3%)
  between operations  0.71 us (3%)
    ppermute x3, waiting for transfers between devices, swap(): return lax.ppermute(x, 'slab', pairs(low, [i + distance for i in low]))  5.58 us
    pallas_call x1, Pallas kernels, march(): pl.pallas_call(kernel, grid_spec=pltpu.PrefetchScalarGridSpec(num_scalar_...  4.72 us
    ppermute x1, starting transfers between devices, neighbours(): lax.ppermute(near, 'col', pairs(range(0, count - 1, 2), range(1, count, 2)))  3.78 us
    ppermute x1, starting transfers between devices, neighbours(): lax.ppermute(far, 'col', pairs(range(1, count - 1, 2), range(2, count, 2)))  3.02 us
    ppermute x1, waiting for transfers between devices, neighbours(): lax.ppermute(far, 'col', pairs(range(1, count - 1, 2), range(2, count, 2)))  2.78 us
    ppermute x1, starting transfers between devices, body(): lax.ppermute(field[:, :1], 'slab', [(i + 1, i) for i in range(slabs - 1)])  2.08 us
    ppermute x3, starting transfers between devices, swap(): return lax.ppermute(x, 'slab', pairs(low, [i + distance for i in low]))  1.71 us
    pallas_call x4, Pallas kernels, close(): pl.pallas_call(kernel, in_specs=[smem()] + [vmem()] * 4, out_specs=vmem()...  1.47 us
  transfers between devices with their start and end apart: 6, of which 4 were waited for; matrix products, arithmetic and copies ran while one was open for 0% of the time, Pallas kernels for 21%

profile of v3, /device:TPU:27, one launch (start us, length us, event | category | flops | bytes accessed | tf_op | source)
XLA Modules:
  0.0 27.7 jit_solution(8078513815637126058)
XLA Ops:
  0.6 0.9 %slice.3 = bf16[2,1,32,1024]{3,2,1,0:T(8,128)(2,1)S(1)} slice(bf16[2,16,32,1024]{3,2,1,0:T(8,128)(2,1)} %field.1), slice={[0:2], [0:1], [0:32], [0:1024]} | slice | bytes 262144 | tf_op jit(solution)/shard_map/slice | solution.py:344
  1.6 2.1 %collective-permute-start = (bf16[2,1,32,1024]{3,2,1,0:T(8,128)(2,1)S(1)}, bf16[2,1,32,1024]{3,2,1,0:T(8,128)(2,1)S(1)}, u32[]{:S(2)}, u32[]{:S(2)}) collective-permute-start(bf16[2,1,32,1024]{3,2,1,0:T(8,128)(2,1)S(1)} %slice.3), channel_id=1, source_target_pairs={{8,0},{16,8},{24,16},{9,1},{17,9},{25,17},{10,2},{18,10},{26,18},{... | collective-permute-start | bytes 393224 | tf_op jit(solution)/shard_map/ppermute | solution.py:344
  3.6 4.7 %march.1 = (f32[4,5,32,256]{3,2,1,0:T(8,128)S(1)}, bf16[4,8,32,256]{3,2,1,0:T(8,128)(2,1)S(1)}, bf16[4,2,32,256]{3,2,1,0:T(8,128)(2,1)S(1)}) custom-call(s32[1]{0:T(128)} %bitcast.1.slab_ref, bf16[2,16,32,1024]{3,2,1,0:T(8,128)(2,1)} %field.1, s32[8,32,1024]{2,1,0:T(8,128)} %plane.1, s32[8,32,1024]{2,1,0:T(8,128)} %frac.1, s32[1,32,1024]{2,1,0:T(8,128)} %counts.1), custom_call_target="tpu_custom_call" | custom-call | flops 98304000 | bytes 4194304 | tf_op jit(solution)/shard_map/march/pallas_call | solution.py:134
  8.4 0.0 collective-permute-done.follow
  8.4 0.4 %close.7 = s16[1,5,32,256]{3,2,1,0:T(8,128)(2,1)S(1)} custom-call(s32[1]{0:T(128)} %bitcast.1.slab_ref, f32[4,5,32,256]{3,2,1,0:T(8,128)S(1)} %get-tuple-element.9.run, bf16[4,8,32,256]{3,2,1,0:T(8,128)(2,1)S(1)} %get-tuple-element.10.late, bf16[4,2,32,256]{3,2,1,0:T(8,128)(2,1)S(1)} %get-tuple-element.11.last, ...), custom_call_target="tpu_custom_call" | custom-call | flops 12288000 | bytes 524288 | tf_op jit(solution)/shard_map/close/pallas_call | solution.py:196
  8.8 0.2 collective-permute-start.2
  9.0 0.4 %close.5 = s16[1,5,32,256]{3,2,1,0:T(8,128)(2,1)S(1)} custom-call(s32[1]{0:T(128)} %bitcast.1.slab_ref, f32[4,5,32,256]{3,2,1,0:T(8,128)S(1)} %get-tuple-element.9.run, bf16[4,8,32,256]{3,2,1,0:T(8,128)(2,1)S(1)} %get-tuple-element.10.late, bf16[4,2,32,256]{3,2,1,0:T(8,128)(2,1)S(1)} %get-tuple-element.11.last, ...), custom_call_target="tpu_custom_call" | custom-call | flops 12288000 | bytes 524288 | tf_op jit(solution)/shard_map/close/pallas_call | solution.py:196
  9.4 1.4 %collective-permute-start.1 = (s16[1,5,32,256]{3,2,1,0:T(8,128)(2,1)S(1)}, s16[1,5,32,256]{3,2,1,0:T(8,128)(2,1)S(1)}, u32[]{:S(2)}, u32[]{:S(2)}) collective-permute-start(s16[1,5,32,256]{3,2,1,0:T(8,128)(2,1)S(1)} %close.5), channel_id=1, source_target_pairs={{0,8},{16,24},{8,0},{24,16},{1,9},{17,25},{9,1},{25,17},{2,10},{18... | collective-permute-start | bytes 245768 | tf_op jit(solution)/shard_map/ppermute | solution.py:325
  10.8 0.3 %close.6.mine = f32[1,5,32,256]{3,2,1,0:T(8,128)S(1)} custom-call(s32[1]{0:T(128)} %bitcast.1.slab_ref, f32[4,5,32,256]{3,2,1,0:T(8,128)S(1)} %get-tuple-element.9.run, bf16[4,8,32,256]{3,2,1,0:T(8,128)(2,1)S(1)} %get-tuple-element.10.late, bf16[4,2,32,256]{3,2,1,0:T(8,128)(2,1)S(1)} %get-tuple-element.11.last, ...), custom_call_target="tpu_custom_call" | custom-call | flops 12288000 | bytes 524288 | tf_op jit(solution)/shard_map/close/pallas_call | solution.py:196
  11.1 1.0 %collective-permute-done.2.got = s16[1,5,32,256]{3,2,1,0:T(8,128)(2,1)S(1)} collective-permute-done((s16[1,5,32,256]{3,2,1,0:T(8,128)(2,1)S(1)}, s16[1,5,32,256]{3,2,1,0:T(8,128)(2,1)S(1)}, u32[]{:S(2)}, u32[]{:S(2)}) %collective-permute-start.2) | collective-permute-done | bytes 81952 | tf_op jit(solution)/shard_map/ppermute | solution.py:325
  12.2 0.1 relay.1
  12.3 0.1 collective-permute-start.3
  12.4 0.3 %close.4.mine = f32[1,5,32,256]{3,2,1,0:T(8,128)S(1)} custom-call(s32[1]{0:T(128)} %bitcast.1.slab_ref, f32[4,5,32,256]{3,2,1,0:T(8,128)S(1)} %get-tuple-element.9.run, bf16[4,8,32,256]{3,2,1,0:T(8,128)(2,1)S(1)} %get-tuple-element.10.late, bf16[4,2,32,256]{3,2,1,0:T(8,128)(2,1)S(1)} %get-tuple-element.11.last, ...), custom_call_target="tpu_custom_call" | custom-call | flops 12288000 | bytes 524288 | tf_op jit(solution)/shard_map/close/pallas_call | solution.py:196
  12.7 0.9 %collective-permute-done.1.refs_0_ = s16[1,5,32,256]{3,2,1,0:T(8,128)(2,1)S(1)} collective-permute-done((s16[1,5,32,256]{3,2,1,0:T(8,128)(2,1)S(1)}, s16[1,5,32,256]{3,2,1,0:T(8,128)(2,1)S(1)}, u32[]{:S(2)}, u32[]{:S(2)}) %collective-permute-start.1) | collective-permute-done | bytes 81952 | tf_op jit(solution)/shard_map/ppermute | solution.py:325
  13.7 3.6 %collective-permute-done.3.refs_1_ = s16[1,5,32,256]{3,2,1,0:T(8,128)(2,1)S(1)} collective-permute-done((s16[1,5,32,256]{3,2,1,0:T(8,128)(2,1)S(1)}, s16[1,5,32,256]{3,2,1,0:T(8,128)(2,1)S(1)}, u32[]{:S(2)}, u32[]{:S(2)}) %collective-permute-start.3) | collective-permute-done | bytes 81952 | tf_op jit(solution)/shard_map/ppermute | solution.py:325
  17.3 0.2 finish.1
  17.5 3.8 %collective-permute-start.4 = (f32[3,256]{1,0:T(4,128)S(1)}, f32[3,256]{1,0:T(4,128)S(1)}, u32[]{:S(2)}, u32[]{:S(2)}) collective-permute-start(f32[3,256]{1,0:T(4,128)S(1)} %get-tuple-element.13), channel_id=1, source_target_pairs={{0,1},{2,3},{4,5},{6,7},{1,0},{3,2},{5,4},{7,6},{8,9},{10,11},{12,... | collective-permute-start | bytes 9224 | tf_op jit(solution)/shard_map/ppermute | solution.py:309
  21.2 3.0 %collective-permute-start.5 = (f32[3,256]{1,0:T(4,128)S(1)}, f32[3,256]{1,0:T(4,128)S(1)}, u32[]{:S(2)}, u32[]{:S(2)}) collective-permute-start(f32[3,256]{1,0:T(4,128)S(1)} %get-tuple-element.14), channel_id=1, source_target_pairs={{1,2},{3,4},{5,6},{2,1},{4,3},{6,5},{9,10},{11,12},{13,14},{10,9},... | collective-permute-start | bytes 9224 | tf_op jit(solution)/shard_map/ppermute | solution.py:308
  24.3 0.0 collective-permute-done.4.near
  24.3 2.8 %collective-permute-done.5.far = f32[3,256]{1,0:T(4,128)S(1)} collective-permute-done((f32[3,256]{1,0:T(4,128)S(1)}, f32[3,256]{1,0:T(4,128)S(1)}, u32[]{:S(2)}, u32[]{:S(2)}) %collective-permute-start.5) | collective-permute-done | bytes 3104 | tf_op jit(solution)/shard_map/ppermute | solution.py:308
  27.0 0.6 %border.1 = (f32[32,256]{1,0:T(8,128)}, f32[32,256]{1,0:T(8,128)}, f32[32,256]{1,0:T(8,128)}) custom-call(s32[1]{0:T(128)} %bitcast.col_ref, f32[3,32,256]{2,1,0:T(8,128)S(1)} %get-tuple-element.12.image, f32[3,256]{1,0:T(4,128)S(1)} %collective-permute-done.4.near, f32[3,256]{1,0:T(4,128)S(1)} %collective-permute-done.5.far), custom_call_target="tpu_custom_call" | custom-call | tf_op jit(solution)/shard_map/border/pallas_call | solution.py:291
Async XLA Ops:
  1.6 6.8 %collective-permute-start = (bf16[2,1,32,1024]{3,2,1,0:T(8,128)(2,1)S(1)}, bf16[2,1,32,1024]{3,2,1,0:T(8,128)(2,1)S(1)}, u32[]{:S(2)}, u32[]{:S(2)}) collective-permute-start(bf16[2,1,32,1024]{3,2,1,0:T(8,128)(2,1)S(1)} %slice.3), channel_id=1, source_target_pairs={{8,0},{16,8},{24,16},{9,1},{17,9},{25,17},{10,2},{18,10},{26,18},{... | collective-permute-start | bytes 393224 | tf_op jit(solution)/shard_map/ppermute | solution.py:344
  8.8 3.4 %collective-permute-start.2 = (s16[1,5,32,256]{3,2,1,0:T(8,128)(2,1)S(1)}, s16[1,5,32,256]{3,2,1,0:T(8,128)(2,1)S(1)}, u32[]{:S(2)}, u32[]{:S(2)}) collective-permute-start(s16[1,5,32,256]{3,2,1,0:T(8,128)(2,1)S(1)} %close.7), channel_id=1, source_target_pairs={{0,8},{16,24},{8,0},{24,16},{1,9},{17,25},{9,1},{25,17},{2,10},{18... | collective-permute-start | bytes 245768 | tf_op jit(solution)/shard_map/ppermute | solution.py:325
  9.4 4.2 %collective-permute-start.1 = (s16[1,5,32,256]{3,2,1,0:T(8,128)(2,1)S(1)}, s16[1,5,32,256]{3,2,1,0:T(8,128)(2,1)S(1)}, u32[]{:S(2)}, u32[]{:S(2)}) collective-permute-start(s16[1,5,32,256]{3,2,1,0:T(8,128)(2,1)S(1)} %close.5), channel_id=1, source_target_pairs={{0,8},{16,24},{8,0},{24,16},{1,9},{17,25},{9,1},{25,17},{2,10},{18... | collective-permute-start | bytes 245768 | tf_op jit(solution)/shard_map/ppermute | solution.py:325
  12.3 5.0 %collective-permute-start.3 = (s16[1,5,32,256]{3,2,1,0:T(8,128)(2,1)S(1)}, s16[1,5,32,256]{3,2,1,0:T(8,128)(2,1)S(1)}, u32[]{:S(2)}, u32[]{:S(2)}) collective-permute-start(s16[1,5,32,256]{3,2,1,0:T(8,128)(2,1)S(1)} %relay.1), channel_id=1, source_target_pairs={{0,16},{8,24},{16,0},{24,8},{1,17},{9,25},{17,1},{25,9},{2,18},{10... | collective-permute-start | bytes 245768 | tf_op jit(solution)/shard_map/ppermute | solution.py:325
  17.5 6.8 %collective-permute-start.4 = (f32[3,256]{1,0:T(4,128)S(1)}, f32[3,256]{1,0:T(4,128)S(1)}, u32[]{:S(2)}, u32[]{:S(2)}) collective-permute-start(f32[3,256]{1,0:T(4,128)S(1)} %get-tuple-element.13), channel_id=1, source_target_pairs={{0,1},{2,3},{4,5},{6,7},{1,0},{3,2},{5,4},{7,6},{8,9},{10,11},{12,... | collective-permute-start | bytes 9224 | tf_op jit(solution)/shard_map/ppermute | solution.py:309
  21.2 5.8 %collective-permute-start.5 = (f32[3,256]{1,0:T(4,128)S(1)}, f32[3,256]{1,0:T(4,128)S(1)}, u32[]{:S(2)}, u32[]{:S(2)}) collective-permute-start(f32[3,256]{1,0:T(4,128)S(1)} %get-tuple-element.14), channel_id=1, source_target_pairs={{1,2},{3,4},{5,6},{2,1},{4,3},{6,5},{9,10},{11,12},{13,14},{10,9},... | collective-permute-start | bytes 9224 | tf_op jit(solution)/shard_map/ppermute | solution.py:308

commit v4 on v3

--- a/solution.py
+++ b/solution.py
@@ -18,10 +18,6 @@
 
 def vmem():
     return pl.BlockSpec(memory_space=pltpu.VMEM)
-
-
-def smem():
-    return pl.BlockSpec(memory_space=pltpu.SMEM)
 
 
 def encode(x):
@@ -108,13 +104,13 @@
     lax.fori_loop(0, (rows // ROWS) * across, one, 0)
 
 
-def march(field, plane, frac, counts, slab, steps, block_of, width):
-    _, depth, rows, _ = field.shape
-    slots = plane.shape[0]
+def march(field, plane, frac, counts, width):
+    _, depth, rows, columns = field.shape
+    slots, steps = plane.shape[0], columns // width
     total_depth = depth * lax.axis_size("slab")
 
-    def kernel(slab_ref, field, plane, frac, counts, run, late, last):
-        base = (slab_ref[0] * (8 * depth)).astype(jnp.float32)
+    def kernel(field, plane, frac, counts, run, late, last):
+        base = (lax.axis_index("slab") * (8 * depth)).astype(jnp.float32)
         last[0] = field[:, depth - 1]
         tiles(rows, width, lambda here, cols: march_rows(
             field, plane, frac, counts, run.at[0], late.at[0], here, cols, base, total_depth
@@ -122,23 +118,20 @@
 
     def spec(*lead):
         zeros = (0,) * len(lead)
-        return pl.BlockSpec(lead + (rows, width), lambda b, s: zeros + (0, block_of(b, s[0])))
+        return pl.BlockSpec(lead + (rows, width), lambda b: zeros + (0, b))
 
     def out(*lead):
         zeros = (0,) * len(lead)
-        return pl.BlockSpec((1,) + lead + (rows, width), lambda b, s: (b,) + zeros + (0, 0))
+        return pl.BlockSpec((1,) + lead + (rows, width), lambda b: (b,) + zeros + (0, 0))
 
     def shape(*lead, kind):
         return jax.ShapeDtypeStruct((steps,) + lead + (rows, width), kind)
 
     return pl.pallas_call(
         kernel,
-        grid_spec=pltpu.PrefetchScalarGridSpec(
-            num_scalar_prefetch=1,
-            grid=(steps,),
-            in_specs=[spec(2, depth), spec(slots), spec(slots), spec(1)],
-            out_specs=[out(5), out(slots), out(2)],
-        ),
+        grid=(steps,),
+        in_specs=[spec(2, depth), spec(slots), spec(slots), spec(1)],
+        out_specs=[out(5), out(slots), out(2)],
         out_shape=[
             shape(5, kind=jnp.float32), shape(slots, kind=jnp.bfloat16),
             shape(2, kind=jnp.bfloat16),
@@ -149,22 +142,21 @@
             transcendentals=0,
         ),
         name="march",
-    )(slab, *(pltpu.with_memory_space_constraint(x, pltpu.HBM)
-              for x in (field, plane, frac, counts)))
-
-
-def close(ahead, follow, slab, depth, first, steps, block_of, coded):
+    )(*(pltpu.with_memory_space_constraint(x, pltpu.HBM) for x in (field, plane, frac, counts)))
+
+
+def close(ahead, follow, depth, first, steps, block_of, coded):
     run, late, last = ahead
     _, slots, rows, width = late.shape
     total_depth = depth * lax.axis_size("slab")
 
-    def kernel(slab_ref, run, late, last, follow, out):
-        s = slab_ref[0]
+    def kernel(run, late, last, follow, out):
+        s = lax.axis_index("slab")
         base = (s * (8 * depth) + 8 * (depth - 1)).astype(jnp.float32)
 
         def step(i, here, cols):
-            b = first + i
-            start = block_of(b, s) * width + cols.start
+            b = block_of(first + i, s)
+            start = b * width + cols.start
             there = pl.ds(pl.multiple_of(start, LANES), LANES)
             low = [last[b, ch, here, cols].astype(jnp.float32) for ch in (0, 1)]
             high = [follow[ch, 0, here, there].astype(jnp.float32) for ch in (0, 1)]
@@ -195,7 +187,7 @@
 
     return pl.pallas_call(
         kernel,
-        in_specs=[smem()] + [vmem()] * 4,
+        in_specs=[vmem()] * 4,
         out_specs=vmem(),
         out_shape=jax.ShapeDtypeStruct((steps, 5, rows, width), WIRE if coded else jnp.float32),
         compiler_params=pltpu.CompilerParams(vmem_limit_bytes=24 << 20),
@@ -204,7 +196,7 @@
             transcendentals=0,
         ),
         name="close",
-    )(slab, run, late, last, follow)
+    )(run, late, last, follow)
 
 
 def join(mine, got, got_first):
@@ -219,11 +211,11 @@
     ]
 
 
-def relay(mine, got, slab):
+def relay(mine, got):
     _, kinds, rows, _ = mine.shape
 
-    def kernel(slab_ref, mine, got, send):
-        got_first = slab_ref[0] & 1 == 1
+    def kernel(mine, got, send):
+        got_first = lax.axis_index("slab") & 1 == 1
         for r in range(0, rows, ROWS):
             here = pl.ds(r, ROWS)
             done = join(
@@ -236,24 +228,24 @@
 
     return pl.pallas_call(
         kernel,
-        in_specs=[smem(), vmem(), vmem()],
+        in_specs=[vmem()] * 2,
         out_specs=vmem(),
         out_shape=jax.ShapeDtypeStruct(got.shape, WIRE),
         compiler_params=pltpu.CompilerParams(vmem_limit_bytes=16 << 20),
         name="relay",
-    )(slab, mine, got)
-
-
-def finish(mine, got, slab, col):
+    )(mine, got)
+
+
+def finish(mine, got):
     _, kinds, rows, width = mine.shape
     runs = [mine, *got]
 
-    def kernel(slab_ref, col_ref, mine, *refs):
+    def kernel(mine, *refs):
         *partner, image, near, far = refs
-        odd = col_ref[0] % 2 == 1
+        odd = lax.axis_index("col") % 2 == 1
         done = [mine[0, what] for what in range(kinds)]
         for bit, got in enumerate(partner):
-            got_first = (slab_ref[0] >> bit) & 1 == 1
+            got_first = (lax.axis_index("slab") >> bit) & 1 == 1
             done = join(done, [decode(got[0, what]) for what in range(kinds)], got_first)
         row = lax.broadcasted_iota(jnp.int32, (rows, width), 0)
         for at, what in enumerate((COLOR, DEEP, COARSE)):
@@ -268,34 +260,37 @@
     edge = jax.ShapeDtypeStruct((3, width), jnp.float32)
     return pl.pallas_call(
         kernel,
-        in_specs=[smem(), smem()] + [vmem()] * len(runs),
+        in_specs=[vmem()] * len(runs),
         out_specs=[vmem()] * 3,
         out_shape=[jax.ShapeDtypeStruct((3, rows, width), jnp.float32), edge, edge],
         compiler_params=pltpu.CompilerParams(vmem_limit_bytes=16 << 20),
         name="finish",
-    )(slab, col, *runs)
-
-
-def border(image, near, far, col):
+    )(*runs)
+
+
+def border(image, near, far):
     _, rows, width = image.shape
-
-    def kernel(col_ref, image, near, far, *outs):
-        odd = col_ref[0] % 2 == 1
+    count = lax.axis_size("col")
+
+    def kernel(image, near, far, *outs):
+        col = lax.axis_index("col")
+        odd = col % 2 == 1
+        outermost = (col == 0) | (col == count - 1)
         row = lax.broadcasted_iota(jnp.int32, (rows, width), 0)
         for at, out in enumerate(outs):
-            a, b = near[pl.ds(at, 1), :], far[pl.ds(at, 1), :]
+            a, b = near[pl.ds(at, 1), :], jnp.where(outermost, 0.0, far[pl.ds(at, 1), :])
             above, below = jnp.where(odd, a, b), jnp.where(odd, b, a)
             extra = jnp.where(row == 0, above, 0.0) + jnp.where(row == rows - 1, below, 0.0)
             out[...] = image[at] + extra
 
     return pl.pallas_call(
         kernel,
-        in_specs=[smem()] + [vmem()] * 3,
+        in_specs=[vmem()] * 3,
         out_specs=[vmem()] * 3,
         out_shape=[jax.ShapeDtypeStruct((rows, width), jnp.float32)] * 3,
         compiler_params=pltpu.CompilerParams(vmem_limit_bytes=16 << 20),
         name="border",
-    )(col, image, near, far)
+    )(image, near, far)
 
 
 def pairs(low, high):
@@ -305,7 +300,7 @@
 
 def neighbours(near, far):
     count = lax.axis_size("col")
-    far = lax.ppermute(far, "col", pairs(range(1, count - 1, 2), range(2, count, 2)))
+    far = lax.ppermute(far, "col", pairs(range(1, count, 2), [*range(2, count, 2), 0]))
     near = lax.ppermute(near, "col", pairs(range(0, count - 1, 2), range(1, count, 2)))
     return near, far
 
@@ -329,8 +324,6 @@
     slabs = lax.axis_size("slab")
     depth, columns = field.shape[1], field.shape[3]
     width = columns // slabs
-    slab = lax.axis_index("slab").reshape(1).astype(jnp.int32)
-    col = lax.axis_index("col").reshape(1).astype(jnp.int32)
     fast = slabs == 4 and width % LANES == 0
     block = width if fast else LANES
     blocks = columns // block
@@ -342,23 +335,23 @@
         return 2 * (((s >> 1) & 1) ^ 1 ^ (b & 1)) + parity
 
     follow = lax.ppermute(field[:, :1], "slab", [(i + 1, i) for i in range(slabs - 1)])
-    ahead = march(field, fine_plane, fine_frac, counts, slab, blocks, block_of, block)
+    ahead = march(field, fine_plane, fine_frac, counts, block)
 
     def part(first, steps, coded):
-        return close(ahead, follow, slab, depth, first, steps, block_of, coded)
+        return close(ahead, follow, depth, first, steps, block_of, coded)
 
     if not fast:
         parts = part(0, blocks, False)
-        image, near, far = finish(wide_exchange(parts, slabs, width), (), slab, col)
-        return border(image, *neighbours(near, far), col)
+        image, near, far = finish(wide_exchange(parts, slabs, width), ())
+        return border(image, *neighbours(near, far))
 
     got_a = swap(part(0, 1, True), slabs, 1)
     keep_a = part(2, 1, False)
-    got = swap(relay(keep_a, got_a, slab), slabs, 2)
+    got = swap(relay(keep_a, got_a), slabs, 2)
     got_b = swap(part(1, 1, True), slabs, 1)
     keep_b = part(3, 1, False)
-    image, near, far = finish(keep_b, (got_b, got), slab, col)
-    return border(image, *neighbours(near, far), col)
+    image, near, far = finish(keep_b, (got_b, got))
+    return border(image, *neighbours(near, far))
 
 
 def solution(mesh):

time: 27.9 us -> 26.1 us (0.935)
  the two profiles are of different devices: /device:TPU:27 before, /device:TPU:0 now
where the time goes in v4:
time: 26.1 us; the launch traced here: 25.9 us
  starting transfers between devices  9.03 us (35%)
  waiting for transfers between devices  8.16 us (31%)
  Pallas kernels  7.09 us (27%)
  local copies, waits for them, and re-layouts  0.92 us (4%)
  between operations  0.7 us (3%)
    ppermute x3, starting transfers between devices, swap(): return lax.ppermute(x, 'slab', pairs(low, [i + distance for i in low]))  4.96 us
    pallas_call x1, Pallas kernels, march(): pl.pallas_call(kernel, grid=(steps,), in_specs=[spec(2, depth), spec(slot...  4.7 us
    ppermute x3, waiting for transfers between devices, swap(): return lax.ppermute(x, 'slab', pairs(low, [i + distance for i in low]))  4.4 us
    ppermute x1, starting transfers between devices, neighbours(): lax.ppermute(far, 'col', pairs(range(1, count, 2), [*range(2, count, 2),...  2.71 us
    ppermute x1, waiting for transfers between devices, body(): lax.ppermute(field[:, :1], 'slab', [(i + 1, i) for i in range(slabs - 1)])  2.44 us
    pallas_call x4, Pallas kernels, close(): pl.pallas_call(kernel, in_specs=[vmem()] * 4, out_specs=vmem(), out_shape...  1.48 us
    ppermute x1, waiting for transfers between devices, neighbours(): lax.ppermute(far, 'col', pairs(range(1, count, 2), [*range(2, count, 2),...  1.33 us
    ppermute x1, starting transfers between devices, body(): lax.ppermute(field[:, :1], 'slab', [(i + 1, i) for i in range(slabs - 1)])  1.29 us
  transfers between devices with their start and end apart: 6, of which 4 were waited for; matrix products, arithmetic and copies ran while one was open for 0% of the time, Pallas kernels for 23%

profile of v4, /device:TPU:0, one launch (start us, length us, event | category | flops | bytes accessed | tf_op | source)
XLA Modules:
  0.0 25.9 jit_solution(15904089227294918287)
XLA Ops:
  0.6 0.9 %slice.3 = bf16[2,1,32,1024]{3,2,1,0:T(8,128)(2,1)S(1)} slice(bf16[2,16,32,1024]{3,2,1,0:T(8,128)(2,1)} %field.1), slice={[0:2], [0:1], [0:32], [0:1024]} | slice | bytes 262144 | tf_op jit(solution)/shard_map/slice | solution.py:337
  1.6 1.3 %collective-permute-start = (bf16[2,1,32,1024]{3,2,1,0:T(8,128)(2,1)S(1)}, bf16[2,1,32,1024]{3,2,1,0:T(8,128)(2,1)S(1)}, u32[]{:S(2)}, u32[]{:S(2)}) collective-permute-start(bf16[2,1,32,1024]{3,2,1,0:T(8,128)(2,1)S(1)} %slice.3), channel_id=1, source_target_pairs={{8,0},{16,8},{24,16},{9,1},{17,9},{25,17},{10,2},{18,10},{26,18},{... | collective-permute-start | bytes 393224 | tf_op jit(solution)/shard_map/ppermute | solution.py:337
  2.9 4.7 %march.1 = (f32[4,5,32,256]{3,2,1,0:T(8,128)S(1)}, bf16[4,8,32,256]{3,2,1,0:T(8,128)(2,1)S(1)}, bf16[4,2,32,256]{3,2,1,0:T(8,128)(2,1)S(1)}) custom-call(bf16[2,16,32,1024]{3,2,1,0:T(8,128)(2,1)} %field.1, s32[8,32,1024]{2,1,0:T(8,128)} %plane.1, s32[8,32,1024]{2,1,0:T(8,128)} %frac.1, s32[1,32,1024]{2,1,0:T(8,128)} %counts.1), custom_call_target="tpu_custom_call" | custom-call | flops 98304000 | bytes 4194304 | tf_op jit(solution)/shard_map/march/pallas_call | solution.py:130
  7.6 2.4 %collective-permute-done.follow = bf16[2,1,32,1024]{3,2,1,0:T(8,128)(2,1)S(1)} collective-permute-done((bf16[2,1,32,1024]{3,2,1,0:T(8,128)(2,1)S(1)}, bf16[2,1,32,1024]{3,2,1,0:T(8,128)(2,1)S(1)}, u32[]{:S(2)}, u32[]{:S(2)}) %collective-permute-start) | collective-permute-done | bytes 131104 | tf_op jit(solution)/shard_map/ppermute | solution.py:337
  10.0 0.4 %close.7 = s16[1,5,32,256]{3,2,1,0:T(8,128)(2,1)S(1)} custom-call(f32[4,5,32,256]{3,2,1,0:T(8,128)S(1)} %get-tuple-element.9.run, bf16[4,8,32,256]{3,2,1,0:T(8,128)(2,1)S(1)} %get-tuple-element.10.late, bf16[4,2,32,256]{3,2,1,0:T(8,128)(2,1)S(1)} %get-tuple-element.11.last, bf16[2,1,32,1024]{3,2,1,0:T(8,128)(2,1)S(1)} %collective-permute-done.follow), custom_call_target="tpu_custom_call" | custom-call | flops 12288000 | bytes 524288 | tf_op jit(solution)/shard_map/close/pallas_call | solution.py:188
  10.4 1.8 %collective-permute-start.2 = (s16[1,5,32,256]{3,2,1,0:T(8,128)(2,1)S(1)}, s16[1,5,32,256]{3,2,1,0:T(8,128)(2,1)S(1)}, u32[]{:S(2)}, u32[]{:S(2)}) collective-permute-start(s16[1,5,32,256]{3,2,1,0:T(8,128)(2,1)S(1)} %close.7), channel_id=1, source_target_pairs={{0,8},{16,24},{8,0},{24,16},{1,9},{17,25},{9,1},{25,17},{2,10},{18... | collective-permute-start | bytes 245768 | tf_op jit(solution)/shard_map/ppermute | solution.py:320
  12.2 0.4 %close.5 = s16[1,5,32,256]{3,2,1,0:T(8,128)(2,1)S(1)} custom-call(f32[4,5,32,256]{3,2,1,0:T(8,128)S(1)} %get-tuple-element.9.run, bf16[4,8,32,256]{3,2,1,0:T(8,128)(2,1)S(1)} %get-tuple-element.10.late, bf16[4,2,32,256]{3,2,1,0:T(8,128)(2,1)S(1)} %get-tuple-element.11.last, bf16[2,1,32,1024]{3,2,1,0:T(8,128)(2,1)S(1)} %collective-permute-done.follow), custom_call_target="tpu_custom_call" | custom-call | flops 12288000 | bytes 524288 | tf_op jit(solution)/shard_map/close/pallas_call | solution.py:188
  12.6 0.4 %collective-permute-start.1 = (s16[1,5,32,256]{3,2,1,0:T(8,128)(2,1)S(1)}, s16[1,5,32,256]{3,2,1,0:T(8,128)(2,1)S(1)}, u32[]{:S(2)}, u32[]{:S(2)}) collective-permute-start(s16[1,5,32,256]{3,2,1,0:T(8,128)(2,1)S(1)} %close.5), channel_id=1, source_target_pairs={{0,8},{16,24},{8,0},{24,16},{1,9},{17,25},{9,1},{25,17},{2,10},{18... | collective-permute-start | bytes 245768 | tf_op jit(solution)/shard_map/ppermute | solution.py:320
  13.0 0.3 %close.6.mine = f32[1,5,32,256]{3,2,1,0:T(8,128)S(1)} custom-call(f32[4,5,32,256]{3,2,1,0:T(8,128)S(1)} %get-tuple-element.9.run, bf16[4,8,32,256]{3,2,1,0:T(8,128)(2,1)S(1)} %get-tuple-element.10.late, bf16[4,2,32,256]{3,2,1,0:T(8,128)(2,1)S(1)} %get-tuple-element.11.last, bf16[2,1,32,1024]{3,2,1,0:T(8,128)(2,1)S(1)} %collective-permute-done.follow), custom_call_target="tpu_custom_call" | custom-call | flops 12288000 | bytes 524288 | tf_op jit(solution)/shard_map/close/pallas_call | solution.py:188
  13.3 2.1 %collective-permute-done.2.got = s16[1,5,32,256]{3,2,1,0:T(8,128)(2,1)S(1)} collective-permute-done((s16[1,5,32,256]{3,2,1,0:T(8,128)(2,1)S(1)}, s16[1,5,32,256]{3,2,1,0:T(8,128)(2,1)S(1)}, u32[]{:S(2)}, u32[]{:S(2)}) %collective-permute-start.2) | collective-permute-done | bytes 81952 | tf_op jit(solution)/shard_map/ppermute | solution.py:320
  15.5 0.1 relay.1
  15.6 2.8 %collective-permute-start.3 = (s16[1,5,32,256]{3,2,1,0:T(8,128)(2,1)S(1)}, s16[1,5,32,256]{3,2,1,0:T(8,128)(2,1)S(1)}, u32[]{:S(2)}, u32[]{:S(2)}) collective-permute-start(s16[1,5,32,256]{3,2,1,0:T(8,128)(2,1)S(1)} %relay.1), channel_id=1, source_target_pairs={{0,16},{8,24},{16,0},{24,8},{1,17},{9,25},{17,1},{25,9},{2,18},{10... | collective-permute-start | bytes 245768 | tf_op jit(solution)/shard_map/ppermute | solution.py:320
  18.4 0.3 %close.4.mine = f32[1,5,32,256]{3,2,1,0:T(8,128)S(1)} custom-call(f32[4,5,32,256]{3,2,1,0:T(8,128)S(1)} %get-tuple-element.9.run, bf16[4,8,32,256]{3,2,1,0:T(8,128)(2,1)S(1)} %get-tuple-element.10.late, bf16[4,2,32,256]{3,2,1,0:T(8,128)(2,1)S(1)} %get-tuple-element.11.last, bf16[2,1,32,1024]{3,2,1,0:T(8,128)(2,1)S(1)} %collective-permute-done.follow), custom_call_target="tpu_custom_call" | custom-call | flops 12288000 | bytes 524288 | tf_op jit(solution)/shard_map/close/pallas_call | solution.py:188
  18.7 0.0 collective-permute-done.1.refs_0_
  18.7 2.3 %collective-permute-done.3.refs_1_ = s16[1,5,32,256]{3,2,1,0:T(8,128)(2,1)S(1)} collective-permute-done((s16[1,5,32,256]{3,2,1,0:T(8,128)(2,1)S(1)}, s16[1,5,32,256]{3,2,1,0:T(8,128)(2,1)S(1)}, u32[]{:S(2)}, u32[]{:S(2)}) %collective-permute-start.3) | collective-permute-done | bytes 81952 | tf_op jit(solution)/shard_map/ppermute | solution.py:320
  21.0 0.2 finish.1
  21.1 0.1 collective-permute-start.4
  21.2 2.7 %collective-permute-start.5 = (f32[3,256]{1,0:T(4,128)S(1)}, f32[3,256]{1,0:T(4,128)S(1)}, u32[]{:S(2)}, u32[]{:S(2)}) collective-permute-start(f32[3,256]{1,0:T(4,128)S(1)} %get-tuple-element.14), channel_id=1, source_target_pairs={{1,2},{3,4},{5,6},{7,0},{2,1},{4,3},{6,5},{0,7},{9,10},{11,12},{13... | collective-permute-start | bytes 9224 | tf_op jit(solution)/shard_map/ppermute | solution.py:303
  23.9 0.0 collective-permute-done.4.near
  23.9 1.3 %collective-permute-done.5.far = f32[3,256]{1,0:T(4,128)S(1)} collective-permute-done((f32[3,256]{1,0:T(4,128)S(1)}, f32[3,256]{1,0:T(4,128)S(1)}, u32[]{:S(2)}, u32[]{:S(2)}) %collective-permute-start.5) | collective-permute-done | bytes 3104 | tf_op jit(solution)/shard_map/ppermute | solution.py:303
  25.3 0.7 %border.1 = (f32[32,256]{1,0:T(8,128)}, f32[32,256]{1,0:T(8,128)}, f32[32,256]{1,0:T(8,128)}) custom-call(f32[3,32,256]{2,1,0:T(8,128)S(1)} %get-tuple-element.12.image, f32[3,256]{1,0:T(4,128)S(1)} %collective-permute-done.4.near, f32[3,256]{1,0:T(4,128)S(1)} %collective-permute-done.5.far), custom_call_target="tpu_custom_call" | custom-call | tf_op jit(solution)/shard_map/border/pallas_call | solution.py:286
Async XLA Ops:
  1.6 8.4 %collective-permute-start = (bf16[2,1,32,1024]{3,2,1,0:T(8,128)(2,1)S(1)}, bf16[2,1,32,1024]{3,2,1,0:T(8,128)(2,1)S(1)}, u32[]{:S(2)}, u32[]{:S(2)}) collective-permute-start(bf16[2,1,32,1024]{3,2,1,0:T(8,128)(2,1)S(1)} %slice.3), channel_id=1, source_target_pairs={{8,0},{16,8},{24,16},{9,1},{17,9},{25,17},{10,2},{18,10},{26,18},{... | collective-permute-start | bytes 393224 | tf_op jit(solution)/shard_map/ppermute | solution.py:337
  10.4 5.0 %collective-permute-start.2 = (s16[1,5,32,256]{3,2,1,0:T(8,128)(2,1)S(1)}, s16[1,5,32,256]{3,2,1,0:T(8,128)(2,1)S(1)}, u32[]{:S(2)}, u32[]{:S(2)}) collective-permute-start(s16[1,5,32,256]{3,2,1,0:T(8,128)(2,1)S(1)} %close.7), channel_id=1, source_target_pairs={{0,8},{16,24},{8,0},{24,16},{1,9},{17,25},{9,1},{25,17},{2,10},{18... | collective-permute-start | bytes 245768 | tf_op jit(solution)/shard_map/ppermute | solution.py:320
  12.6 6.1 %collective-permute-start.1 = (s16[1,5,32,256]{3,2,1,0:T(8,128)(2,1)S(1)}, s16[1,5,32,256]{3,2,1,0:T(8,128)(2,1)S(1)}, u32[]{:S(2)}, u32[]{:S(2)}) collective-permute-start(s16[1,5,32,256]{3,2,1,0:T(8,128)(2,1)S(1)} %close.5), channel_id=1, source_target_pairs={{0,8},{16,24},{8,0},{24,16},{1,9},{17,25},{9,1},{25,17},{2,10},{18... | collective-permute-start | bytes 245768 | tf_op jit(solution)/shard_map/ppermute | solution.py:320
  15.6 5.4 %collective-permute-start.3 = (s16[1,5,32,256]{3,2,1,0:T(8,128)(2,1)S(1)}, s16[1,5,32,256]{3,2,1,0:T(8,128)(2,1)S(1)}, u32[]{:S(2)}, u32[]{:S(2)}) collective-permute-start(s16[1,5,32,256]{3,2,1,0:T(8,128)(2,1)S(1)} %relay.1), channel_id=1, source_target_pairs={{0,16},{8,24},{16,0},{24,8},{1,17},{9,25},{17,1},{25,9},{2,18},{10... | collective-permute-start | bytes 245768 | tf_op jit(solution)/shard_map/ppermute | solution.py:320
  21.1 2.8 %collective-permute-start.4 = (f32[3,256]{1,0:T(4,128)S(1)}, f32[3,256]{1,0:T(4,128)S(1)}, u32[]{:S(2)}, u32[]{:S(2)}) collective-permute-start(f32[3,256]{1,0:T(4,128)S(1)} %get-tuple-element.13), channel_id=1, source_target_pairs={{0,1},{2,3},{4,5},{6,7},{1,0},{3,2},{5,4},{7,6},{8,9},{10,11},{12,... | collective-permute-start | bytes 9224 | tf_op jit(solution)/shard_map/ppermute | solution.py:304
  21.2 4.0 %collective-permute-start.5 = (f32[3,256]{1,0:T(4,128)S(1)}, f32[3,256]{1,0:T(4,128)S(1)}, u32[]{:S(2)}, u32[]{:S(2)}) collective-permute-start(f32[3,256]{1,0:T(4,128)S(1)} %get-tuple-element.14), channel_id=1, source_target_pairs={{1,2},{3,4},{5,6},{7,0},{2,1},{4,3},{6,5},{0,7},{9,10},{11,12},{13... | collective-permute-start | bytes 9224 | tf_op jit(solution)/shard_map/ppermute | solution.py:303

commit v5 on v4

--- a/solution.py
+++ b/solution.py
@@ -299,8 +299,13 @@
 
 
 def neighbours(near, far):
-    count = lax.axis_size("col")
-    far = lax.ppermute(far, "col", pairs(range(1, count, 2), [*range(2, count, 2), 0]))
+    slabs, count = lax.axis_size("slab"), lax.axis_size("col")
+    far = lax.ppermute(far, ("slab", "col"), [
+        (s * count + a, t * count + b)
+        for s in range(slabs)
+        for a, b in pairs(range(1, count - 1, 2), range(2, count, 2)) + [(0, 0), (count - 1,) * 2]
+        for t in [s ^ 1 if a == b else s]
+    ])
     near = lax.ppermute(near, "col", pairs(range(0, count - 1, 2), range(1, count, 2)))
     return near, far
 

time: 26.1 us -> 26 us (level)
  the two profiles are of different devices: /device:TPU:0 before, /device:TPU:27 now
where the time goes in v5:
time: 26 us; the launch traced here: 25.8 us
  starting transfers between devices  8.75 us (34%)
  waiting for transfers between devices  8.32 us (32%)
  Pallas kernels  7.12 us (27%)
  local copies, waits for them, and re-layouts  0.92 us (4%)
  between operations  0.7 us (3%)
    ppermute x3, waiting for transfers between devices, swap(): return lax.ppermute(x, 'slab', pairs(low, [i + distance for i in low]))  5.57 us
    pallas_call x1, Pallas kernels, march(): pl.pallas_call(kernel, grid=(steps,), in_specs=[spec(2, depth), spec(slot...  4.7 us
    ppermute x1, starting transfers between devices, neighbours(): lax.ppermute(near, 'col', pairs(range(0, count - 1, 2), range(1, count, 2)))  3.78 us
    ppermute x1, waiting for transfers between devices, neighbours(): lax.ppermute(far, ('slab', 'col'), [(s * count + a, t * count + b) for s...  2.75 us
    ppermute x1, starting transfers between devices, body(): lax.ppermute(field[:, :1], 'slab', [(i + 1, i) for i in range(slabs - 1)])  2.08 us
    ppermute x3, starting transfers between devices, swap(): return lax.ppermute(x, 'slab', pairs(low, [i + distance for i in low]))  1.71 us
    pallas_call x4, Pallas kernels, close(): pl.pallas_call(kernel, in_specs=[vmem()] * 4, out_specs=vmem(), out_shape...  1.5 us
    ppermute x1, starting transfers between devices, neighbours(): lax.ppermute(far, ('slab', 'col'), [(s * count + a, t * count + b) for s...  1.17 us
  transfers between devices with their start and end apart: 6, of which 4 were waited for; matrix products, arithmetic and copies ran while one was open for 0% of the time, Pallas kernels for 23%

profile of v5, /device:TPU:27, one launch (start us, length us, event | category | flops | bytes accessed | tf_op | source)
XLA Modules:
  0.0 25.8 jit_solution(2493386112026411800)
XLA Ops:
  0.6 0.9 %slice.3 = bf16[2,1,32,1024]{3,2,1,0:T(8,128)(2,1)S(1)} slice(bf16[2,16,32,1024]{3,2,1,0:T(8,128)(2,1)} %field.1), slice={[0:2], [0:1], [0:32], [0:1024]} | slice | bytes 262144 | tf_op jit(solution)/shard_map/slice | solution.py:342
  1.6 2.1 %collective-permute-start = (bf16[2,1,32,1024]{3,2,1,0:T(8,128)(2,1)S(1)}, bf16[2,1,32,1024]{3,2,1,0:T(8,128)(2,1)S(1)}, u32[]{:S(2)}, u32[]{:S(2)}) collective-permute-start(bf16[2,1,32,1024]{3,2,1,0:T(8,128)(2,1)S(1)} %slice.3), channel_id=1, source_target_pairs={{8,0},{16,8},{24,16},{9,1},{17,9},{25,17},{10,2},{18,10},{26,18},{... | collective-permute-start | bytes 393224 | tf_op jit(solution)/shard_map/ppermute | solution.py:342
  3.6 4.7 %march.1 = (f32[4,5,32,256]{3,2,1,0:T(8,128)S(1)}, bf16[4,8,32,256]{3,2,1,0:T(8,128)(2,1)S(1)}, bf16[4,2,32,256]{3,2,1,0:T(8,128)(2,1)S(1)}) custom-call(bf16[2,16,32,1024]{3,2,1,0:T(8,128)(2,1)} %field.1, s32[8,32,1024]{2,1,0:T(8,128)} %plane.1, s32[8,32,1024]{2,1,0:T(8,128)} %frac.1, s32[1,32,1024]{2,1,0:T(8,128)} %counts.1), custom_call_target="tpu_custom_call" | custom-call | flops 98304000 | bytes 4194304 | tf_op jit(solution)/shard_map/march/pallas_call | solution.py:130
  8.3 0.0 collective-permute-done.follow
  8.4 0.4 %close.7 = s16[1,5,32,256]{3,2,1,0:T(8,128)(2,1)S(1)} custom-call(f32[4,5,32,256]{3,2,1,0:T(8,128)S(1)} %get-tuple-element.9.run, bf16[4,8,32,256]{3,2,1,0:T(8,128)(2,1)S(1)} %get-tuple-element.10.late, bf16[4,2,32,256]{3,2,1,0:T(8,128)(2,1)S(1)} %get-tuple-element.11.last, bf16[2,1,32,1024]{3,2,1,0:T(8,128)(2,1)S(1)} %collective-permute-done.follow), custom_call_target="tpu_custom_call" | custom-call | flops 12288000 | bytes 524288 | tf_op jit(solution)/shard_map/close/pallas_call | solution.py:188
  8.8 0.2 collective-permute-start.2
  9.0 0.4 %close.5 = s16[1,5,32,256]{3,2,1,0:T(8,128)(2,1)S(1)} custom-call(f32[4,5,32,256]{3,2,1,0:T(8,128)S(1)} %get-tuple-element.9.run, bf16[4,8,32,256]{3,2,1,0:T(8,128)(2,1)S(1)} %get-tuple-element.10.late, bf16[4,2,32,256]{3,2,1,0:T(8,128)(2,1)S(1)} %get-tuple-element.11.last, bf16[2,1,32,1024]{3,2,1,0:T(8,128)(2,1)S(1)} %collective-permute-done.follow), custom_call_target="tpu_custom_call" | custom-call | flops 12288000 | bytes 524288 | tf_op jit(solution)/shard_map/close/pallas_call | solution.py:188
  9.4 1.4 %collective-permute-start.1 = (s16[1,5,32,256]{3,2,1,0:T(8,128)(2,1)S(1)}, s16[1,5,32,256]{3,2,1,0:T(8,128)(2,1)S(1)}, u32[]{:S(2)}, u32[]{:S(2)}) collective-permute-start(s16[1,5,32,256]{3,2,1,0:T(8,128)(2,1)S(1)} %close.5), channel_id=1, source_target_pairs={{0,8},{16,24},{8,0},{24,16},{1,9},{17,25},{9,1},{25,17},{2,10},{18... | collective-permute-start | bytes 245768 | tf_op jit(solution)/shard_map/ppermute | solution.py:325
  10.8 0.3 %close.6.mine = f32[1,5,32,256]{3,2,1,0:T(8,128)S(1)} custom-call(f32[4,5,32,256]{3,2,1,0:T(8,128)S(1)} %get-tuple-element.9.run, bf16[4,8,32,256]{3,2,1,0:T(8,128)(2,1)S(1)} %get-tuple-element.10.late, bf16[4,2,32,256]{3,2,1,0:T(8,128)(2,1)S(1)} %get-tuple-element.11.last, bf16[2,1,32,1024]{3,2,1,0:T(8,128)(2,1)S(1)} %collective-permute-done.follow), custom_call_target="tpu_custom_call" | custom-call | flops 12288000 | bytes 524288 | tf_op jit(solution)/shard_map/close/pallas_call | solution.py:188
  11.1 1.0 %collective-permute-done.2.got = s16[1,5,32,256]{3,2,1,0:T(8,128)(2,1)S(1)} collective-permute-done((s16[1,5,32,256]{3,2,1,0:T(8,128)(2,1)S(1)}, s16[1,5,32,256]{3,2,1,0:T(8,128)(2,1)S(1)}, u32[]{:S(2)}, u32[]{:S(2)}) %collective-permute-start.2) | collective-permute-done | bytes 81952 | tf_op jit(solution)/shard_map/ppermute | solution.py:325
  12.2 0.1 relay.1
  12.3 0.1 collective-permute-start.3
  12.4 0.3 %close.4.mine = f32[1,5,32,256]{3,2,1,0:T(8,128)S(1)} custom-call(f32[4,5,32,256]{3,2,1,0:T(8,128)S(1)} %get-tuple-element.9.run, bf16[4,8,32,256]{3,2,1,0:T(8,128)(2,1)S(1)} %get-tuple-element.10.late, bf16[4,2,32,256]{3,2,1,0:T(8,128)(2,1)S(1)} %get-tuple-element.11.last, bf16[2,1,32,1024]{3,2,1,0:T(8,128)(2,1)S(1)} %collective-permute-done.follow), custom_call_target="tpu_custom_call" | custom-call | flops 12288000 | bytes 524288 | tf_op jit(solution)/shard_map/close/pallas_call | solution.py:188
  12.7 0.9 %collective-permute-done.1.refs_0_ = s16[1,5,32,256]{3,2,1,0:T(8,128)(2,1)S(1)} collective-permute-done((s16[1,5,32,256]{3,2,1,0:T(8,128)(2,1)S(1)}, s16[1,5,32,256]{3,2,1,0:T(8,128)(2,1)S(1)}, u32[]{:S(2)}, u32[]{:S(2)}) %collective-permute-start.1) | collective-permute-done | bytes 81952 | tf_op jit(solution)/shard_map/ppermute | solution.py:325
  13.7 3.6 %collective-permute-done.3.refs_1_ = s16[1,5,32,256]{3,2,1,0:T(8,128)(2,1)S(1)} collective-permute-done((s16[1,5,32,256]{3,2,1,0:T(8,128)(2,1)S(1)}, s16[1,5,32,256]{3,2,1,0:T(8,128)(2,1)S(1)}, u32[]{:S(2)}, u32[]{:S(2)}) %collective-permute-start.3) | collective-permute-done | bytes 81952 | tf_op jit(solution)/shard_map/ppermute | solution.py:325
  17.3 0.2 finish.1
  17.4 3.8 %collective-permute-start.4 = (f32[3,256]{1,0:T(4,128)S(1)}, f32[3,256]{1,0:T(4,128)S(1)}, u32[]{:S(2)}, u32[]{:S(2)}) collective-permute-start(f32[3,256]{1,0:T(4,128)S(1)} %get-tuple-element.13), channel_id=1, source_target_pairs={{0,1},{2,3},{4,5},{6,7},{1,0},{3,2},{5,4},{7,6},{8,9},{10,11},{12,... | collective-permute-start | bytes 9224 | tf_op jit(solution)/shard_map/ppermute | solution.py:309
  21.2 1.2 %collective-permute-start.5 = (f32[3,256]{1,0:T(4,128)S(1)}, f32[3,256]{1,0:T(4,128)S(1)}, u32[]{:S(2)}, u32[]{:S(2)}) collective-permute-start(f32[3,256]{1,0:T(4,128)S(1)} %get-tuple-element.14), channel_id=1, source_target_pairs={{1,2},{3,4},{5,6},{2,1},{4,3},{6,5},{0,8},{7,15},{9,10},{11,12},{1... | collective-permute-start | bytes 9224 | tf_op jit(solution)/shard_map/ppermute | solution.py:303
  22.4 0.0 collective-permute-done.4.near
  22.4 2.8 %collective-permute-done.5.far = f32[3,256]{1,0:T(4,128)S(1)} collective-permute-done((f32[3,256]{1,0:T(4,128)S(1)}, f32[3,256]{1,0:T(4,128)S(1)}, u32[]{:S(2)}, u32[]{:S(2)}) %collective-permute-start.5) | collective-permute-done | bytes 3104 | tf_op jit(solution)/shard_map/ppermute | solution.py:303
  25.1 0.7 %border.1 = (f32[32,256]{1,0:T(8,128)}, f32[32,256]{1,0:T(8,128)}, f32[32,256]{1,0:T(8,128)}) custom-call(f32[3,32,256]{2,1,0:T(8,128)S(1)} %get-tuple-element.12.image, f32[3,256]{1,0:T(4,128)S(1)} %collective-permute-done.4.near, f32[3,256]{1,0:T(4,128)S(1)} %collective-permute-done.5.far), custom_call_target="tpu_custom_call" | custom-call | tf_op jit(solution)/shard_map/border/pallas_call | solution.py:286
Async XLA Ops:
  1.6 6.8 %collective-permute-start = (bf16[2,1,32,1024]{3,2,1,0:T(8,128)(2,1)S(1)}, bf16[2,1,32,1024]{3,2,1,0:T(8,128)(2,1)S(1)}, u32[]{:S(2)}, u32[]{:S(2)}) collective-permute-start(bf16[2,1,32,1024]{3,2,1,0:T(8,128)(2,1)S(1)} %slice.3), channel_id=1, source_target_pairs={{8,0},{16,8},{24,16},{9,1},{17,9},{25,17},{10,2},{18,10},{26,18},{... | collective-permute-start | bytes 393224 | tf_op jit(solution)/shard_map/ppermute | solution.py:342
  8.8 3.4 %collective-permute-start.2 = (s16[1,5,32,256]{3,2,1,0:T(8,128)(2,1)S(1)}, s16[1,5,32,256]{3,2,1,0:T(8,128)(2,1)S(1)}, u32[]{:S(2)}, u32[]{:S(2)}) collective-permute-start(s16[1,5,32,256]{3,2,1,0:T(8,128)(2,1)S(1)} %close.7), channel_id=1, source_target_pairs={{0,8},{16,24},{8,0},{24,16},{1,9},{17,25},{9,1},{25,17},{2,10},{18... | collective-permute-start | bytes 245768 | tf_op jit(solution)/shard_map/ppermute | solution.py:325
  9.4 4.2 %collective-permute-start.1 = (s16[1,5,32,256]{3,2,1,0:T(8,128)(2,1)S(1)}, s16[1,5,32,256]{3,2,1,0:T(8,128)(2,1)S(1)}, u32[]{:S(2)}, u32[]{:S(2)}) collective-permute-start(s16[1,5,32,256]{3,2,1,0:T(8,128)(2,1)S(1)} %close.5), channel_id=1, source_target_pairs={{0,8},{16,24},{8,0},{24,16},{1,9},{17,25},{9,1},{25,17},{2,10},{18... | collective-permute-start | bytes 245768 | tf_op jit(solution)/shard_map/ppermute | solution.py:325
  12.3 5.0 %collective-permute-start.3 = (s16[1,5,32,256]{3,2,1,0:T(8,128)(2,1)S(1)}, s16[1,5,32,256]{3,2,1,0:T(8,128)(2,1)S(1)}, u32[]{:S(2)}, u32[]{:S(2)}) collective-permute-start(s16[1,5,32,256]{3,2,1,0:T(8,128)(2,1)S(1)} %relay.1), channel_id=1, source_target_pairs={{0,16},{8,24},{16,0},{24,8},{1,17},{9,25},{17,1},{25,9},{2,18},{10... | collective-permute-start | bytes 245768 | tf_op jit(solution)/shard_map/ppermute | solution.py:325
  17.4 5.0 %collective-permute-start.4 = (f32[3,256]{1,0:T(4,128)S(1)}, f32[3,256]{1,0:T(4,128)S(1)}, u32[]{:S(2)}, u32[]{:S(2)}) collective-permute-start(f32[3,256]{1,0:T(4,128)S(1)} %get-tuple-element.13), channel_id=1, source_target_pairs={{0,1},{2,3},{4,5},{6,7},{1,0},{3,2},{5,4},{7,6},{8,9},{10,11},{12,... | collective-permute-start | bytes 9224 | tf_op jit(solution)/shard_map/ppermute | solution.py:309
  21.2 3.9 %collective-permute-start.5 = (f32[3,256]{1,0:T(4,128)S(1)}, f32[3,256]{1,0:T(4,128)S(1)}, u32[]{:S(2)}, u32[]{:S(2)}) collective-permute-start(f32[3,256]{1,0:T(4,128)S(1)} %get-tuple-element.14), channel_id=1, source_target_pairs={{1,2},{3,4},{5,6},{2,1},{4,3},{6,5},{0,8},{7,15},{9,10},{11,12},{1... | collective-permute-start | bytes 9224 | tf_op jit(solution)/shard_map/ppermute | solution.py:303

commit v6 on v5

--- a/solution.py
+++ b/solution.py
@@ -11,8 +11,7 @@
 ROWS = 16
 LANES = 128
 COLOR, DEEP, FINE, COARSE, COARSE_PASS = range(5)
-OCTAVES = 24.0
-STEPS = 65534.0 / OCTAVES
+OCTAVES = (22.0, 22.0, 10.0, 22.0, 10.0)
 WIRE = jnp.int16
 
 
@@ -20,24 +19,23 @@
     return pl.BlockSpec(memory_space=pltpu.VMEM)
 
 
-def encode(x):
-    if WIRE == jnp.float32:
-        return x
-    y = jnp.maximum(jnp.log2(x) * STEPS + 65535.5, 0.0)
-    return (y.astype(jnp.int32) - 32768).astype(jnp.int16)
-
-
-def decode(code):
-    if WIRE == jnp.float32:
-        return code
+def encode(x, what):
+    y = jnp.maximum(jnp.log2(x) * (65534.0 / OCTAVES[what]) + 65535.5, 0.0)
+    return (y.astype(jnp.int32) - 32768).astype(WIRE)
+
+
+def decode(code, what):
     y = code.astype(jnp.int32).astype(jnp.float32)
-    x = jnp.exp2((y - 32767.0) * (1.0 / STEPS))
+    x = jnp.exp2((y - 32767.0) * (OCTAVES[what] / 65534.0))
     return jnp.where(y > -32767.5, x, 0.0)
 
 
+SCALES = (LOG2E, 0.5)
+
+
 def shade(raw0, raw1, power):
-    soft = jnp.log2(1.0 + jnp.exp2(raw0 * LOG2E))
-    return jnp.exp2(soft * power), 1.0 + jnp.tanh(0.5 * raw1)
+    soft = jnp.log2(1.0 + jnp.exp2(raw0))
+    return jnp.exp2(soft * power), 1.0 + jnp.tanh(raw1)
 
 
 def march_rows(field, plane, frac, counts, run, late, here, cols, base, total_depth):
@@ -65,7 +63,7 @@
         values = []
         for ch in (0, 1):
             e, o = even[ch].astype(jnp.float32), odd[ch].astype(jnp.float32)
-            values.append(e + to_odd * (o - e))
+            values.append((e + to_odd * (o - e)) * SCALES[ch])
         factor, emission = shade(*values, -(depth / slots) * (2.0 / total_depth))
         rest = jnp.where(live > i, place - 8.0 * (depth - 1), -1.0)
         early = (live > i) & (place < 8.0 * (depth - 1))
@@ -82,7 +80,7 @@
     passed = jnp.ones(size, jnp.float32)
     for z in range(7, depth - 1, 8):
         values = [
-            0.5 * (field[ch, z, here, cols].astype(jnp.float32)
+            (0.5 * SCALES[ch]) * (field[ch, z, here, cols].astype(jnp.float32)
                    + field[ch, z + 1, here, cols].astype(jnp.float32))
             for ch in (0, 1)
         ]
@@ -158,8 +156,8 @@
             b = block_of(first + i, s)
             start = b * width + cols.start
             there = pl.ds(pl.multiple_of(start, LANES), LANES)
-            low = [last[b, ch, here, cols].astype(jnp.float32) for ch in (0, 1)]
-            high = [follow[ch, 0, here, there].astype(jnp.float32) for ch in (0, 1)]
+            low = [last[b, ch, here, cols].astype(jnp.float32) * SCALES[ch] for ch in (0, 1)]
+            high = [follow[ch, 0, here, there].astype(jnp.float32) * SCALES[ch] for ch in (0, 1)]
             slope = [(h - l) * 0.125 for h, l in zip(high, low)]
             color, deep, passed = (run[b, what, here, cols] for what in (COLOR, DEEP, FINE))
             for k in range(slots):
@@ -180,7 +178,7 @@
                 COARSE: 0.5 * coarse, COARSE_PASS: through * factor,
             }
             for what, value in done.items():
-                out[i, what, here, cols] = encode(value) if coded else value
+                out[i, what, here, cols] = encode(value, what) if coded else value
 
         for i in range(steps):
             tiles(rows, width, functools.partial(step, i))
@@ -220,11 +218,11 @@
             here = pl.ds(r, ROWS)
             done = join(
                 [mine[0, what, here, :] for what in range(kinds)],
-                [decode(got[0, what, here, :]) for what in range(kinds)],
+                [decode(got[0, what, here, :], what) for what in range(kinds)],
                 got_first,
             )
             for what in range(kinds):
-                send[0, what, here, :] = encode(done[what])
+                send[0, what, here, :] = encode(done[what], what)
 
     return pl.pallas_call(
         kernel,
@@ -246,7 +244,7 @@
         done = [mine[0, what] for what in range(kinds)]
         for bit, got in enumerate(partner):
             got_first = (lax.axis_index("slab") >> bit) & 1 == 1
-            done = join(done, [decode(got[0, what]) for what in range(kinds)], got_first)
+            done = join(done, [decode(got[0, what], what) for what in range(kinds)], got_first)
         row = lax.broadcasted_iota(jnp.int32, (rows, width), 0)
         for at, what in enumerate((COLOR, DEEP, COARSE)):
             x = done[what]

time: 26 us -> 26.6 us (1.023)
  the two profiles are of different devices: /device:TPU:27 before, /device:TPU:0 now
where the time goes in v6:
time: 26.6 us; the launch traced here: 26.4 us
  waiting for transfers between devices  10.8 us (41%)
  starting transfers between devices  7.08 us (27%)
  Pallas kernels  6.95 us (26%)
  local copies, waits for them, and re-layouts  0.92 us (3%)
  between operations  0.71 us (3%)
    ppermute x3, waiting for transfers between devices, swap(): return lax.ppermute(x, 'slab', pairs(low, [i + distance for i in low]))  5.39 us
    ppermute x3, starting transfers between devices, swap(): return lax.ppermute(x, 'slab', pairs(low, [i + distance for i in low]))  4.97 us
    pallas_call x1, Pallas kernels, march(): pl.pallas_call(kernel, grid=(steps,), in_specs=[spec(2, depth), spec(slot...  4.69 us
    ppermute x1, waiting for transfers between devices, neighbours(): lax.ppermute(far, ('slab', 'col'), [(s * count + a, t * count + b) for s...  2.52 us
    ppermute x1, waiting for transfers between devices, body(): lax.ppermute(field[:, :1], 'slab', [(i + 1, i) for i in range(slabs - 1)])  2.45 us
    pallas_call x4, Pallas kernels, close(): pl.pallas_call(kernel, in_specs=[vmem()] * 4, out_specs=vmem(), out_shape...  1.34 us
    ppermute x1, starting transfers between devices, body(): lax.ppermute(field[:, :1], 'slab', [(i + 1, i) for i in range(slabs - 1)])  1.29 us
    slice x1, local copies, waits for them, and re-layouts, body(): field[:, :1]  0.92 us
  transfers between devices with their start and end apart: 6, of which 5 were waited for; matrix products, arithmetic and copies ran while one was open for 0% of the time, Pallas kernels for 22%

profile of v6, /device:TPU:0, one launch (start us, length us, event | category | flops | bytes accessed | tf_op | source)
XLA Modules:
  0.0 26.4 jit_solution(2368430105508965291)
XLA Ops:
  0.6 0.9 %slice.3 = bf16[2,1,32,1024]{3,2,1,0:T(8,128)(2,1)S(1)} slice(bf16[2,16,32,1024]{3,2,1,0:T(8,128)(2,1)} %field.1), slice={[0:2], [0:1], [0:32], [0:1024]} | slice | bytes 262144 | tf_op jit(solution)/shard_map/slice | solution.py:340
  1.6 1.3 %collective-permute-start = (bf16[2,1,32,1024]{3,2,1,0:T(8,128)(2,1)S(1)}, bf16[2,1,32,1024]{3,2,1,0:T(8,128)(2,1)S(1)}, u32[]{:S(2)}, u32[]{:S(2)}) collective-permute-start(bf16[2,1,32,1024]{3,2,1,0:T(8,128)(2,1)S(1)} %slice.3), channel_id=1, source_target_pairs={{8,0},{16,8},{24,16},{9,1},{17,9},{25,17},{10,2},{18,10},{26,18},{... | collective-permute-start | bytes 393224 | tf_op jit(solution)/shard_map/ppermute | solution.py:340
  2.9 4.7 %march.1 = (f32[4,5,32,256]{3,2,1,0:T(8,128)S(1)}, bf16[4,8,32,256]{3,2,1,0:T(8,128)(2,1)S(1)}, bf16[4,2,32,256]{3,2,1,0:T(8,128)(2,1)S(1)}) custom-call(bf16[2,16,32,1024]{3,2,1,0:T(8,128)(2,1)} %field.1, s32[8,32,1024]{2,1,0:T(8,128)} %plane.1, s32[8,32,1024]{2,1,0:T(8,128)} %frac.1, s32[1,32,1024]{2,1,0:T(8,128)} %counts.1), custom_call_target="tpu_custom_call" | custom-call | flops 98304000 | bytes 4194304 | tf_op jit(solution)/shard_map/march/pallas_call | solution.py:128
  7.6 2.4 %collective-permute-done.follow = bf16[2,1,32,1024]{3,2,1,0:T(8,128)(2,1)S(1)} collective-permute-done((bf16[2,1,32,1024]{3,2,1,0:T(8,128)(2,1)S(1)}, bf16[2,1,32,1024]{3,2,1,0:T(8,128)(2,1)S(1)}, u32[]{:S(2)}, u32[]{:S(2)}) %collective-permute-start) | collective-permute-done | bytes 131104 | tf_op jit(solution)/shard_map/ppermute | solution.py:340
  10.0 0.4 %close.7 = s16[1,5,32,256]{3,2,1,0:T(8,128)(2,1)S(1)} custom-call(f32[4,5,32,256]{3,2,1,0:T(8,128)S(1)} %get-tuple-element.9.run, bf16[4,8,32,256]{3,2,1,0:T(8,128)(2,1)S(1)} %get-tuple-element.10.late, bf16[4,2,32,256]{3,2,1,0:T(8,128)(2,1)S(1)} %get-tuple-element.11.last, bf16[2,1,32,1024]{3,2,1,0:T(8,128)(2,1)S(1)} %collective-permute-done.follow), custom_call_target="tpu_custom_call" | custom-call | flops 12288000 | bytes 524288 | tf_op jit(solution)/shard_map/close/pallas_call | solution.py:186
  10.4 1.8 %collective-permute-start.2 = (s16[1,5,32,256]{3,2,1,0:T(8,128)(2,1)S(1)}, s16[1,5,32,256]{3,2,1,0:T(8,128)(2,1)S(1)}, u32[]{:S(2)}, u32[]{:S(2)}) collective-permute-start(s16[1,5,32,256]{3,2,1,0:T(8,128)(2,1)S(1)} %close.7), channel_id=1, source_target_pairs={{0,8},{16,24},{8,0},{24,16},{1,9},{17,25},{9,1},{25,17},{2,10},{18... | collective-permute-start | bytes 245768 | tf_op jit(solution)/shard_map/ppermute | solution.py:323
  12.2 0.4 %close.5 = s16[1,5,32,256]{3,2,1,0:T(8,128)(2,1)S(1)} custom-call(f32[4,5,32,256]{3,2,1,0:T(8,128)S(1)} %get-tuple-element.9.run, bf16[4,8,32,256]{3,2,1,0:T(8,128)(2,1)S(1)} %get-tuple-element.10.late, bf16[4,2,32,256]{3,2,1,0:T(8,128)(2,1)S(1)} %get-tuple-element.11.last, bf16[2,1,32,1024]{3,2,1,0:T(8,128)(2,1)S(1)} %collective-permute-done.follow), custom_call_target="tpu_custom_call" | custom-call | flops 12288000 | bytes 524288 | tf_op jit(solution)/shard_map/close/pallas_call | solution.py:186
  12.5 0.4 %collective-permute-start.1 = (s16[1,5,32,256]{3,2,1,0:T(8,128)(2,1)S(1)}, s16[1,5,32,256]{3,2,1,0:T(8,128)(2,1)S(1)}, u32[]{:S(2)}, u32[]{:S(2)}) collective-permute-start(s16[1,5,32,256]{3,2,1,0:T(8,128)(2,1)S(1)} %close.5), channel_id=1, source_target_pairs={{0,8},{16,24},{8,0},{24,16},{1,9},{17,25},{9,1},{25,17},{2,10},{18... | collective-permute-start | bytes 245768 | tf_op jit(solution)/shard_map/ppermute | solution.py:323
  12.9 0.3 %close.6.mine = f32[1,5,32,256]{3,2,1,0:T(8,128)S(1)} custom-call(f32[4,5,32,256]{3,2,1,0:T(8,128)S(1)} %get-tuple-element.9.run, bf16[4,8,32,256]{3,2,1,0:T(8,128)(2,1)S(1)} %get-tuple-element.10.late, bf16[4,2,32,256]{3,2,1,0:T(8,128)(2,1)S(1)} %get-tuple-element.11.last, bf16[2,1,32,1024]{3,2,1,0:T(8,128)(2,1)S(1)} %collective-permute-done.follow), custom_call_target="tpu_custom_call" | custom-call | flops 12288000 | bytes 524288 | tf_op jit(solution)/shard_map/close/pallas_call | solution.py:186
  13.2 2.2 %collective-permute-done.2.got = s16[1,5,32,256]{3,2,1,0:T(8,128)(2,1)S(1)} collective-permute-done((s16[1,5,32,256]{3,2,1,0:T(8,128)(2,1)S(1)}, s16[1,5,32,256]{3,2,1,0:T(8,128)(2,1)S(1)}, u32[]{:S(2)}, u32[]{:S(2)}) %collective-permute-start.2) | collective-permute-done | bytes 81952 | tf_op jit(solution)/shard_map/ppermute | solution.py:323
  15.5 0.1 relay.1
  15.6 2.8 %collective-permute-start.3 = (s16[1,5,32,256]{3,2,1,0:T(8,128)(2,1)S(1)}, s16[1,5,32,256]{3,2,1,0:T(8,128)(2,1)S(1)}, u32[]{:S(2)}, u32[]{:S(2)}) collective-permute-start(s16[1,5,32,256]{3,2,1,0:T(8,128)(2,1)S(1)} %relay.1), channel_id=1, source_target_pairs={{0,16},{8,24},{16,0},{24,8},{1,17},{9,25},{17,1},{25,9},{2,18},{10... | collective-permute-start | bytes 245768 | tf_op jit(solution)/shard_map/ppermute | solution.py:323
  18.4 0.3 %close.4.mine = f32[1,5,32,256]{3,2,1,0:T(8,128)S(1)} custom-call(f32[4,5,32,256]{3,2,1,0:T(8,128)S(1)} %get-tuple-element.9.run, bf16[4,8,32,256]{3,2,1,0:T(8,128)(2,1)S(1)} %get-tuple-element.10.late, bf16[4,2,32,256]{3,2,1,0:T(8,128)(2,1)S(1)} %get-tuple-element.11.last, bf16[2,1,32,1024]{3,2,1,0:T(8,128)(2,1)S(1)} %collective-permute-done.follow), custom_call_target="tpu_custom_call" | custom-call | flops 12288000 | bytes 524288 | tf_op jit(solution)/shard_map/close/pallas_call | solution.py:186
  18.7 0.0 collective-permute-done.1.refs_0_
  18.7 3.2 %collective-permute-done.3.refs_1_ = s16[1,5,32,256]{3,2,1,0:T(8,128)(2,1)S(1)} collective-permute-done((s16[1,5,32,256]{3,2,1,0:T(8,128)(2,1)S(1)}, s16[1,5,32,256]{3,2,1,0:T(8,128)(2,1)S(1)}, u32[]{:S(2)}, u32[]{:S(2)}) %collective-permute-start.3) | collective-permute-done | bytes 81952 | tf_op jit(solution)/shard_map/ppermute | solution.py:323
  21.9 0.2 finish.1
  22.0 0.1 collective-permute-start.4
  22.1 0.7 %collective-permute-start.5 = (f32[3,256]{1,0:T(4,128)S(1)}, f32[3,256]{1,0:T(4,128)S(1)}, u32[]{:S(2)}, u32[]{:S(2)}) collective-permute-start(f32[3,256]{1,0:T(4,128)S(1)} %get-tuple-element.14), channel_id=1, source_target_pairs={{1,2},{3,4},{5,6},{2,1},{4,3},{6,5},{0,8},{7,15},{9,10},{11,12},{1... | collective-permute-start | bytes 9224 | tf_op jit(solution)/shard_map/ppermute | solution.py:301
  22.8 0.4 %collective-permute-done.4.near = f32[3,256]{1,0:T(4,128)S(1)} collective-permute-done((f32[3,256]{1,0:T(4,128)S(1)}, f32[3,256]{1,0:T(4,128)S(1)}, u32[]{:S(2)}, u32[]{:S(2)}) %collective-permute-start.4) | collective-permute-done | bytes 3104 | tf_op jit(solution)/shard_map/ppermute | solution.py:307
  23.2 2.5 %collective-permute-done.5.far = f32[3,256]{1,0:T(4,128)S(1)} collective-permute-done((f32[3,256]{1,0:T(4,128)S(1)}, f32[3,256]{1,0:T(4,128)S(1)}, u32[]{:S(2)}, u32[]{:S(2)}) %collective-permute-start.5) | collective-permute-done | bytes 3104 | tf_op jit(solution)/shard_map/ppermute | solution.py:301
  25.8 0.7 %border.1 = (f32[32,256]{1,0:T(8,128)}, f32[32,256]{1,0:T(8,128)}, f32[32,256]{1,0:T(8,128)}) custom-call(f32[3,32,256]{2,1,0:T(8,128)S(1)} %get-tuple-element.12.image, f32[3,256]{1,0:T(4,128)S(1)} %collective-permute-done.4.near, f32[3,256]{1,0:T(4,128)S(1)} %collective-permute-done.5.far), custom_call_target="tpu_custom_call" | custom-call | tf_op jit(solution)/shard_map/border/pallas_call | solution.py:284
Async XLA Ops:
  1.6 8.4 %collective-permute-start = (bf16[2,1,32,1024]{3,2,1,0:T(8,128)(2,1)S(1)}, bf16[2,1,32,1024]{3,2,1,0:T(8,128)(2,1)S(1)}, u32[]{:S(2)}, u32[]{:S(2)}) collective-permute-start(bf16[2,1,32,1024]{3,2,1,0:T(8,128)(2,1)S(1)} %slice.3), channel_id=1, source_target_pairs={{8,0},{16,8},{24,16},{9,1},{17,9},{25,17},{10,2},{18,10},{26,18},{... | collective-permute-start | bytes 393224 | tf_op jit(solution)/shard_map/ppermute | solution.py:340
  10.4 5.1 %collective-permute-start.2 = (s16[1,5,32,256]{3,2,1,0:T(8,128)(2,1)S(1)}, s16[1,5,32,256]{3,2,1,0:T(8,128)(2,1)S(1)}, u32[]{:S(2)}, u32[]{:S(2)}) collective-permute-start(s16[1,5,32,256]{3,2,1,0:T(8,128)(2,1)S(1)} %close.7), channel_id=1, source_target_pairs={{0,8},{16,24},{8,0},{24,16},{1,9},{17,25},{9,1},{25,17},{2,10},{18... | collective-permute-start | bytes 245768 | tf_op jit(solution)/shard_map/ppermute | solution.py:323
  12.5 6.1 %collective-permute-start.1 = (s16[1,5,32,256]{3,2,1,0:T(8,128)(2,1)S(1)}, s16[1,5,32,256]{3,2,1,0:T(8,128)(2,1)S(1)}, u32[]{:S(2)}, u32[]{:S(2)}) collective-permute-start(s16[1,5,32,256]{3,2,1,0:T(8,128)(2,1)S(1)} %close.5), channel_id=1, source_target_pairs={{0,8},{16,24},{8,0},{24,16},{1,9},{17,25},{9,1},{25,17},{2,10},{18... | collective-permute-start | bytes 245768 | tf_op jit(solution)/shard_map/ppermute | solution.py:323
  15.6 6.3 %collective-permute-start.3 = (s16[1,5,32,256]{3,2,1,0:T(8,128)(2,1)S(1)}, s16[1,5,32,256]{3,2,1,0:T(8,128)(2,1)S(1)}, u32[]{:S(2)}, u32[]{:S(2)}) collective-permute-start(s16[1,5,32,256]{3,2,1,0:T(8,128)(2,1)S(1)} %relay.1), channel_id=1, source_target_pairs={{0,16},{8,24},{16,0},{24,8},{1,17},{9,25},{17,1},{25,9},{2,18},{10... | collective-permute-start | bytes 245768 | tf_op jit(solution)/shard_map/ppermute | solution.py:323
  22.0 1.2 %collective-permute-start.4 = (f32[3,256]{1,0:T(4,128)S(1)}, f32[3,256]{1,0:T(4,128)S(1)}, u32[]{:S(2)}, u32[]{:S(2)}) collective-permute-start(f32[3,256]{1,0:T(4,128)S(1)} %get-tuple-element.13), channel_id=1, source_target_pairs={{0,1},{2,3},{4,5},{6,7},{1,0},{3,2},{5,4},{7,6},{8,9},{10,11},{12,... | collective-permute-start | bytes 9224 | tf_op jit(solution)/shard_map/ppermute | solution.py:307
  22.1 3.7 %collective-permute-start.5 = (f32[3,256]{1,0:T(4,128)S(1)}, f32[3,256]{1,0:T(4,128)S(1)}, u32[]{:S(2)}, u32[]{:S(2)}) collective-permute-start(f32[3,256]{1,0:T(4,128)S(1)} %get-tuple-element.14), channel_id=1, source_target_pairs={{1,2},{3,4},{5,6},{2,1},{4,3},{6,5},{0,8},{7,15},{9,10},{11,12},{1... | collective-permute-start | bytes 9224 | tf_op jit(solution)/shard_map/ppermute | solution.py:301

commit v7 on v6

--- a/solution.py
+++ b/solution.py
@@ -209,7 +209,7 @@
     ]
 
 
-def relay(mine, got):
+def relay(mine, got, coded):
     _, kinds, rows, _ = mine.shape
 
     def kernel(mine, got, send):
@@ -222,13 +222,13 @@
                 got_first,
             )
             for what in range(kinds):
-                send[0, what, here, :] = encode(done[what], what)
+                send[0, what, here, :] = encode(done[what], what) if coded else done[what]
 
     return pl.pallas_call(
         kernel,
         in_specs=[vmem()] * 2,
         out_specs=vmem(),
-        out_shape=jax.ShapeDtypeStruct(got.shape, WIRE),
+        out_shape=jax.ShapeDtypeStruct(got.shape, WIRE if coded else jnp.float32),
         compiler_params=pltpu.CompilerParams(vmem_limit_bytes=16 << 20),
         name="relay",
     )(mine, got)
@@ -242,8 +242,8 @@
         *partner, image, near, far = refs
         odd = lax.axis_index("col") % 2 == 1
         done = [mine[0, what] for what in range(kinds)]
-        for bit, got in enumerate(partner):
-            got_first = (lax.axis_index("slab") >> bit) & 1 == 1
+        for got in partner:
+            got_first = (lax.axis_index("slab") >> 1) & 1 == 1
             done = join(done, [decode(got[0, what], what) for what in range(kinds)], got_first)
         row = lax.broadcasted_iota(jnp.int32, (rows, width), 0)
         for at, what in enumerate((COLOR, DEEP, COARSE)):
@@ -350,10 +350,10 @@
 
     got_a = swap(part(0, 1, True), slabs, 1)
     keep_a = part(2, 1, False)
-    got = swap(relay(keep_a, got_a), slabs, 2)
+    got = swap(relay(keep_a, got_a, True), slabs, 2)
     got_b = swap(part(1, 1, True), slabs, 1)
     keep_b = part(3, 1, False)
-    image, near, far = finish(keep_b, (got_b, got))
+    image, near, far = finish(relay(keep_b, got_b, False), (got,))
     return border(image, *neighbours(near, far))
 
 

time: 26.6 us -> 26.6 us (level)
  no operation moved by 1% of the time
where the time goes in v7:
time: 26.6 us; the launch traced here: 26.4 us
  waiting for transfers between devices  10.7 us (40%)
  starting transfers between devices  7.08 us (27%)
  Pallas kernels  6.96 us (26%)
  local copies, waits for them, and re-layouts  0.92 us (3%)
  between operations  0.71 us (3%)
    ppermute x3, waiting for transfers between devices, swap(): return lax.ppermute(x, 'slab', pairs(low, [i + distance for i in low]))  5.32 us
    ppermute x3, starting transfers between devices, swap(): return lax.ppermute(x, 'slab', pairs(low, [i + distance for i in low]))  4.97 us
    pallas_call x1, Pallas kernels, march(): pl.pallas_call(kernel, grid=(steps,), in_specs=[spec(2, depth), spec(slot...  4.69 us
    ppermute x1, waiting for transfers between devices, neighbours(): lax.ppermute(far, ('slab', 'col'), [(s * count + a, t * count + b) for s...  2.52 us
    ppermute x1, waiting for transfers between devices, body(): lax.ppermute(field[:, :1], 'slab', [(i + 1, i) for i in range(slabs - 1)])  2.45 us
    pallas_call x4, Pallas kernels, close(): pl.pallas_call(kernel, in_specs=[vmem()] * 4, out_specs=vmem(), out_shape...  1.34 us
    ppermute x1, starting transfers between devices, body(): lax.ppermute(field[:, :1], 'slab', [(i + 1, i) for i in range(slabs - 1)])  1.29 us
    slice x1, local copies, waits for them, and re-layouts, body(): field[:, :1]  0.92 us
  transfers between devices with their start and end apart: 6, of which 5 were waited for; matrix products, arithmetic and copies ran while one was open for 0% of the time, Pallas kernels for 22%

profile of v7, /device:TPU:0, one launch (start us, length us, event | category | flops | bytes accessed | tf_op | source)
XLA Modules:
  0.0 26.4 jit_solution(17574859414551993697)
XLA Ops:
  0.6 0.9 %slice.3 = bf16[2,1,32,1024]{3,2,1,0:T(8,128)(2,1)S(1)} slice(bf16[2,16,32,1024]{3,2,1,0:T(8,128)(2,1)} %field.1), slice={[0:2], [0:1], [0:32], [0:1024]} | slice | bytes 262144 | tf_op jit(solution)/shard_map/slice | solution.py:340
  1.6 1.3 %collective-permute-start = (bf16[2,1,32,1024]{3,2,1,0:T(8,128)(2,1)S(1)}, bf16[2,1,32,1024]{3,2,1,0:T(8,128)(2,1)S(1)}, u32[]{:S(2)}, u32[]{:S(2)}) collective-permute-start(bf16[2,1,32,1024]{3,2,1,0:T(8,128)(2,1)S(1)} %slice.3), channel_id=1, source_target_pairs={{8,0},{16,8},{24,16},{9,1},{17,9},{25,17},{10,2},{18,10},{26,18},{... | collective-permute-start | bytes 393224 | tf_op jit(solution)/shard_map/ppermute | solution.py:340
  2.9 4.7 %march.1 = (f32[4,5,32,256]{3,2,1,0:T(8,128)S(1)}, bf16[4,8,32,256]{3,2,1,0:T(8,128)(2,1)S(1)}, bf16[4,2,32,256]{3,2,1,0:T(8,128)(2,1)S(1)}) custom-call(bf16[2,16,32,1024]{3,2,1,0:T(8,128)(2,1)} %field.1, s32[8,32,1024]{2,1,0:T(8,128)} %plane.1, s32[8,32,1024]{2,1,0:T(8,128)} %frac.1, s32[1,32,1024]{2,1,0:T(8,128)} %counts.1), custom_call_target="tpu_custom_call" | custom-call | flops 98304000 | bytes 4194304 | tf_op jit(solution)/shard_map/march/pallas_call | solution.py:128
  7.6 2.4 %collective-permute-done.follow = bf16[2,1,32,1024]{3,2,1,0:T(8,128)(2,1)S(1)} collective-permute-done((bf16[2,1,32,1024]{3,2,1,0:T(8,128)(2,1)S(1)}, bf16[2,1,32,1024]{3,2,1,0:T(8,128)(2,1)S(1)}, u32[]{:S(2)}, u32[]{:S(2)}) %collective-permute-start) | collective-permute-done | bytes 131104 | tf_op jit(solution)/shard_map/ppermute | solution.py:340
  10.0 0.4 %close.7 = s16[1,5,32,256]{3,2,1,0:T(8,128)(2,1)S(1)} custom-call(f32[4,5,32,256]{3,2,1,0:T(8,128)S(1)} %get-tuple-element.9.run, bf16[4,8,32,256]{3,2,1,0:T(8,128)(2,1)S(1)} %get-tuple-element.10.late, bf16[4,2,32,256]{3,2,1,0:T(8,128)(2,1)S(1)} %get-tuple-element.11.last, bf16[2,1,32,1024]{3,2,1,0:T(8,128)(2,1)S(1)} %collective-permute-done.follow), custom_call_target="tpu_custom_call" | custom-call | flops 12288000 | bytes 524288 | tf_op jit(solution)/shard_map/close/pallas_call | solution.py:186
  10.4 1.8 %collective-permute-start.2 = (s16[1,5,32,256]{3,2,1,0:T(8,128)(2,1)S(1)}, s16[1,5,32,256]{3,2,1,0:T(8,128)(2,1)S(1)}, u32[]{:S(2)}, u32[]{:S(2)}) collective-permute-start(s16[1,5,32,256]{3,2,1,0:T(8,128)(2,1)S(1)} %close.7), channel_id=1, source_target_pairs={{0,8},{16,24},{8,0},{24,16},{1,9},{17,25},{9,1},{25,17},{2,10},{18... | collective-permute-start | bytes 245768 | tf_op jit(solution)/shard_map/ppermute | solution.py:323
  12.2 0.4 %close.5 = s16[1,5,32,256]{3,2,1,0:T(8,128)(2,1)S(1)} custom-call(f32[4,5,32,256]{3,2,1,0:T(8,128)S(1)} %get-tuple-element.9.run, bf16[4,8,32,256]{3,2,1,0:T(8,128)(2,1)S(1)} %get-tuple-element.10.late, bf16[4,2,32,256]{3,2,1,0:T(8,128)(2,1)S(1)} %get-tuple-element.11.last, bf16[2,1,32,1024]{3,2,1,0:T(8,128)(2,1)S(1)} %collective-permute-done.follow), custom_call_target="tpu_custom_call" | custom-call | flops 12288000 | bytes 524288 | tf_op jit(solution)/shard_map/close/pallas_call | solution.py:186
  12.5 0.4 %collective-permute-start.1 = (s16[1,5,32,256]{3,2,1,0:T(8,128)(2,1)S(1)}, s16[1,5,32,256]{3,2,1,0:T(8,128)(2,1)S(1)}, u32[]{:S(2)}, u32[]{:S(2)}) collective-permute-start(s16[1,5,32,256]{3,2,1,0:T(8,128)(2,1)S(1)} %close.5), channel_id=1, source_target_pairs={{0,8},{16,24},{8,0},{24,16},{1,9},{17,25},{9,1},{25,17},{2,10},{18... | collective-permute-start | bytes 245768 | tf_op jit(solution)/shard_map/ppermute | solution.py:323
  12.9 0.3 %close.6.mine = f32[1,5,32,256]{3,2,1,0:T(8,128)S(1)} custom-call(f32[4,5,32,256]{3,2,1,0:T(8,128)S(1)} %get-tuple-element.9.run, bf16[4,8,32,256]{3,2,1,0:T(8,128)(2,1)S(1)} %get-tuple-element.10.late, bf16[4,2,32,256]{3,2,1,0:T(8,128)(2,1)S(1)} %get-tuple-element.11.last, bf16[2,1,32,1024]{3,2,1,0:T(8,128)(2,1)S(1)} %collective-permute-done.follow), custom_call_target="tpu_custom_call" | custom-call | flops 12288000 | bytes 524288 | tf_op jit(solution)/shard_map/close/pallas_call | solution.py:186
  13.2 2.2 %collective-permute-done.2.got = s16[1,5,32,256]{3,2,1,0:T(8,128)(2,1)S(1)} collective-permute-done((s16[1,5,32,256]{3,2,1,0:T(8,128)(2,1)S(1)}, s16[1,5,32,256]{3,2,1,0:T(8,128)(2,1)S(1)}, u32[]{:S(2)}, u32[]{:S(2)}) %collective-permute-start.2) | collective-permute-done | bytes 81952 | tf_op jit(solution)/shard_map/ppermute | solution.py:323
  15.5 0.1 relay.3
  15.6 2.8 %collective-permute-start.3 = (s16[1,5,32,256]{3,2,1,0:T(8,128)(2,1)S(1)}, s16[1,5,32,256]{3,2,1,0:T(8,128)(2,1)S(1)}, u32[]{:S(2)}, u32[]{:S(2)}) collective-permute-start(s16[1,5,32,256]{3,2,1,0:T(8,128)(2,1)S(1)} %relay.3), channel_id=1, source_target_pairs={{0,16},{8,24},{16,0},{24,8},{1,17},{9,25},{17,1},{25,9},{2,18},{10... | collective-permute-start | bytes 245768 | tf_op jit(solution)/shard_map/ppermute | solution.py:323
  18.4 0.3 %close.4.mine = f32[1,5,32,256]{3,2,1,0:T(8,128)S(1)} custom-call(f32[4,5,32,256]{3,2,1,0:T(8,128)S(1)} %get-tuple-element.9.run, bf16[4,8,32,256]{3,2,1,0:T(8,128)(2,1)S(1)} %get-tuple-element.10.late, bf16[4,2,32,256]{3,2,1,0:T(8,128)(2,1)S(1)} %get-tuple-element.11.last, bf16[2,1,32,1024]{3,2,1,0:T(8,128)(2,1)S(1)} %collective-permute-done.follow), custom_call_target="tpu_custom_call" | custom-call | flops 12288000 | bytes 524288 | tf_op jit(solution)/shard_map/close/pallas_call | solution.py:186
  18.7 0.0 collective-permute-done.1.got
  18.7 0.1 relay.2.mine
  18.8 3.1 %collective-permute-done.3.refs_0_ = s16[1,5,32,256]{3,2,1,0:T(8,128)(2,1)S(1)} collective-permute-done((s16[1,5,32,256]{3,2,1,0:T(8,128)(2,1)S(1)}, s16[1,5,32,256]{3,2,1,0:T(8,128)(2,1)S(1)}, u32[]{:S(2)}, u32[]{:S(2)}) %collective-permute-start.3) | collective-permute-done | bytes 81952 | tf_op jit(solution)/shard_map/ppermute | solution.py:323
  21.9 0.1 finish.1
  22.0 0.1 collective-permute-start.4
  22.0 0.7 %collective-permute-start.5 = (f32[3,256]{1,0:T(4,128)S(1)}, f32[3,256]{1,0:T(4,128)S(1)}, u32[]{:S(2)}, u32[]{:S(2)}) collective-permute-start(f32[3,256]{1,0:T(4,128)S(1)} %get-tuple-element.14), channel_id=1, source_target_pairs={{1,2},{3,4},{5,6},{2,1},{4,3},{6,5},{0,8},{7,15},{9,10},{11,12},{1... | collective-permute-start | bytes 9224 | tf_op jit(solution)/shard_map/ppermute | solution.py:301
  22.8 0.4 %collective-permute-done.4.near = f32[3,256]{1,0:T(4,128)S(1)} collective-permute-done((f32[3,256]{1,0:T(4,128)S(1)}, f32[3,256]{1,0:T(4,128)S(1)}, u32[]{:S(2)}, u32[]{:S(2)}) %collective-permute-start.4) | collective-permute-done | bytes 3104 | tf_op jit(solution)/shard_map/ppermute | solution.py:307
  23.2 2.5 %collective-permute-done.5.far = f32[3,256]{1,0:T(4,128)S(1)} collective-permute-done((f32[3,256]{1,0:T(4,128)S(1)}, f32[3,256]{1,0:T(4,128)S(1)}, u32[]{:S(2)}, u32[]{:S(2)}) %collective-permute-start.5) | collective-permute-done | bytes 3104 | tf_op jit(solution)/shard_map/ppermute | solution.py:301
  25.7 0.7 %border.1 = (f32[32,256]{1,0:T(8,128)}, f32[32,256]{1,0:T(8,128)}, f32[32,256]{1,0:T(8,128)}) custom-call(f32[3,32,256]{2,1,0:T(8,128)S(1)} %get-tuple-element.12.image, f32[3,256]{1,0:T(4,128)S(1)} %collective-permute-done.4.near, f32[3,256]{1,0:T(4,128)S(1)} %collective-permute-done.5.far), custom_call_target="tpu_custom_call" | custom-call | tf_op jit(solution)/shard_map/border/pallas_call | solution.py:284
Async XLA Ops:
  1.6 8.4 %collective-permute-start = (bf16[2,1,32,1024]{3,2,1,0:T(8,128)(2,1)S(1)}, bf16[2,1,32,1024]{3,2,1,0:T(8,128)(2,1)S(1)}, u32[]{:S(2)}, u32[]{:S(2)}) collective-permute-start(bf16[2,1,32,1024]{3,2,1,0:T(8,128)(2,1)S(1)} %slice.3), channel_id=1, source_target_pairs={{8,0},{16,8},{24,16},{9,1},{17,9},{25,17},{10,2},{18,10},{26,18},{... | collective-permute-start | bytes 393224 | tf_op jit(solution)/shard_map/ppermute | solution.py:340
  10.4 5.1 %collective-permute-start.2 = (s16[1,5,32,256]{3,2,1,0:T(8,128)(2,1)S(1)}, s16[1,5,32,256]{3,2,1,0:T(8,128)(2,1)S(1)}, u32[]{:S(2)}, u32[]{:S(2)}) collective-permute-start(s16[1,5,32,256]{3,2,1,0:T(8,128)(2,1)S(1)} %close.7), channel_id=1, source_target_pairs={{0,8},{16,24},{8,0},{24,16},{1,9},{17,25},{9,1},{25,17},{2,10},{18... | collective-permute-start | bytes 245768 | tf_op jit(solution)/shard_map/ppermute | solution.py:323
  12.5 6.1 %collective-permute-start.1 = (s16[1,5,32,256]{3,2,1,0:T(8,128)(2,1)S(1)}, s16[1,5,32,256]{3,2,1,0:T(8,128)(2,1)S(1)}, u32[]{:S(2)}, u32[]{:S(2)}) collective-permute-start(s16[1,5,32,256]{3,2,1,0:T(8,128)(2,1)S(1)} %close.5), channel_id=1, source_target_pairs={{0,8},{16,24},{8,0},{24,16},{1,9},{17,25},{9,1},{25,17},{2,10},{18... | collective-permute-start | bytes 245768 | tf_op jit(solution)/shard_map/ppermute | solution.py:323
  15.6 6.3 %collective-permute-start.3 = (s16[1,5,32,256]{3,2,1,0:T(8,128)(2,1)S(1)}, s16[1,5,32,256]{3,2,1,0:T(8,128)(2,1)S(1)}, u32[]{:S(2)}, u32[]{:S(2)}) collective-permute-start(s16[1,5,32,256]{3,2,1,0:T(8,128)(2,1)S(1)} %relay.3), channel_id=1, source_target_pairs={{0,16},{8,24},{16,0},{24,8},{1,17},{9,25},{17,1},{25,9},{2,18},{10... | collective-permute-start | bytes 245768 | tf_op jit(solution)/shard_map/ppermute | solution.py:323
  22.0 1.2 %collective-permute-start.4 = (f32[3,256]{1,0:T(4,128)S(1)}, f32[3,256]{1,0:T(4,128)S(1)}, u32[]{:S(2)}, u32[]{:S(2)}) collective-permute-start(f32[3,256]{1,0:T(4,128)S(1)} %get-tuple-element.13), channel_id=1, source_target_pairs={{0,1},{2,3},{4,5},{6,7},{1,0},{3,2},{5,4},{7,6},{8,9},{10,11},{12,... | collective-permute-start | bytes 9224 | tf_op jit(solution)/shard_map/ppermute | solution.py:307
  22.0 3.7 %collective-permute-start.5 = (f32[3,256]{1,0:T(4,128)S(1)}, f32[3,256]{1,0:T(4,128)S(1)}, u32[]{:S(2)}, u32[]{:S(2)}) collective-permute-start(f32[3,256]{1,0:T(4,128)S(1)} %get-tuple-element.14), channel_id=1, source_target_pairs={{1,2},{3,4},{5,6},{2,1},{4,3},{6,5},{0,8},{7,15},{9,10},{11,12},{1... | collective-permute-start | bytes 9224 | tf_op jit(solution)/shard_map/ppermute | solution.py:301

commit v8 on v7

--- a/solution.py
+++ b/solution.py
@@ -102,12 +102,12 @@
     lax.fori_loop(0, (rows // ROWS) * across, one, 0)
 
 
-def march(field, plane, frac, counts, width):
-    _, depth, rows, columns = field.shape
-    slots, steps = plane.shape[0], columns // width
+def march(field, plane, frac, counts, slab, steps, block_of, width):
+    _, depth, rows, _ = field.shape
+    slots = plane.shape[0]
     total_depth = depth * lax.axis_size("slab")
 
-    def kernel(field, plane, frac, counts, run, late, last):
+    def kernel(_, field, plane, frac, counts, run, late, last):
         base = (lax.axis_index("slab") * (8 * depth)).astype(jnp.float32)
         last[0] = field[:, depth - 1]
         tiles(rows, width, lambda here, cols: march_rows(
@@ -116,20 +116,23 @@
 
     def spec(*lead):
         zeros = (0,) * len(lead)
-        return pl.BlockSpec(lead + (rows, width), lambda b: zeros + (0, b))
+        return pl.BlockSpec(lead + (rows, width), lambda b, s: zeros + (0, block_of(b, s[0])))
 
     def out(*lead):
         zeros = (0,) * len(lead)
-        return pl.BlockSpec((1,) + lead + (rows, width), lambda b: (b,) + zeros + (0, 0))
+        return pl.BlockSpec((1,) + lead + (rows, width), lambda b, s: (b,) + zeros + (0, 0))
 
     def shape(*lead, kind):
         return jax.ShapeDtypeStruct((steps,) + lead + (rows, width), kind)
 
     return pl.pallas_call(
         kernel,
-        grid=(steps,),
-        in_specs=[spec(2, depth), spec(slots), spec(slots), spec(1)],
-        out_specs=[out(5), out(slots), out(2)],
+        grid_spec=pltpu.PrefetchScalarGridSpec(
+            num_scalar_prefetch=1,
+            grid=(steps,),
+            in_specs=[spec(2, depth), spec(slots), spec(slots), spec(1)],
+            out_specs=[out(5), out(slots), out(2)],
+        ),
         out_shape=[
             shape(5, kind=jnp.float32), shape(slots, kind=jnp.bfloat16),
             shape(2, kind=jnp.bfloat16),
@@ -140,24 +143,29 @@
             transcendentals=0,
         ),
         name="march",
-    )(*(pltpu.with_memory_space_constraint(x, pltpu.HBM) for x in (field, plane, frac, counts)))
-
-
-def close(ahead, follow, depth, first, steps, block_of, coded):
+    )(slab, *(pltpu.with_memory_space_constraint(x, pltpu.HBM)
+              for x in (field, plane, frac, counts)))
+
+
+def close(ahead, follow, depth, steps, run_of, place_of, coded):
     run, late, last = ahead
     _, slots, rows, width = late.shape
     total_depth = depth * lax.axis_size("slab")
 
     def kernel(run, late, last, follow, out):
         s = lax.axis_index("slab")
+        behind = s < lax.axis_size("slab") - 1
         base = (s * (8 * depth) + 8 * (depth - 1)).astype(jnp.float32)
 
         def step(i, here, cols):
-            b = block_of(first + i, s)
-            start = b * width + cols.start
+            b = run_of(i, s)
+            start = place_of(b, s) * width + cols.start
             there = pl.ds(pl.multiple_of(start, LANES), LANES)
             low = [last[b, ch, here, cols].astype(jnp.float32) * SCALES[ch] for ch in (0, 1)]
-            high = [follow[ch, 0, here, there].astype(jnp.float32) * SCALES[ch] for ch in (0, 1)]
+            high = [
+                jnp.where(behind, follow[ch, 0, here, there].astype(jnp.float32) * SCALES[ch], 0.0)
+                for ch in (0, 1)
+            ]
             slope = [(h - l) * 0.125 for h, l in zip(high, low)]
             color, deep, passed = (run[b, what, here, cols] for what in (COLOR, DEEP, FINE))
             for k in range(slots):
@@ -197,6 +205,36 @@
     )(run, late, last, follow)
 
 
+def heads(field, half_of):
+    channels, _, rows, columns = field.shape
+    width = columns // 2
+
+    def kernel(field, first, second, sem):
+        half = half_of(lax.axis_index("slab"))
+        copies = [
+            pltpu.make_async_copy(
+                field.at[ch, 0, :, pl.ds(pl.multiple_of(at * width, width), width)],
+                out.at[ch, 0], sem.at[i, ch],
+            )
+            for i, (out, at) in enumerate(((first, half), (second, 1 - half)))
+            for ch in range(channels)
+        ]
+        for copy in copies:
+            copy.start()
+        for copy in copies:
+            copy.wait()
+
+    return pl.pallas_call(
+        kernel,
+        in_specs=[pl.BlockSpec(memory_space=pltpu.HBM)],
+        out_specs=[vmem()] * 2,
+        out_shape=[jax.ShapeDtypeStruct((channels, 1, rows, width), field.dtype)] * 2,
+        scratch_shapes=[pltpu.SemaphoreType.DMA((2, channels))],
+        compiler_params=pltpu.CompilerParams(vmem_limit_bytes=16 << 20),
+        name="heads",
+    )(pltpu.with_memory_space_constraint(field, pltpu.HBM))
+
+
 def join(mine, got, got_first):
     first = [jnp.where(got_first, g, m) for m, g in zip(mine, got)]
     last = [jnp.where(got_first, m, g) for m, g in zip(mine, got)]
@@ -318,41 +356,50 @@
     return jnp.stack(done)[None]
 
 
-def swap(x, count, distance):
+def swap(x, route):
+    return lax.ppermute(x, "slab", route)
+
+
+def across(count, distance):
     low = [i for i in range(count) if not i & distance]
-    return lax.ppermute(x, "slab", pairs(low, [i + distance for i in low]))
+    return pairs(low, [i + distance for i in low])
 
 
 def body(field, fine_plane, fine_frac, counts):
     slabs = lax.axis_size("slab")
     depth, columns = field.shape[1], field.shape[3]
     width = columns // slabs
-    fast = slabs == 4 and width % LANES == 0
-    block = width if fast else LANES
-    blocks = columns // block
-
-    def block_of(b, s):
-        if not fast:
-            return b
-        parity = jnp.where(b < 2, 1 - (s & 1), s & 1)
-        return 2 * (((s >> 1) & 1) ^ 1 ^ (b & 1)) + parity
-
-    follow = lax.ppermute(field[:, :1], "slab", [(i + 1, i) for i in range(slabs - 1)])
-    ahead = march(field, fine_plane, fine_frac, counts, block)
-
-    def part(first, steps, coded):
-        return close(ahead, follow, depth, first, steps, block_of, coded)
-
-    if not fast:
-        parts = part(0, blocks, False)
+    slab = lax.axis_index("slab").reshape(1).astype(jnp.int32)
+    inputs = (field, fine_plane, fine_frac, counts, slab)
+    if slabs != 4 or width % LANES:
+        blocks = columns // LANES
+        ahead = march(*inputs, blocks, lambda b, s: b, LANES)
+        follow = lax.ppermute(field[:, :1], "slab", [(i + 1, i) for i in range(slabs - 1)])
+        parts = close(ahead, follow, depth, blocks, lambda i, s: i, lambda b, s: b, False)
         image, near, far = finish(wide_exchange(parts, slabs, width), ())
         return border(image, *neighbours(near, far))
 
-    got_a = swap(part(0, 1, True), slabs, 1)
-    keep_a = part(2, 1, False)
-    got = swap(relay(keep_a, got_a, True), slabs, 2)
-    got_b = swap(part(1, 1, True), slabs, 1)
-    keep_b = part(3, 1, False)
+    def early(s):
+        return 1 - ((s >> 1) & 1)
+
+    ring = [((i + 1) % slabs, i) for i in range(slabs)]
+    head_a, head_b = heads(field, lambda s: early((s + slabs - 1) % slabs))
+    follow_a = swap(head_a, ring)
+    follow_b = swap(head_b, ring)
+    theirs, ours = (lambda i, s: 1 - (s & 1)), (lambda i, s: s & 1)
+
+    ahead = march(*inputs, 2, lambda b, s: 2 * early(s) + b, width)
+    same = lambda b, s: b
+    send_a = close(ahead, follow_a, depth, 1, theirs, same, True)
+    got_a = swap(send_a, across(slabs, 1))
+    keep_a = close(ahead, follow_a, depth, 1, ours, same, False)
+    only = lambda i, s: 0
+    ahead = march(*inputs, 1, lambda b, s: 2 * (1 - early(s)) + theirs(b, s), width)
+    send_b = close(ahead, follow_b, depth, 1, only, theirs, True)
+    got_b = swap(send_b, across(slabs, 1))
+    got = swap(relay(keep_a, got_a, True), across(slabs, 2))
+    ahead = march(*inputs, 1, lambda b, s: 2 * (1 - early(s)) + ours(b, s), width)
+    keep_b = close(ahead, follow_b, depth, 1, only, ours, False)
     image, near, far = finish(relay(keep_b, got_b, False), (got,))
     return border(image, *neighbours(near, far))
 

time: 26.6 us -> 28.8 us (1.083)
  starting transfers between devices: 7.08 us -> 13.6 us
  waiting for transfers between devices: 10.7 us -> 4.5 us
  Pallas kernels: 6.96 us -> 9.67 us
  local copies, waits for them, and re-layouts: 0.92 us -> 0 us
    ppermute x4 -> x5, starting transfers between devices: 6.26 us -> 13.5 us  [swap(): return lax.ppermute(x, 'slab', route)]
    ppermute x4 -> x5, waiting for transfers between devices: 7.76 us -> 0.9 us  [swap(): return lax.ppermute(x, 'slab', route)]
    pallas_call x1 -> x4, Pallas kernels: 4.69 us -> 7.34 us  [the longest x3 6.49 us: march(): pl.pallas_call(kernel, grid_spec=pltpu.PrefetchScalarGridSpec(num_scalar_...]
    slice x1 -> x0, local copies, waits for them, and re-layouts: 0.92 us -> none  [body(): field[:, :1]]
    ppermute x1, starting transfers between devices: 0.75 us -> 0.07 us  [neighbours(): lax.ppermute(far, ('slab', 'col'), [(s * count + a, t * count + b) for s...]
    ppermute x1, waiting for transfers between devices: 0.4 us -> 1.07 us  [neighbours(): lax.ppermute(near, 'col', pairs(range(0, count - 1, 2), range(1, count, 2)))]
  transfers between devices with their start and end apart: 6 -> 7, of which waited for: 5 -> 3; matrix products, arithmetic and copies ran while one was open for 0% -> 0% of each run, Pallas kernels for 22% -> 27%
where the time goes in v8:
time: 28.8 us; the launch traced here: 28.5 us
  starting transfers between devices  13.6 us (47%)
  Pallas kernels  9.67 us (34%)
  waiting for transfers between devices  4.5 us (16%)
  between operations  0.76 us (3%)
    ppermute x5, starting transfers between devices, swap(): return lax.ppermute(x, 'slab', route)  13.5 us
    pallas_call x3, Pallas kernels, march(): pl.pallas_call(kernel, grid_spec=pltpu.PrefetchScalarGridSpec(num_scalar_...  6.49 us
    ppermute x1, waiting for transfers between devices, neighbours(): lax.ppermute(far, ('slab', 'col'), [(s * count + a, t * count + b) for s...  2.52 us
    pallas_call x4, Pallas kernels, close(): pl.pallas_call(kernel, in_specs=[vmem()] * 4, out_specs=vmem(), out_shape...  1.4 us
    ppermute x1, waiting for transfers between devices, neighbours(): lax.ppermute(near, 'col', pairs(range(0, count - 1, 2), range(1, count, 2)))  1.07 us
    ppermute x5, waiting for transfers between devices, swap(): return lax.ppermute(x, 'slab', route)  0.9 us
    pallas_call x1, Pallas kernels, heads(): pl.pallas_call(kernel, in_specs=[pl.BlockSpec(memory_space=pltpu.HBM)], o...  0.86 us
    pallas_call x1, Pallas kernels, border(): pl.pallas_call(kernel, in_specs=[vmem()] * 3, out_specs=[vmem()] * 3, out...  0.65 us
  transfers between devices with their start and end apart: 7, of which 3 were waited for; matrix products, arithmetic and copies ran while one was open for 0% of the time, Pallas kernels for 27%

profile of v8, /device:TPU:0, one launch (start us, length us, event | category | flops | bytes accessed | tf_op | source)
XLA Modules:
  0.0 28.5 jit_solution(12890193399174124822)
XLA Ops:
  0.6 0.9 %heads.1 = (bf16[2,1,32,512]{3,2,1,0:T(8,128)(2,1)S(1)}, bf16[2,1,32,512]{3,2,1,0:T(8,128)(2,1)S(1)}) custom-call(bf16[2,16,32,1024]{3,2,1,0:T(8,128)(2,1)} %field.7), custom_call_target="tpu_custom_call" | custom-call | tf_op jit(solution)/shard_map/heads/pallas_call | solution.py:227
  1.5 5.1 %collective-permute-start.2 = (bf16[2,1,32,512]{3,2,1,0:T(8,128)(2,1)S(1)}, bf16[2,1,32,512]{3,2,1,0:T(8,128)(2,1)S(1)}, u32[]{:S(2)}, u32[]{:S(2)}) collective-permute-start(bf16[2,1,32,512]{3,2,1,0:T(8,128)(2,1)S(1)} %get-tuple-element.27), channel_id=1, source_target_pairs={{8,0},{16,8},{24,16},{0,24},{9,1},{17,9},{25,17},{1,25},{10,2},{18... | collective-permute-start | bytes 196616 | tf_op jit(solution)/shard_map/ppermute | solution.py:360
  6.6 2.7 %march.5 = (f32[2,5,32,256]{3,2,1,0:T(8,128)S(1)}, bf16[2,8,32,256]{3,2,1,0:T(8,128)(2,1)S(1)}, bf16[2,2,32,256]{3,2,1,0:T(8,128)(2,1)S(1)}) custom-call(s32[1]{0:T(128)} %bitcast._, bf16[2,16,32,1024]{3,2,1,0:T(8,128)(2,1)} %field.7, s32[8,32,1024]{2,1,0:T(8,128)} %plane.5, s32[8,32,1024]{2,1,0:T(8,128)} %frac.5, s32[1,32,1024]{2,1,0:T(8,128)} %counts.5), custom_call_target="tpu_custom_call" | custom-call | flops 49152000 | bytes 2097152 | tf_op jit(solution)/shard_map/march/pallas_call | solution.py:128
  9.3 0.0 collective-permute-done.2.follow
  9.3 0.4 %close.7 = s16[1,5,32,256]{3,2,1,0:T(8,128)(2,1)S(1)} custom-call(f32[2,5,32,256]{3,2,1,0:T(8,128)S(1)} %get-tuple-element.24.run, bf16[2,8,32,256]{3,2,1,0:T(8,128)(2,1)S(1)} %get-tuple-element.25.late, bf16[2,2,32,256]{3,2,1,0:T(8,128)(2,1)S(1)} %get-tuple-element.26.last, bf16[2,1,32,512]{3,2,1,0:T(8,128)(2,1)S(1)} %collective-permute-done.2.follow), custom_call_target="tpu_custom_call" | custom-call | flops 12288000 | bytes 524288 | tf_op jit(solution)/shard_map/close/pallas_call | solution.py:194
  9.7 0.1 collective-permute-start.3
  9.8 3.4 %collective-permute-start = (bf16[2,1,32,512]{3,2,1,0:T(8,128)(2,1)S(1)}, bf16[2,1,32,512]{3,2,1,0:T(8,128)(2,1)S(1)}, u32[]{:S(2)}, u32[]{:S(2)}) collective-permute-start(bf16[2,1,32,512]{3,2,1,0:T(8,128)(2,1)S(1)} %get-tuple-element.20), channel_id=1, source_target_pairs={{8,0},{16,8},{24,16},{0,24},{9,1},{17,9},{25,17},{1,25},{10,2},{18... | collective-permute-start | bytes 196616 | tf_op jit(solution)/shard_map/ppermute | solution.py:360
  13.2 1.9 %march.4 = (f32[1,5,32,256]{3,2,1,0:T(8,128)S(1)}, bf16[1,8,32,256]{3,2,1,0:T(8,128)(2,1)S(1)}, bf16[1,2,32,256]{3,2,1,0:T(8,128)(2,1)S(1)}) custom-call(s32[1]{0:T(128)} %bitcast._, bf16[2,16,32,1024]{3,2,1,0:T(8,128)(2,1)} %field.7, s32[8,32,1024]{2,1,0:T(8,128)} %plane.5, s32[8,32,1024]{2,1,0:T(8,128)} %frac.5, s32[1,32,1024]{2,1,0:T(8,128)} %counts.5), custom_call_target="tpu_custom_call" | custom-call | flops 24576000 | bytes 1048576 | tf_op jit(solution)/shard_map/march/pallas_call | solution.py:128
  15.1 0.0 collective-permute-done.follow
  15.1 0.4 %close.5 = s16[1,5,32,256]{3,2,1,0:T(8,128)(2,1)S(1)} custom-call(f32[1,5,32,256]{3,2,1,0:T(8,128)S(1)} %get-tuple-element.21.run, bf16[1,8,32,256]{3,2,1,0:T(8,128)(2,1)S(1)} %get-tuple-element.22.late, bf16[1,2,32,256]{3,2,1,0:T(8,128)(2,1)S(1)} %get-tuple-element.23.last, bf16[2,1,32,512]{3,2,1,0:T(8,128)(2,1)S(1)} %collective-permute-done.follow), custom_call_target="tpu_custom_call" | custom-call | flops 12288000 | bytes 524288 | tf_op jit(solution)/shard_map/close/pallas_call | solution.py:194
  15.5 1.4 %collective-permute-start.1 = (s16[1,5,32,256]{3,2,1,0:T(8,128)(2,1)S(1)}, s16[1,5,32,256]{3,2,1,0:T(8,128)(2,1)S(1)}, u32[]{:S(2)}, u32[]{:S(2)}) collective-permute-start(s16[1,5,32,256]{3,2,1,0:T(8,128)(2,1)S(1)} %close.5), channel_id=1, source_target_pairs={{0,8},{16,24},{8,0},{24,16},{1,9},{17,25},{9,1},{25,17},{2,10},{18... | collective-permute-start | bytes 245768 | tf_op jit(solution)/shard_map/ppermute | solution.py:360
  16.9 0.3 %close.6.mine = f32[1,5,32,256]{3,2,1,0:T(8,128)S(1)} custom-call(f32[2,5,32,256]{3,2,1,0:T(8,128)S(1)} %get-tuple-element.24.run, bf16[2,8,32,256]{3,2,1,0:T(8,128)(2,1)S(1)} %get-tuple-element.25.late, bf16[2,2,32,256]{3,2,1,0:T(8,128)(2,1)S(1)} %get-tuple-element.26.last, bf16[2,1,32,512]{3,2,1,0:T(8,128)(2,1)S(1)} %collective-permute-done.2.follow), custom_call_target="tpu_custom_call" | custom-call | flops 12288000 | bytes 524288 | tf_op jit(solution)/shard_map/close/pallas_call | solution.py:194
  17.3 0.1 relay.3
  17.4 3.4 %collective-permute-start.4 = (s16[1,5,32,256]{3,2,1,0:T(8,128)(2,1)S(1)}, s16[1,5,32,256]{3,2,1,0:T(8,128)(2,1)S(1)}, u32[]{:S(2)}, u32[]{:S(2)}) collective-permute-start(s16[1,5,32,256]{3,2,1,0:T(8,128)(2,1)S(1)} %relay.3), channel_id=1, source_target_pairs={{0,16},{8,24},{16,0},{24,8},{1,17},{9,25},{17,1},{25,9},{2,18},{10... | collective-permute-start | bytes 245768 | tf_op jit(solution)/shard_map/ppermute | solution.py:360
  20.8 1.9 %march.3 = (f32[1,5,32,256]{3,2,1,0:T(8,128)S(1)}, bf16[1,8,32,256]{3,2,1,0:T(8,128)(2,1)S(1)}, bf16[1,2,32,256]{3,2,1,0:T(8,128)(2,1)S(1)}) custom-call(s32[1]{0:T(128)} %bitcast._, bf16[2,16,32,1024]{3,2,1,0:T(8,128)(2,1)} %field.7, s32[8,32,1024]{2,1,0:T(8,128)} %plane.5, s32[8,32,1024]{2,1,0:T(8,128)} %frac.5, s32[1,32,1024]{2,1,0:T(8,128)} %counts.5), custom_call_target="tpu_custom_call" | custom-call | flops 24576000 | bytes 1048576 | tf_op jit(solution)/shard_map/march/pallas_call | solution.py:128
  22.7 0.3 %close.4.mine = f32[1,5,32,256]{3,2,1,0:T(8,128)S(1)} custom-call(f32[1,5,32,256]{3,2,1,0:T(8,128)S(1)} %get-tuple-element.17.run, bf16[1,8,32,256]{3,2,1,0:T(8,128)(2,1)S(1)} %get-tuple-element.18.late, bf16[1,2,32,256]{3,2,1,0:T(8,128)(2,1)S(1)} %get-tuple-element.19.last, bf16[2,1,32,512]{3,2,1,0:T(8,128)(2,1)S(1)} %collective-permute-done.follow), custom_call_target="tpu_custom_call" | custom-call | flops 12288000 | bytes 524288 | tf_op jit(solution)/shard_map/close/pallas_call | solution.py:194
  23.1 0.1 relay.2.mine
  23.1 0.9 %collective-permute-done.4.refs_0_ = s16[1,5,32,256]{3,2,1,0:T(8,128)(2,1)S(1)} collective-permute-done((s16[1,5,32,256]{3,2,1,0:T(8,128)(2,1)S(1)}, s16[1,5,32,256]{3,2,1,0:T(8,128)(2,1)S(1)}, u32[]{:S(2)}, u32[]{:S(2)}) %collective-permute-start.4) | collective-permute-done | bytes 81952 | tf_op jit(solution)/shard_map/ppermute | solution.py:360
  24.0 0.1 finish.1
  24.1 0.1 collective-permute-start.5
  24.2 0.1 collective-permute-start.6
  24.3 1.1 %collective-permute-done.5.near = f32[3,256]{1,0:T(4,128)S(1)} collective-permute-done((f32[3,256]{1,0:T(4,128)S(1)}, f32[3,256]{1,0:T(4,128)S(1)}, u32[]{:S(2)}, u32[]{:S(2)}) %collective-permute-start.5) | collective-permute-done | bytes 3104 | tf_op jit(solution)/shard_map/ppermute | solution.py:345
  25.4 2.5 %collective-permute-done.6.far = f32[3,256]{1,0:T(4,128)S(1)} collective-permute-done((f32[3,256]{1,0:T(4,128)S(1)}, f32[3,256]{1,0:T(4,128)S(1)}, u32[]{:S(2)}, u32[]{:S(2)}) %collective-permute-start.6) | collective-permute-done | bytes 3104 | tf_op jit(solution)/shard_map/ppermute | solution.py:339
  27.9 0.7 %border.1 = (f32[32,256]{1,0:T(8,128)}, f32[32,256]{1,0:T(8,128)}, f32[32,256]{1,0:T(8,128)}) custom-call(f32[3,32,256]{2,1,0:T(8,128)S(1)} %get-tuple-element.28.image, f32[3,256]{1,0:T(4,128)S(1)} %collective-permute-done.5.near, f32[3,256]{1,0:T(4,128)S(1)} %collective-permute-done.6.far), custom_call_target="tpu_custom_call" | custom-call | tf_op jit(solution)/shard_map/border/pallas_call | solution.py:322
  (2 shorter events, 0.0 us)
Async XLA Ops:
  1.5 7.8 %collective-permute-start.2 = (bf16[2,1,32,512]{3,2,1,0:T(8,128)(2,1)S(1)}, bf16[2,1,32,512]{3,2,1,0:T(8,128)(2,1)S(1)}, u32[]{:S(2)}, u32[]{:S(2)}) collective-permute-start(bf16[2,1,32,512]{3,2,1,0:T(8,128)(2,1)S(1)} %get-tuple-element.27), channel_id=1, source_target_pairs={{8,0},{16,8},{24,16},{0,24},{9,1},{17,9},{25,17},{1,25},{10,2},{18... | collective-permute-start | bytes 196616 | tf_op jit(solution)/shard_map/ppermute | solution.py:360
  9.7 7.5 %collective-permute-start.3 = (s16[1,5,32,256]{3,2,1,0:T(8,128)(2,1)S(1)}, s16[1,5,32,256]{3,2,1,0:T(8,128)(2,1)S(1)}, u32[]{:S(2)}, u32[]{:S(2)}) collective-permute-start(s16[1,5,32,256]{3,2,1,0:T(8,128)(2,1)S(1)} %close.7), channel_id=1, source_target_pairs={{0,8},{16,24},{8,0},{24,16},{1,9},{17,25},{9,1},{25,17},{2,10},{18... | collective-permute-start | bytes 245768 | tf_op jit(solution)/shard_map/ppermute | solution.py:360
  9.8 5.3 %collective-permute-start = (bf16[2,1,32,512]{3,2,1,0:T(8,128)(2,1)S(1)}, bf16[2,1,32,512]{3,2,1,0:T(8,128)(2,1)S(1)}, u32[]{:S(2)}, u32[]{:S(2)}) collective-permute-start(bf16[2,1,32,512]{3,2,1,0:T(8,128)(2,1)S(1)} %get-tuple-element.20), channel_id=1, source_target_pairs={{8,0},{16,8},{24,16},{0,24},{9,1},{17,9},{25,17},{1,25},{10,2},{18... | collective-permute-start | bytes 196616 | tf_op jit(solution)/shard_map/ppermute | solution.py:360
  15.5 7.6 %collective-permute-start.1 = (s16[1,5,32,256]{3,2,1,0:T(8,128)(2,1)S(1)}, s16[1,5,32,256]{3,2,1,0:T(8,128)(2,1)S(1)}, u32[]{:S(2)}, u32[]{:S(2)}) collective-permute-start(s16[1,5,32,256]{3,2,1,0:T(8,128)(2,1)S(1)} %close.5), channel_id=1, source_target_pairs={{0,8},{16,24},{8,0},{24,16},{1,9},{17,25},{9,1},{25,17},{2,10},{18... | collective-permute-start | bytes 245768 | tf_op jit(solution)/shard_map/ppermute | solution.py:360
  17.4 6.6 %collective-permute-start.4 = (s16[1,5,32,256]{3,2,1,0:T(8,128)(2,1)S(1)}, s16[1,5,32,256]{3,2,1,0:T(8,128)(2,1)S(1)}, u32[]{:S(2)}, u32[]{:S(2)}) collective-permute-start(s16[1,5,32,256]{3,2,1,0:T(8,128)(2,1)S(1)} %relay.3), channel_id=1, source_target_pairs={{0,16},{8,24},{16,0},{24,8},{1,17},{9,25},{17,1},{25,9},{2,18},{10... | collective-permute-start | bytes 245768 | tf_op jit(solution)/shard_map/ppermute | solution.py:360
  24.1 1.2 %collective-permute-start.5 = (f32[3,256]{1,0:T(4,128)S(1)}, f32[3,256]{1,0:T(4,128)S(1)}, u32[]{:S(2)}, u32[]{:S(2)}) collective-permute-start(f32[3,256]{1,0:T(4,128)S(1)} %get-tuple-element.29), channel_id=1, source_target_pairs={{0,1},{2,3},{4,5},{6,7},{1,0},{3,2},{5,4},{7,6},{8,9},{10,11},{12,... | collective-permute-start | bytes 9224 | tf_op jit(solution)/shard_map/ppermute | solution.py:345
  24.2 3.7 %collective-permute-start.6 = (f32[3,256]{1,0:T(4,128)S(1)}, f32[3,256]{1,0:T(4,128)S(1)}, u32[]{:S(2)}, u32[]{:S(2)}) collective-permute-start(f32[3,256]{1,0:T(4,128)S(1)} %get-tuple-element.30), channel_id=1, source_target_pairs={{1,2},{3,4},{5,6},{2,1},{4,3},{6,5},{0,8},{7,15},{9,10},{11,12},{1... | collective-permute-start | bytes 9224 | tf_op jit(solution)/shard_map/ppermute | solution.py:339

commit v9 on v7

--- a/solution.py
+++ b/solution.py
@@ -197,6 +197,30 @@
     )(run, late, last, follow)
 
 
+def head(field):
+    channels, _, rows, columns = field.shape
+
+    def kernel(field, out, sem):
+        copies = [
+            pltpu.make_async_copy(field.at[ch, 0], out.at[ch, 0], sem.at[ch])
+            for ch in range(channels)
+        ]
+        for copy in copies:
+            copy.start()
+        for copy in copies:
+            copy.wait()
+
+    return pl.pallas_call(
+        kernel,
+        in_specs=[pl.BlockSpec(memory_space=pltpu.HBM)],
+        out_specs=vmem(),
+        out_shape=jax.ShapeDtypeStruct((channels, 1, rows, columns), field.dtype),
+        scratch_shapes=[pltpu.SemaphoreType.DMA((channels,))],
+        compiler_params=pltpu.CompilerParams(vmem_limit_bytes=16 << 20),
+        name="head",
+    )(pltpu.with_memory_space_constraint(field, pltpu.HBM))
+
+
 def join(mine, got, got_first):
     first = [jnp.where(got_first, g, m) for m, g in zip(mine, got)]
     last = [jnp.where(got_first, m, g) for m, g in zip(mine, got)]
@@ -337,7 +361,7 @@
         parity = jnp.where(b < 2, 1 - (s & 1), s & 1)
         return 2 * (((s >> 1) & 1) ^ 1 ^ (b & 1)) + parity
 
-    follow = lax.ppermute(field[:, :1], "slab", [(i + 1, i) for i in range(slabs - 1)])
+    follow = lax.ppermute(head(field), "slab", [(i + 1, i) for i in range(slabs - 1)])
     ahead = march(field, fine_plane, fine_frac, counts, block)
 
     def part(first, steps, coded):

time: 26.6 us -> 26.6 us (level)
  local copies, waits for them, and re-layouts: 0.92 us -> 0 us
  Pallas kernels: 6.96 us -> 7.85 us
    slice x1 -> x0, local copies, waits for them, and re-layouts: 0.92 us -> none  [body(): field[:, :1]]
    pallas_call x0 -> x1, Pallas kernels: none -> 0.89 us  [head(): pl.pallas_call(kernel, in_specs=[pl.BlockSpec(memory_space=pltpu.HBM)], o...]
where the time goes in v9:
time: 26.6 us; the launch traced here: 26.3 us
  waiting for transfers between devices  10.7 us (40%)
  Pallas kernels  7.85 us (30%)
  starting transfers between devices  7.08 us (27%)
  between operations  0.72 us (3%)
    ppermute x3, waiting for transfers between devices, swap(): return lax.ppermute(x, 'slab', pairs(low, [i + distance for i in low]))  5.32 us
    ppermute x3, starting transfers between devices, swap(): return lax.ppermute(x, 'slab', pairs(low, [i + distance for i in low]))  4.97 us
    pallas_call x1, Pallas kernels, march(): pl.pallas_call(kernel, grid=(steps,), in_specs=[spec(2, depth), spec(slot...  4.69 us
    ppermute x1, waiting for transfers between devices, neighbours(): lax.ppermute(far, ('slab', 'col'), [(s * count + a, t * count + b) for s...  2.52 us
    ppermute x1, waiting for transfers between devices, body(): lax.ppermute(head(field), 'slab', [(i + 1, i) for i in range(slabs - 1)])  2.45 us
    pallas_call x4, Pallas kernels, close(): pl.pallas_call(kernel, in_specs=[vmem()] * 4, out_specs=vmem(), out_shape...  1.34 us
    ppermute x1, starting transfers between devices, body(): lax.ppermute(head(field), 'slab', [(i + 1, i) for i in range(slabs - 1)])  1.29 us
    pallas_call x1, Pallas kernels, head(): pl.pallas_call(kernel, in_specs=[pl.BlockSpec(memory_space=pltpu.HBM)], o...  0.89 us
  transfers between devices with their start and end apart: 6, of which 5 were waited for; matrix products, arithmetic and copies ran while one was open for 0% of the time, Pallas kernels for 22%

profile of v9, /device:TPU:0, one launch (start us, length us, event | category | flops | bytes accessed | tf_op | source)
XLA Modules:
  0.0 26.3 jit_solution(3716670940703414528)
XLA Ops:
  0.6 0.9 %head.1 = bf16[2,1,32,1024]{3,2,1,0:T(8,128)(2,1)S(1)} custom-call(bf16[2,16,32,1024]{3,2,1,0:T(8,128)(2,1)} %field.3), custom_call_target="tpu_custom_call" | custom-call | tf_op jit(solution)/shard_map/head/pallas_call | solution.py:213
  1.5 1.3 %collective-permute-start = (bf16[2,1,32,1024]{3,2,1,0:T(8,128)(2,1)S(1)}, bf16[2,1,32,1024]{3,2,1,0:T(8,128)(2,1)S(1)}, u32[]{:S(2)}, u32[]{:S(2)}) collective-permute-start(bf16[2,1,32,1024]{3,2,1,0:T(8,128)(2,1)S(1)} %head.1), channel_id=1, source_target_pairs={{8,0},{16,8},{24,16},{9,1},{17,9},{25,17},{10,2},{18,10},{26,18},{... | collective-permute-start | bytes 393224 | tf_op jit(solution)/shard_map/ppermute | solution.py:364
  2.8 4.7 %march.1 = (f32[4,5,32,256]{3,2,1,0:T(8,128)S(1)}, bf16[4,8,32,256]{3,2,1,0:T(8,128)(2,1)S(1)}, bf16[4,2,32,256]{3,2,1,0:T(8,128)(2,1)S(1)}) custom-call(bf16[2,16,32,1024]{3,2,1,0:T(8,128)(2,1)} %field.3, s32[8,32,1024]{2,1,0:T(8,128)} %plane.1, s32[8,32,1024]{2,1,0:T(8,128)} %frac.1, s32[1,32,1024]{2,1,0:T(8,128)} %counts.1), custom_call_target="tpu_custom_call" | custom-call | flops 98304000 | bytes 4194304 | tf_op jit(solution)/shard_map/march/pallas_call | solution.py:128
  7.5 2.4 %collective-permute-done.follow = bf16[2,1,32,1024]{3,2,1,0:T(8,128)(2,1)S(1)} collective-permute-done((bf16[2,1,32,1024]{3,2,1,0:T(8,128)(2,1)S(1)}, bf16[2,1,32,1024]{3,2,1,0:T(8,128)(2,1)S(1)}, u32[]{:S(2)}, u32[]{:S(2)}) %collective-permute-start) | collective-permute-done | bytes 131104 | tf_op jit(solution)/shard_map/ppermute | solution.py:364
  10.0 0.4 %close.7 = s16[1,5,32,256]{3,2,1,0:T(8,128)(2,1)S(1)} custom-call(f32[4,5,32,256]{3,2,1,0:T(8,128)S(1)} %get-tuple-element.9.run, bf16[4,8,32,256]{3,2,1,0:T(8,128)(2,1)S(1)} %get-tuple-element.10.late, bf16[4,2,32,256]{3,2,1,0:T(8,128)(2,1)S(1)} %get-tuple-element.11.last, bf16[2,1,32,1024]{3,2,1,0:T(8,128)(2,1)S(1)} %collective-permute-done.follow), custom_call_target="tpu_custom_call" | custom-call | flops 12288000 | bytes 524288 | tf_op jit(solution)/shard_map/close/pallas_call | solution.py:186
  10.4 1.8 %collective-permute-start.2 = (s16[1,5,32,256]{3,2,1,0:T(8,128)(2,1)S(1)}, s16[1,5,32,256]{3,2,1,0:T(8,128)(2,1)S(1)}, u32[]{:S(2)}, u32[]{:S(2)}) collective-permute-start(s16[1,5,32,256]{3,2,1,0:T(8,128)(2,1)S(1)} %close.7), channel_id=1, source_target_pairs={{0,8},{16,24},{8,0},{24,16},{1,9},{17,25},{9,1},{25,17},{2,10},{18... | collective-permute-start | bytes 245768 | tf_op jit(solution)/shard_map/ppermute | solution.py:347
  12.2 0.4 %close.5 = s16[1,5,32,256]{3,2,1,0:T(8,128)(2,1)S(1)} custom-call(f32[4,5,32,256]{3,2,1,0:T(8,128)S(1)} %get-tuple-element.9.run, bf16[4,8,32,256]{3,2,1,0:T(8,128)(2,1)S(1)} %get-tuple-element.10.late, bf16[4,2,32,256]{3,2,1,0:T(8,128)(2,1)S(1)} %get-tuple-element.11.last, bf16[2,1,32,1024]{3,2,1,0:T(8,128)(2,1)S(1)} %collective-permute-done.follow), custom_call_target="tpu_custom_call" | custom-call | flops 12288000 | bytes 524288 | tf_op jit(solution)/shard_map/close/pallas_call | solution.py:186
  12.5 0.4 %collective-permute-start.1 = (s16[1,5,32,256]{3,2,1,0:T(8,128)(2,1)S(1)}, s16[1,5,32,256]{3,2,1,0:T(8,128)(2,1)S(1)}, u32[]{:S(2)}, u32[]{:S(2)}) collective-permute-start(s16[1,5,32,256]{3,2,1,0:T(8,128)(2,1)S(1)} %close.5), channel_id=1, source_target_pairs={{0,8},{16,24},{8,0},{24,16},{1,9},{17,25},{9,1},{25,17},{2,10},{18... | collective-permute-start | bytes 245768 | tf_op jit(solution)/shard_map/ppermute | solution.py:347
  12.9 0.3 %close.6.mine = f32[1,5,32,256]{3,2,1,0:T(8,128)S(1)} custom-call(f32[4,5,32,256]{3,2,1,0:T(8,128)S(1)} %get-tuple-element.9.run, bf16[4,8,32,256]{3,2,1,0:T(8,128)(2,1)S(1)} %get-tuple-element.10.late, bf16[4,2,32,256]{3,2,1,0:T(8,128)(2,1)S(1)} %get-tuple-element.11.last, bf16[2,1,32,1024]{3,2,1,0:T(8,128)(2,1)S(1)} %collective-permute-done.follow), custom_call_target="tpu_custom_call" | custom-call | flops 12288000 | bytes 524288 | tf_op jit(solution)/shard_map/close/pallas_call | solution.py:186
  13.2 2.2 %collective-permute-done.2.got = s16[1,5,32,256]{3,2,1,0:T(8,128)(2,1)S(1)} collective-permute-done((s16[1,5,32,256]{3,2,1,0:T(8,128)(2,1)S(1)}, s16[1,5,32,256]{3,2,1,0:T(8,128)(2,1)S(1)}, u32[]{:S(2)}, u32[]{:S(2)}) %collective-permute-start.2) | collective-permute-done | bytes 81952 | tf_op jit(solution)/shard_map/ppermute | solution.py:347
  15.4 0.1 relay.3
  15.5 2.8 %collective-permute-start.3 = (s16[1,5,32,256]{3,2,1,0:T(8,128)(2,1)S(1)}, s16[1,5,32,256]{3,2,1,0:T(8,128)(2,1)S(1)}, u32[]{:S(2)}, u32[]{:S(2)}) collective-permute-start(s16[1,5,32,256]{3,2,1,0:T(8,128)(2,1)S(1)} %relay.3), channel_id=1, source_target_pairs={{0,16},{8,24},{16,0},{24,8},{1,17},{9,25},{17,1},{25,9},{2,18},{10... | collective-permute-start | bytes 245768 | tf_op jit(solution)/shard_map/ppermute | solution.py:347
  18.4 0.3 %close.4.mine = f32[1,5,32,256]{3,2,1,0:T(8,128)S(1)} custom-call(f32[4,5,32,256]{3,2,1,0:T(8,128)S(1)} %get-tuple-element.9.run, bf16[4,8,32,256]{3,2,1,0:T(8,128)(2,1)S(1)} %get-tuple-element.10.late, bf16[4,2,32,256]{3,2,1,0:T(8,128)(2,1)S(1)} %get-tuple-element.11.last, bf16[2,1,32,1024]{3,2,1,0:T(8,128)(2,1)S(1)} %collective-permute-done.follow), custom_call_target="tpu_custom_call" | custom-call | flops 12288000 | bytes 524288 | tf_op jit(solution)/shard_map/close/pallas_call | solution.py:186
  18.7 0.0 collective-permute-done.1.got
  18.7 0.1 relay.2.mine
  18.8 3.1 %collective-permute-done.3.refs_0_ = s16[1,5,32,256]{3,2,1,0:T(8,128)(2,1)S(1)} collective-permute-done((s16[1,5,32,256]{3,2,1,0:T(8,128)(2,1)S(1)}, s16[1,5,32,256]{3,2,1,0:T(8,128)(2,1)S(1)}, u32[]{:S(2)}, u32[]{:S(2)}) %collective-permute-start.3) | collective-permute-done | bytes 81952 | tf_op jit(solution)/shard_map/ppermute | solution.py:347
  21.8 0.1 finish.1
  21.9 0.1 collective-permute-start.4
  22.0 0.7 %collective-permute-start.5 = (f32[3,256]{1,0:T(4,128)S(1)}, f32[3,256]{1,0:T(4,128)S(1)}, u32[]{:S(2)}, u32[]{:S(2)}) collective-permute-start(f32[3,256]{1,0:T(4,128)S(1)} %get-tuple-element.14), channel_id=1, source_target_pairs={{1,2},{3,4},{5,6},{2,1},{4,3},{6,5},{0,8},{7,15},{9,10},{11,12},{1... | collective-permute-start | bytes 9224 | tf_op jit(solution)/shard_map/ppermute | solution.py:325
  22.8 0.4 %collective-permute-done.4.near = f32[3,256]{1,0:T(4,128)S(1)} collective-permute-done((f32[3,256]{1,0:T(4,128)S(1)}, f32[3,256]{1,0:T(4,128)S(1)}, u32[]{:S(2)}, u32[]{:S(2)}) %collective-permute-start.4) | collective-permute-done | bytes 3104 | tf_op jit(solution)/shard_map/ppermute | solution.py:331
  23.2 2.5 %collective-permute-done.5.far = f32[3,256]{1,0:T(4,128)S(1)} collective-permute-done((f32[3,256]{1,0:T(4,128)S(1)}, f32[3,256]{1,0:T(4,128)S(1)}, u32[]{:S(2)}, u32[]{:S(2)}) %collective-permute-start.5) | collective-permute-done | bytes 3104 | tf_op jit(solution)/shard_map/ppermute | solution.py:325
  25.7 0.7 %border.1 = (f32[32,256]{1,0:T(8,128)}, f32[32,256]{1,0:T(8,128)}, f32[32,256]{1,0:T(8,128)}) custom-call(f32[3,32,256]{2,1,0:T(8,128)S(1)} %get-tuple-element.12.image, f32[3,256]{1,0:T(4,128)S(1)} %collective-permute-done.4.near, f32[3,256]{1,0:T(4,128)S(1)} %collective-permute-done.5.far), custom_call_target="tpu_custom_call" | custom-call | tf_op jit(solution)/shard_map/border/pallas_call | solution.py:308
Async XLA Ops:
  1.5 8.4 %collective-permute-start = (bf16[2,1,32,1024]{3,2,1,0:T(8,128)(2,1)S(1)}, bf16[2,1,32,1024]{3,2,1,0:T(8,128)(2,1)S(1)}, u32[]{:S(2)}, u32[]{:S(2)}) collective-permute-start(bf16[2,1,32,1024]{3,2,1,0:T(8,128)(2,1)S(1)} %head.1), channel_id=1, source_target_pairs={{8,0},{16,8},{24,16},{9,1},{17,9},{25,17},{10,2},{18,10},{26,18},{... | collective-permute-start | bytes 393224 | tf_op jit(solution)/shard_map/ppermute | solution.py:364
  10.4 5.1 %collective-permute-start.2 = (s16[1,5,32,256]{3,2,1,0:T(8,128)(2,1)S(1)}, s16[1,5,32,256]{3,2,1,0:T(8,128)(2,1)S(1)}, u32[]{:S(2)}, u32[]{:S(2)}) collective-permute-start(s16[1,5,32,256]{3,2,1,0:T(8,128)(2,1)S(1)} %close.7), channel_id=1, source_target_pairs={{0,8},{16,24},{8,0},{24,16},{1,9},{17,25},{9,1},{25,17},{2,10},{18... | collective-permute-start | bytes 245768 | tf_op jit(solution)/shard_map/ppermute | solution.py:347
  12.5 6.1 %collective-permute-start.1 = (s16[1,5,32,256]{3,2,1,0:T(8,128)(2,1)S(1)}, s16[1,5,32,256]{3,2,1,0:T(8,128)(2,1)S(1)}, u32[]{:S(2)}, u32[]{:S(2)}) collective-permute-start(s16[1,5,32,256]{3,2,1,0:T(8,128)(2,1)S(1)} %close.5), channel_id=1, source_target_pairs={{0,8},{16,24},{8,0},{24,16},{1,9},{17,25},{9,1},{25,17},{2,10},{18... | collective-permute-start | bytes 245768 | tf_op jit(solution)/shard_map/ppermute | solution.py:347
  15.5 6.3 %collective-permute-start.3 = (s16[1,5,32,256]{3,2,1,0:T(8,128)(2,1)S(1)}, s16[1,5,32,256]{3,2,1,0:T(8,128)(2,1)S(1)}, u32[]{:S(2)}, u32[]{:S(2)}) collective-permute-start(s16[1,5,32,256]{3,2,1,0:T(8,128)(2,1)S(1)} %relay.3), channel_id=1, source_target_pairs={{0,16},{8,24},{16,0},{24,8},{1,17},{9,25},{17,1},{25,9},{2,18},{10... | collective-permute-start | bytes 245768 | tf_op jit(solution)/shard_map/ppermute | solution.py:347
  21.9 1.2 %collective-permute-start.4 = (f32[3,256]{1,0:T(4,128)S(1)}, f32[3,256]{1,0:T(4,128)S(1)}, u32[]{:S(2)}, u32[]{:S(2)}) collective-permute-start(f32[3,256]{1,0:T(4,128)S(1)} %get-tuple-element.13), channel_id=1, source_target_pairs={{0,1},{2,3},{4,5},{6,7},{1,0},{3,2},{5,4},{7,6},{8,9},{10,11},{12,... | collective-permute-start | bytes 9224 | tf_op jit(solution)/shard_map/ppermute | solution.py:331
  22.0 3.7 %collective-permute-start.5 = (f32[3,256]{1,0:T(4,128)S(1)}, f32[3,256]{1,0:T(4,128)S(1)}, u32[]{:S(2)}, u32[]{:S(2)}) collective-permute-start(f32[3,256]{1,0:T(4,128)S(1)} %get-tuple-element.14), channel_id=1, source_target_pairs={{1,2},{3,4},{5,6},{2,1},{4,3},{6,5},{0,8},{7,15},{9,10},{11,12},{1... | collective-permute-start | bytes 9224 | tf_op jit(solution)/shard_map/ppermute | solution.py:325
